TPU v7x, 512 devices: a whole 4x4x16 slice. The times are simulated.
512 devices in a mesh: freq: 16 (over x, z_lo), line: 32 (over z_hi, y, core).
Axes of the slice: x: 4, y: 4, z: 16 (z_hi: 4, z_lo: 4; z = z_hi * 4 + z_lo), core: 2. Of those that a mesh axis runs over, the one named last changes fastest.
Arguments:
- field: float32 [16, 2, 4, 96, 64, 256], P('freq', None, None, None, 'line'), may hold values from -6 to 6
- live_count: int32 [64], P('line'), may hold values from 64 to 256
- line_owner: int32 [64], replicated, may hold values from 0 to 63, each once
- decomposer: float32 [16, 2, 4, 4, 64, 256], P('freq', None, None, None, 'line'), may hold values from -1.4 to 2.4
- reflection: bfloat16 [16, 1024, 2, 16384], P('freq', None, None, 'line'), may hold values from -0.0625 to 0.0625
- direct_wave: float32 [1024, 16, 2, 384], P('line', 'freq'), may hold values from -6 to 6
Outputs:
- focusing: float32 [1024, 16, 2, 384], P('line', 'freq')
- trace_energy: float32 [1024], P('line')
Inputs may be any that keep to these rules, and one draw needn't show every extreme that they name: `line_owner`: each crossline position appears once.
All inputs are finite; a program needn't handle non-finite values.
Results may differ from a plain program's by a relative error of at most 0.0023.
Values may be sent and summed in bfloat16 or wider, within the bound.
No kernel may reach another device: no remote copies, remote signals or barrier semaphores. Data moves between devices by JAX's collectives and lax.ppermute only.
A program may use at most 64 MiB of HBM per device.

v0:
```python
import math

import jax
import jax.numpy as jnp
from jax import lax
from jax.sharding import Mesh
from jax.sharding import PartitionSpec as P

LINE = ("line_0", "line_1", "line_2")


def in_blocks(shard, dim, count):
    before, after = (shard.shape[:dim], shard.shape[dim + 1 :])
    return jnp.moveaxis(shard.reshape(*before, count, -1, *after), dim, 0)


def scatter_pairs(shard, chips, core, dim):
    sizes = (lax.axis_size(chips), lax.axis_size(core))
    blocks = in_blocks(shard, dim, sizes[0] * sizes[1])
    inside = blocks.shape[1:]
    blocks = blocks.reshape(*sizes, *inside).swapaxes(0, 1).reshape(-1, *inside)
    blocks = lax.psum_scatter(blocks, core, scatter_dimension=0, tiled=True)
    return lax.psum_scatter(blocks, chips, scatter_dimension=0, tiled=True)[0]


def sent_to_all(shard, axis):
    count = lax.axis_size(axis)
    return lax.all_to_all(
        jnp.broadcast_to(shard[None], (count, *shard.shape)), axis, 0, 0, tiled=True
    )


def over_copies(shard, axis):
    return sent_to_all(shard, axis).sum(axis=0)


def phase_tables(line_owner, length):
    wavenum = jnp.arange(length, dtype=jnp.int32)
    products = wavenum[:, None] * line_owner[None, :] % length
    angles = products.astype(jnp.float32) * (2.0 * math.pi / length)
    return (jnp.cos(angles), jnp.sin(angles))


def decompose(operator, spectrum):
    real_rows = []
    imag_rows = []
    for target in range(4):
        real_sum = None
        imag_sum = None
        for source in range(4):
            weight_real = operator[:, 0, target, source][:, None]
            weight_imag = operator[:, 1, target, source][:, None]
            field_real = spectrum[:, 0, source]
            field_imag = spectrum[:, 1, source]
            term_real = weight_real * field_real - weight_imag * field_imag
            term_imag = weight_real * field_imag + weight_imag * field_real
            real_sum = term_real if real_sum is None else real_sum + term_real
            imag_sum = term_imag if imag_sum is None else imag_sum + term_imag
        real_rows.append(real_sum)
        imag_rows.append(imag_sum)
    return jnp.stack([jnp.stack(real_rows, 1), jnp.stack(imag_rows, 1)], 1)


def on_device(field, live_count, line_owner, decomposer, reflection, direct_wave):
    length = line_owner.shape[0]
    receivers = field.shape[5]
    cosine, sine_table = phase_tables(line_owner, length)
    forward_table = jnp.stack([jnp.stack([cosine, sine_table]), jnp.stack([-sine_table, cosine])])
    inverse_table = (
        jnp.stack([jnp.stack([cosine.T, -sine_table.T]), jnp.stack([sine_table.T, cosine.T])])
        / length
    )
    live_mask = jnp.arange(receivers, dtype=jnp.int32)[None, :] < live_count[:, None]
    live_field = jnp.where(live_mask, field, jnp.float32(0.0))
    operator = lax.all_gather(decomposer, LINE, axis=4, tiled=True)
    every_line = lax.all_to_all(live_field, LINE, split_axis=3, concat_axis=4, tiled=True)
    space_all = jnp.einsum(
        "yxjk,fxiokr->fyiojr",
        inverse_table,
        decompose(
            operator,
            jnp.einsum(
                "yxkj,fxiojr->fyiokr", forward_table, every_line, precision=lax.Precision.HIGHEST
            ),
        ),
        precision=lax.Precision.HIGHEST,
    )
    wavefield = lax.all_to_all(
        space_all.astype(jnp.bfloat16), LINE, split_axis=4, concat_axis=3, tiled=True
    )
    freq_count = wavefield.shape[0]
    channels = wavefield.shape[2] * wavefield.shape[3]
    positions = wavefield.shape[4] * wavefield.shape[5]
    wave_bf = wavefield.reshape(freq_count, 2, channels, positions)
    real_part = wave_bf[:, 0]
    imag_part = wave_bf[:, 1]
    stacked = jnp.stack(
        [jnp.stack([real_part, imag_part], 1), jnp.stack([-imag_part, real_part], 1)], 1
    )
    reflected = scatter_pairs(
        jnp.einsum("fsxq,fxocq->sfoc", reflection, stacked, preferred_element_type=jnp.float32),
        ("line_0", "line_1"),
        "line_2",
        0,
    )
    focusing = direct_wave - reflected
    total_freqs = freq_count * lax.axis_size("freq")
    freq_index = lax.axis_index("freq") * freq_count + jnp.arange(freq_count, dtype=jnp.int32)
    weights = 2.0 * (freq_index + 1).astype(jnp.float32) / (total_freqs * (total_freqs + 1))
    partial_value = jnp.sum(jnp.sum(reflected * reflected, axis=(2, 3)) * weights[None, :], axis=1)
    energy_sum = over_copies(partial_value, "freq")
    trace_energy = jnp.sqrt(energy_sum / (2 * channels) + 1e-06)
    return (focusing, trace_energy)


def solution(mesh):
    finer = Mesh(
        mesh.devices.reshape(mesh.shape["freq"], 4, 4, 2), ("freq", "line_0", "line_1", "line_2")
    )
    in_specs = (
        P("freq", None, None, None, LINE, None),
        P(LINE),
        P(),
        P("freq", None, None, None, LINE, None),
        P("freq", None, None, LINE),
        P(LINE, "freq", None, None),
    )
    out_specs = (P(LINE, "freq", None, None), P(LINE))
    return jax.shard_map(
        on_device, mesh=finer, in_specs=in_specs, out_specs=out_specs, check_vma=False
    )
```

profile of v0, /device:TPU:8, one launch (start us, length us, event | category | flops | bytes accessed | tf_op | source)
XLA Modules:
  0.0 385.9 jit_solution(8191804675190697036)
XLA Ops:
  7.2 1.5 copy.86
  8.7 0.7 iota_compare_fusion
  9.4 3.5 copy_select_fusion
  12.9 18.5 %all-to-all-start = ((f32[1,2,4,96,2,256]{5,4,2,1,0,3:T(2,128)}), f32[1,2,4,96,2,256]{5,4,2,1,0,3:T(2,128)S(1)}, u32[]{:S(2)}, u32[]{:S(2)}) async-start(f32[1,2,4,96,2,256]{5,4,2,1,0,3:T(2,128)} %copy_select_fusion), calls=%async_computation | async-start | bytes 3145728 | tf_op jit(solution)/shard_map/all_to_all | solution.py:76
  33.0 100.7 %all-gather.2.cloned.1.call-done = f32[1,2,4,4,64,256]{5,3,2,1,0,4:T(4,128)} async-done(((f32[1,2,4,4,2,256]{5,3,2,1,0,4:T(4,128)}), f32[1,2,4,4,64,256]{5,3,2,1,0,4:T(4,128)}) %all-gather.2.cloned.1.call-update) | async-done | bytes 2097168 | tf_op jit(solution)/shard_map/all_gather | solution.py:75
  133.7 3.3 fusion.51
  137.0 4.3 %fusion.50 = (f32[1,1,1,1,64,256]{5,3,2,1,0,4:T(1,128)S(1)}, f32[1,1,1,1,64,256]{5,3,2,1,0,4:T(1,128)S(1)}, f32[1,1,1,1,64,256]{5,3,2,1,0,4:T(1,128)S(1)}, f32[1...) fusion(f32[1,2,4,4,64,256]{5,3,2,1,0,4:T(4,128)} %all-gather.2., ...), kind=kLoop, calls=%fused_computation.116 | loop fusion | bytes 2490368 | tf_op jit(solution)/shard_map/slice | solution.py:51
  149.9 0.9 copy.201
  150.8 1.1 reshape.1466
  151.9 2.5 fusion.12
  158.5 0.7 copy-done.26
  159.3 1.6 fusion.17
  160.8 0.8 copy.97
  161.6 49.5 %all_to_all.36 = bf16[1,2,4,3,64,256]{5,1,3,2,0,4:T(2,128)(2,1)S(1)} all-to-all(bf16[1,2,4,3,64,256]{5,1,3,2,0,4:T(2,128)(2,1)S(1)} %copy.97), channel_id=1, replica_groups=mesh['freq'=16,'line_0'=4,'line_1'=4,'line_2'=2] {'line_0','line_1','lin..., dimensions={4} | all-to-all | bytes 1572864 | tf_op jit(solution)/shard_map/all_to_all | solution.py:88
  212.9 1.4 copy-done.30
  214.4 3.5 fusion.3
  217.8 2.4 copy.100
  220.2 1.9 copy.101
  222.2 18.9 %reduce-scatter.3.cloned.1.call-done = f32[16,32,1,2,384]{4,1,3,2,0:T(8,128)} async-done(((f32[32,32,1,2,384]{4,1,3,2,0:T(8,128)}), f32[16,32,1,2,384]{4,1,3,2,0:T(8,128)}) %reduce-scatter.3.cloned.1.call-update) | async-done | bytes 1572880 | tf_op jit(solution)/shard_map/reduce_scatter | solution.py:22
  241.1 122.4 %reduce-scatter.5.cloned.1.call-done = f32[1,32,1,2,384]{4,1,3,2,0:T(8,128)} async-done(((f32[16,32,1,2,384]{4,1,3,2,0:T(8,128)}), f32[1,32,1,2,384]{4,1,3,2,0:T(8,128)}) %reduce-scatter.5.cloned.1.call-update) | async-done | bytes 98320 | tf_op jit(solution)/shard_map/reduce_scatter | solution.py:23
  363.5 1.0 fusion.26
  365.1 5.7 %all-to-all-start.2 = ((f32[16,1,32]{2,1,0:T(1,128)}), f32[16,1,32]{2,1,0:T(1,128)S(1)}, u32[]{:S(2)}, u32[]{:S(2)}) async-start(f32[16,1,32]{2,1,0:T(1,128)} %broadcast_in_dim.12), calls=%async_computation.4 | async-start | bytes 16384 | tf_op jit(solution)/shard_map/all_to_all | solution.py:28
  370.9 0.7 copy.104
  371.6 7.2 %all-to-all-done.2 = f32[16,1,32]{2,1,0:T(1,128)S(1)} async-done(((f32[16,1,32]{2,1,0:T(1,128)}), f32[16,1,32]{2,1,0:T(1,128)S(1)}, u32[]{:S(2)}, u32[]{:S(2)}) %all-to-all-start.2) | async-done | bytes 2080 | tf_op jit(solution)/shard_map/all_to_all | solution.py:28
  (105 shorter events, 17.1 us)
Async XLA Ops:
  7.2 126.5 %all-gather.2.cloned.1.call-start = ((), (), s32[]{:S(2)}) async-start(), calls=%async_computation.5 | async-start | bytes 2162688 | tf_op jit(solution)/shard_map/all_gather | solution.py:75
  12.9 18.5 %copy-start.29 = (s32[64]{0:T(128)S(1)}, s32[64]{0:T(128)}, u32[]{:S(2)}) copy-start(s32[64]{0:T(128)} %param.8) | copy-start | bytes 772
  12.9 137.0 %all-to-all-start = ((f32[1,2,4,96,2,256]{5,4,2,1,0,3:T(2,128)}), f32[1,2,4,96,2,256]{5,4,2,1,0,3:T(2,128)S(1)}, u32[]{:S(2)}, u32[]{:S(2)}) async-start(f32[1,2,4,96,2,256]{5,4,2,1,0,3:T(2,128)} %copy_select_fusion), calls=%async_computation | async-start | bytes 3145728 | tf_op jit(solution)/shard_map/all_to_all | solution.py:76
  31.4 209.7 %reduce-scatter.3.cloned.1.call-start = ((), (), s32[]{:S(2)}) async-start(), calls=%async_computation.6 | async-start | bytes 4718592 | tf_op jit(solution)/shard_map/reduce_scatter | solution.py:22
  151.9 2.5 copy-start.2
  151.9 2.5 copy-start.3
  154.6 0.9 copy-start.6
  154.6 1.0 copy-start.7
  154.6 1.0 copy-start.10
  154.6 1.0 copy-start.11
  155.8 0.9 copy-start.13
  155.8 0.9 copy-start.14
  155.8 1.0 copy-start.15
  155.8 1.0 copy-start.18
  155.9 1.0 copy-start.19
  157.0 0.9 copy-start.21
  157.0 0.9 copy-start.22
  157.1 1.0 copy-start.23
  157.1 1.0 copy-start.24
  157.1 1.0 copy-start.25
  212.8 1.6 copy-start.30
  222.1 141.4 %copy-start.28 = (f32[32,1,2,384]{3,2,1,0:T(2,128)S(1)}, f32[32,1,2,384]{3,2,1,0:T(2,128)}, u32[]{:S(2)}) copy-start(f32[32,1,2,384]{3,2,1,0:T(2,128)} %param.11) | copy-start | bytes 294916
  222.2 141.3 %reduce-scatter.5.cloned.1.call-start = ((), (), s32[]{:S(2)}) async-start(), calls=%async_computation.7 | async-start | bytes 1671168 | tf_op jit(solution)/shard_map/reduce_scatter | solution.py:23
  365.1 13.7 %all-to-all-start.2 = ((f32[16,1,32]{2,1,0:T(1,128)}), f32[16,1,32]{2,1,0:T(1,128)S(1)}, u32[]{:S(2)}, u32[]{:S(2)}) async-start(f32[16,1,32]{2,1,0:T(1,128)} %broadcast_in_dim.12), calls=%async_computation.4 | async-start | bytes 16384 | tf_op jit(solution)/shard_map/all_to_all | solution.py:28
  (12 other events, 10.4 us)
Sparse Core Ops, SparseCore 0:
  11.1 122.5 all-gather.1
  222.3 18.7 reduce-scatter.2
  245.2 118.2 reduce-scatter.4
where the time goes:
time: 387 us; the launch traced here: 386 us
  waiting for transfers between devices  249 us (64%)
  blocking collectives  49.5 us (13%)
  local copies, waits for them, and re-layouts  32.4 us (8%)
  starting transfers between devices  24.3 us (6%)
  between operations  14.2 us (4%)
  other arithmetic  8.75 us (2%)
  matrix products  7.49 us (2%)
    reduce_scatter x1, waiting for transfers between devices, scatter_pairs(): return lax.psum_scatter(blocks, chips, scatter_dimension=0, tiled=True)[0]  122 us
    all_gather x1, waiting for transfers between devices, on_device(): operator = lax.all_gather(decomposer, LINE, axis=4, tiled=True)  101 us
    all_to_all x1, blocking collectives, on_device(): lax.all_to_all(space_all.astype(jnp.bfloat16), LINE, split_axis=4, concat...  49.5 us
    reduce_scatter x1, waiting for transfers between devices, scatter_pairs(): blocks = lax.psum_scatter(blocks, core, scatter_dimension=0, tiled=True)  18.9 us
    all_to_all x1, starting transfers between devices, on_device(): lax.all_to_all(live_field, LINE, split_axis=3, concat_axis=4, tiled=True)  18.5 us
    unnamed x80, local copies, waits for them, and re-layouts  15.5 us
  transfers between devices with their start and end apart: 5, of which 4 were waited for; matrix products, arithmetic and copies ran while one was open for 6% of the time, Pallas kernels for 0%

commit v1 on v0

v1 whole, which is shorter than its diff:
```python
import math

import jax
import jax.numpy as jnp
from jax import lax
from jax.experimental import pallas as pl
from jax.experimental.pallas import tpu as pltpu
from jax.sharding import Mesh
from jax.sharding import PartitionSpec as P

LINE = ("line_0", "line_1", "line_2")
LOW_SCALE = 2048.0


def phase_tables(line_owner, length):
    wavenum = jnp.arange(length, dtype=jnp.int32)
    owner = line_owner.reshape(32, 2).T.reshape(64)
    wavenum = wavenum.reshape(32, 2).T.reshape(64)
    products = wavenum[:, None] * owner[None, :] % length
    angles = products.astype(jnp.float32) * (2.0 * math.pi / length)
    return (jnp.cos(angles), jnp.sin(angles))


def in_two_terms(table):
    high = table.astype(jnp.bfloat16)
    low = (table - high.astype(jnp.float32)).astype(jnp.bfloat16)
    return jnp.concatenate(
        [jnp.concatenate([high, high], 1), jnp.concatenate([low, low], 1)], 0
    )


def transform_tables(line_owner):
    length = line_owner.shape[0]
    cosine, sine = phase_tables(line_owner, length)
    forward = jnp.stack([jnp.stack([cosine, sine]), jnp.stack([-sine, cosine])])
    forward = forward.reshape(2, 2, 64, 2, 32).transpose(0, 2, 3, 1, 4).reshape(128, 128)
    inverse = jnp.stack([jnp.stack([cosine.T, -sine.T]), jnp.stack([sine.T, cosine.T])]) / length
    inverse = inverse.reshape(2, 2, 2, 32, 64).transpose(2, 0, 3, 1, 4).reshape(128, 128)
    return in_two_terms(forward), in_two_terms(inverse)


def middle_kernel(message_ref, forward_ref, inverse_ref, out_ref, wave_ref):
    lane = lax.broadcasted_iota(jnp.int32, (64, 128), 1)
    forward = forward_ref[...]
    inverse = inverse_ref[...]

    def transform(table, value):
        high = value.astype(jnp.bfloat16)
        low = (value - high.astype(jnp.float32)).astype(jnp.bfloat16)
        both = jnp.dot(
            table, jnp.concatenate([high, low], 0), preferred_element_type=jnp.float32
        )
        return both[:128] + both[128:]

    for r in range(8):
        tiles = [
            jnp.concatenate(
                [message_ref[pl.ds((g * 3 + t) * 8 + r, 32, stride=104), :] for g in range(4)], 0
            )
            for t in range(3)
        ]
        spectrum = transform(forward, jnp.concatenate(tiles, 1))
        operator = message_ref[pl.ds(96 + r, 32, stride=104), :]
        operator = operator + pltpu.roll(operator, 64, 1) * jnp.float32(1.0 / LOW_SCALE)
        operator = jnp.concatenate([operator, pltpu.roll(operator, 96, 1)], 0)
        parts = []
        for part in range(2):
            t0, t1, t2 = [
                spectrum[64 * part : 64 * part + 64, 128 * t : 128 * t + 128] for t in range(3)
            ]
            parts.append(
                [
                    t0,
                    pltpu.roll(jnp.where(lane >= 96, t0, t1), 32, 1),
                    pltpu.roll(jnp.where(lane >= 64, t1, t2), 64, 1),
                    pltpu.roll(t2, 96, 1),
                ]
            )
        rows = [[], []]
        for target in range(4):
            real_sum = None
            imag_sum = None
            for source in range(4):
                at = target * 4 + source
                weight_real = operator[:, at : at + 1]
                weight_imag = operator[:, 16 + at : 17 + at]
                field_real = parts[0][source]
                field_imag = parts[1][source]
                term_real = weight_real * field_real - weight_imag * field_imag
                term_imag = weight_real * field_imag + weight_imag * field_real
                real_sum = term_real if real_sum is None else real_sum + term_real
                imag_sum = term_imag if imag_sum is None else imag_sum + term_imag
            rows[0].append(real_sum)
            rows[1].append(imag_sum)
        decomposed = []
        for part in range(2):
            q0, q1, q2, q3 = rows[part]
            q1 = pltpu.roll(q1, 96, 1)
            q2 = pltpu.roll(q2, 64, 1)
            q3 = pltpu.roll(q3, 32, 1)
            decomposed.append(
                jnp.concatenate(
                    [
                        jnp.where(lane < 96, q0, q1),
                        jnp.where(lane < 64, q1, q2),
                        jnp.where(lane < 32, q2, q3),
                    ],
                    1,
                )
            )
        wave = transform(inverse, jnp.concatenate(decomposed, 0))
        for g in range(4):
            for t in range(3):
                wave_ref[pl.ds((g * 3 + t) * 8 + r, 32, stride=96), :] = wave[
                    32 * g : 32 * g + 32, 128 * t : 128 * t + 128
                ]
    out_ref[...] = wave_ref[...].reshape(32, 12, 8, 128).astype(jnp.bfloat16)


def middle(message, forward, inverse):
    return pl.pallas_call(
        middle_kernel,
        out_shape=jax.ShapeDtypeStruct((32, 12, 8, 128), jnp.bfloat16),
        in_specs=[pl.BlockSpec(memory_space=pltpu.VMEM)] * 3,
        out_specs=pl.BlockSpec(memory_space=pltpu.VMEM),
        scratch_shapes=[pltpu.VMEM((3072, 128), jnp.float32)],
    )(message.astype(jnp.float32).reshape(3328, 128), forward, inverse)


def outgoing(field, live_count, decomposer):
    receivers = field.shape[5]
    live_mask = jnp.arange(receivers, dtype=jnp.int32)[None, :] < live_count[:, None]
    live_field = jnp.where(live_mask, field[0], jnp.float32(0.0)).astype(jnp.float16)
    live_field = live_field.reshape(2, 384, 2, 32, 8)
    live_field = live_field.transpose(3, 2, 0, 4, 1).reshape(32, 2, 2, 8, 3, 128)
    live_field = live_field.transpose(0, 1, 2, 4, 3, 5).reshape(32, 12, 8, 128)
    operator = decomposer[0].reshape(32, 2, 256).transpose(2, 1, 0).reshape(32, 1, 8, 64)
    high = operator.astype(jnp.float16)
    low = ((operator - high.astype(jnp.float32)) * LOW_SCALE).astype(jnp.float16)
    return jnp.concatenate([live_field, jnp.concatenate([high, low], 3)], 1)


def summed(blocks, axis, scale):
    count = lax.axis_size(axis)
    blocks = (blocks * scale).astype(jnp.float16).reshape(count, -1, blocks.shape[-1])
    blocks = lax.all_to_all(blocks, axis, 0, 0, tiled=True)
    return blocks.astype(jnp.float32).sum(axis=0) * (1.0 / scale)


def over_copies(shard, axis):
    count = lax.axis_size(axis)
    shards = jnp.broadcast_to(shard[None], (count, *shard.shape))
    return lax.all_to_all(shards, axis, 0, 0, tiled=True).sum(axis=0)


def on_device(field, live_count, line_owner, decomposer, reflection, direct_wave):
    forward, inverse = transform_tables(line_owner)
    message = outgoing(field, live_count, decomposer)
    message = lax.all_to_all(message, LINE, 0, 0, tiled=True)
    wave = lax.all_to_all(middle(message, forward, inverse), LINE, 0, 0, tiled=True)
    wave = wave.reshape(32, 2, 2, 3, 8, 128).transpose(2, 1, 0, 4, 3, 5).reshape(2, 512, 384)
    panel = reflection[0].reshape(4, 4, 2, 32, 1024).transpose(2, 1, 0, 3, 4).reshape(1024, 1024)
    stacked = jnp.concatenate(
        [jnp.concatenate([wave[0], wave[1]], 1), jnp.concatenate([-wave[1], wave[0]], 1)], 0
    )
    product = jnp.dot(panel, stacked, preferred_element_type=jnp.float32)
    product = summed(product, "line_2", 1.0)
    product = summed(product, "line_1", 0.5)
    product = summed(product, "line_0", 0.125)
    reflected = product.reshape(32, 1, 2, 384)
    focusing = direct_wave - reflected
    total_freqs = lax.axis_size("freq")
    weight = 2.0 * (lax.axis_index("freq") + 1).astype(jnp.float32) / (total_freqs * (total_freqs + 1))
    partial_value = jnp.sum(reflected * reflected, axis=(1, 2, 3)) * weight
    energy_sum = over_copies(partial_value, "freq")
    trace_energy = jnp.sqrt(energy_sum / 768 + 1e-06)
    return (focusing, trace_energy)


def solution(mesh):
    finer = Mesh(
        mesh.devices.reshape(mesh.shape["freq"], 4, 4, 2), ("freq", "line_0", "line_1", "line_2")
    )
    in_specs = (
        P("freq", None, None, None, LINE, None),
        P(LINE),
        P(),
        P("freq", None, None, None, LINE, None),
        P("freq", None, None, LINE),
        P(LINE, "freq", None, None),
    )
    out_specs = (P(LINE, "freq", None, None), P(LINE))
    return jax.shard_map(
        on_device, mesh=finer, in_specs=in_specs, out_specs=out_specs, check_vma=False
    )
```

time: 387 us -> 199 us (0.51)
  the two profiles are of different devices: /device:TPU:8 before, /device:TPU:2 now
where the time goes in v1:
time: 199 us; the launch traced here: 198 us
  waiting for transfers between devices  103 us (52%)
  starting transfers between devices  40 us (20%)
  blocking collectives  20.3 us (10%)
  local copies, waits for them, and re-layouts  15.3 us (8%)
  Pallas kernels  9.21 us (5%)
  other arithmetic  7.65 us (4%)
    all_to_all x1, waiting for transfers between devices, on_device(): message = lax.all_to_all(message, LINE, 0, 0, tiled=True)  41.7 us
    all_to_all x1, waiting for transfers between devices, on_device(): lax.all_to_all(middle(message, forward, inverse), LINE, 0, 0, tiled=True)  39 us
    all_to_all x2, blocking collectives, summed(): blocks = lax.all_to_all(blocks, axis, 0, 0, tiled=True)  20.3 us
    all_to_all x1, starting transfers between devices, on_device(): message = lax.all_to_all(message, LINE, 0, 0, tiled=True)  18.1 us
    all_to_all x1, waiting for transfers between devices, summed(): blocks = lax.all_to_all(blocks, axis, 0, 0, tiled=True)  16.3 us
    pallas_call x1, Pallas kernels, middle(): pl.pallas_call(middle_kernel, out_shape=jax.ShapeDtypeStruct((32, 12, 8,...  9.21 us
    all_to_all x1, starting transfers between devices, on_device(): lax.all_to_all(middle(message, forward, inverse), LINE, 0, 0, tiled=True)  9.11 us
    all_to_all x1, starting transfers between devices, over_copies(): return lax.all_to_all(shards, axis, 0, 0, tiled=True).sum(axis=0)  7.79 us
  transfers between devices with their start and end apart: 4, of which 4 were waited for; matrix products, arithmetic and copies ran while one was open for 4% of the time, Pallas kernels for 0%

profile of v1, /device:TPU:2, one launch (start us, length us, event | category | flops | bytes accessed | tf_op | source)
XLA Modules:
  0.0 198.0 jit_solution(10573700436220319162)
XLA Ops:
  0.6 1.0 copy.105
  1.9 2.8 %copy.103 = f32[1,2,4,96,2,256]{3,2,5,4,1,0:T(4,128)S(1)} copy(f32[1,2,4,96,2,256]{5,4,3,2,1,0:T(2,128)} %param.6) | data formatting | bytes 3145728 | tf_op args[0]
  4.7 2.2 %squeeze.11 = f32[2,384,2,32,8]{1,4,3,2,0:T(8,128)} reshape(f32[1,2,4,96,2,256]{3,2,5,4,1,0:T(4,128)S(1)} %copy.103) | data formatting | bytes 3145728 | tf_op jit(solution)/shard_map/squeeze | solution.py:133
  6.9 1.6 fusion.7
  8.8 1.1 pad_maximum_fusion
  10.0 18.1 %all-to-all-start = ((f16[32,13,8,128]{3,2,1,0:T(8,128)(2,1)}), f16[32,13,8,128]{3,2,1,0:T(8,128)(2,1)S(1)}, u32[]{:S(2)}, u32[]{:S(2)}) async-start(f16[32,13,8,128]{3,2,1,0:T(8,128)(2,1)} %pad_maximum_fusion), calls=%async_computation | async-start | bytes 1703936 | tf_op jit(solution)/shard_map/all_to_all | solution.py:159
  29.5 0.7 maximum_maximum_fusion
  30.2 41.7 %all-to-all-done = f16[32,13,8,128]{3,2,1,0:T(8,128)(2,1)S(1)} async-done(((f16[32,13,8,128]{3,2,1,0:T(8,128)(2,1)}), f16[32,13,8,128]{3,2,1,0:T(8,128)(2,1)S(1)}, u32[]{:S(2)}, u32[]{:S(2)}) %all-to-all-start) | async-done | bytes 852000 | tf_op jit(solution)/shard_map/all_to_all | solution.py:159
  71.9 1.4 bitcast_convert_fusion.message_ref
  73.3 9.2 %shard_map.77 = bf16[32,12,8,128]{3,2,1,0:T(8,128)(2,1)} custom-call(f32[3328,128]{1,0:T(8,128)} %bitcast_convert_fusion.message_ref, bf16[256,256]{1,0:T(8,128)(2,1)} %get-tuple-element.18.forward_ref, bf16[256,256]{1,0:T(8,128)(2,1)} %get-tuple-element.19.inverse_ref), custom_call_target="tpu_custom_call" | custom-call | tf_op jit(solution)/shard_map/pallas_call | solution.py:121
  82.5 9.1 %all-to-all-start.1 = ((bf16[32,12,8,128]{3,2,1,0:T(8,128)(2,1)}), bf16[32,12,8,128]{3,2,1,0:T(8,128)(2,1)S(1)}, u32[]{:S(2)}, u32[]{:S(2)}) async-start(bf16[32,12,8,128]{3,2,1,0:T(8,128)(2,1)} %shard_map.77), calls=%async_computation.1 | async-start | bytes 1572864 | tf_op jit(solution)/shard_map/all_to_all | solution.py:160
  91.6 3.2 %reshape_squeeze.7 = bf16[4,4,2,32,1024]{4,3,2,1,0:T(8,128)(2,1)S(1)} reshape(bf16[1,1024,2,512]{3,2,1,0:T(2,128)(2,1)} %param.10) | data formatting | bytes 4194304 | tf_op jit(solution)/shard_map/reshape;squeeze | solution.py:162
  94.9 1.6 copy.114
  96.4 39.0 %all-to-all-done.1 = bf16[32,12,8,128]{3,2,1,0:T(8,128)(2,1)S(1)} async-done(((bf16[32,12,8,128]{3,2,1,0:T(8,128)(2,1)}), bf16[32,12,8,128]{3,2,1,0:T(8,128)(2,1)S(1)}, u32[]{:S(2)}, u32[]{:S(2)}) %all-to-all-start.1) | async-done | bytes 786464 | tf_op jit(solution)/shard_map/all_to_all | solution.py:160
  135.7 1.4 copy-done
  137.1 1.8 convolution_convert_fusion
  139.3 5.0 %all_to_all.31 = f16[2,512,768]{1,2,0:T(8,128)(2,1)S(1)} all-to-all(f16[2,512,768]{1,2,0:T(8,128)(2,1)S(1)} %bitcast.45), channel_id=1, replica_groups=mesh['freq'=16,'line_0'=4,'line_1'=4,'line_2'=2] {'line_2'}, dimensions={0} | all-to-all | bytes 3145728 | tf_op jit(solution)/shard_map/all_to_all | solution.py:146
  144.7 15.3 %all_to_all.32 = f16[4,128,768]{1,2,0:T(8,128)(2,1)S(1)} all-to-all(f16[4,128,768]{1,2,0:T(8,128)(2,1)S(1)} %copy_bitcast_fusion.1), channel_id=1, replica_groups=mesh['freq'=16,'line_0'=4,'line_1'=4,'line_2'=2] {'line_1'}, dimensions={0} | all-to-all | bytes 1572864 | tf_op jit(solution)/shard_map/all_to_all | solution.py:146
  160.2 0.8 copy.119
  161.0 5.0 %all-to-all-start.4 = ((f16[4,32,768]{2,1,0:T(8,128)(2,1)}), f16[4,32,768]{2,1,0:T(8,128)(2,1)S(1)}, u32[]{:S(2)}, u32[]{:S(2)}) async-start(f16[4,32,768]{2,1,0:T(8,128)(2,1)} %bitcast.18), calls=%async_computation.4 | async-start | bytes 393216 | tf_op jit(solution)/shard_map/all_to_all | solution.py:146
  166.0 16.3 %all-to-all-done.4 = f16[4,32,768]{2,1,0:T(8,128)(2,1)S(1)} async-done(((f16[4,32,768]{2,1,0:T(8,128)(2,1)}), f16[4,32,768]{2,1,0:T(8,128)(2,1)S(1)}, u32[]{:S(2)}, u32[]{:S(2)}) %all-to-all-start.4) | async-done | bytes 196640 | tf_op jit(solution)/shard_map/all_to_all | solution.py:146
  183.1 7.8 %all-to-all-start.5 = ((f32[16,1,32]{2,1,0:T(1,128)}), f32[16,1,32]{2,1,0:T(1,128)S(1)}, u32[]{:S(2)}, u32[]{:S(2)}) async-start(f32[16,1,32]{2,1,0:T(1,128)} %broadcast_in_dim.18), calls=%async_computation.5 | async-start | bytes 16384 | tf_op jit(solution)/shard_map/all_to_all | solution.py:153
  190.9 0.7 sub.23
  191.6 5.8 %all-to-all-done.5 = f32[16,1,32]{2,1,0:T(1,128)S(1)} async-done(((f32[16,1,32]{2,1,0:T(1,128)}), f32[16,1,32]{2,1,0:T(1,128)S(1)}, u32[]{:S(2)}, u32[]{:S(2)}) %all-to-all-start.5) | async-done | bytes 2080 | tf_op jit(solution)/shard_map/all_to_all | solution.py:153
  (43 shorter events, 4.4 us)
Async XLA Ops:
  4.6 2.2 %copy-start.2 = (s32[2]{0:T(128)S(1)}, s32[2]{0:T(128)}, u32[]{:S(2)}) copy-start(s32[2]{0:T(128)} %param.7) | copy-start | bytes 28
  8.8 19.3 %copy-start.3 = (s32[64]{0:T(128)S(1)}, s32[64]{0:T(128)}, u32[]{:S(2)}) copy-start(s32[64]{0:T(128)} %param.8) | copy-start | bytes 772
  10.0 62.0 %all-to-all-start = ((f16[32,13,8,128]{3,2,1,0:T(8,128)(2,1)}), f16[32,13,8,128]{3,2,1,0:T(8,128)(2,1)S(1)}, u32[]{:S(2)}, u32[]{:S(2)}) async-start(f16[32,13,8,128]{3,2,1,0:T(8,128)(2,1)} %pad_maximum_fusion), calls=%async_computation | async-start | bytes 1703936 | tf_op jit(solution)/shard_map/all_to_all | solution.py:159
  82.5 52.9 %all-to-all-start.1 = ((bf16[32,12,8,128]{3,2,1,0:T(8,128)(2,1)}), bf16[32,12,8,128]{3,2,1,0:T(8,128)(2,1)S(1)}, u32[]{:S(2)}, u32[]{:S(2)}) async-start(bf16[32,12,8,128]{3,2,1,0:T(8,128)(2,1)} %shard_map.77), calls=%async_computation.1 | async-start | bytes 1572864 | tf_op jit(solution)/shard_map/all_to_all | solution.py:160
  135.5 1.6 copy-start
  160.0 30.9 %copy-start.1 = (f32[32,1,2,384]{3,2,1,0:T(2,128)S(1)}, f32[32,1,2,384]{3,2,1,0:T(2,128)}, u32[]{:S(2)}) copy-start(f32[32,1,2,384]{3,2,1,0:T(2,128)} %param.11) | copy-start | bytes 294916
  161.0 21.3 %all-to-all-start.4 = ((f16[4,32,768]{2,1,0:T(8,128)(2,1)}), f16[4,32,768]{2,1,0:T(8,128)(2,1)S(1)}, u32[]{:S(2)}, u32[]{:S(2)}) async-start(f16[4,32,768]{2,1,0:T(8,128)(2,1)} %bitcast.18), calls=%async_computation.4 | async-start | bytes 393216 | tf_op jit(solution)/shard_map/all_to_all | solution.py:146
  183.1 14.3 %all-to-all-start.5 = ((f32[16,1,32]{2,1,0:T(1,128)}), f32[16,1,32]{2,1,0:T(1,128)S(1)}, u32[]{:S(2)}, u32[]{:S(2)}) async-start(f32[16,1,32]{2,1,0:T(1,128)} %broadcast_in_dim.18), calls=%async_computation.5 | async-start | bytes 16384 | tf_op jit(solution)/shard_map/all_to_all | solution.py:153

commit v2 on v1

--- a/solution.py
+++ b/solution.py
@@ -9,32 +9,42 @@
 from jax.sharding import PartitionSpec as P
 
 LINE = ("line_0", "line_1", "line_2")
+RECEIVER = ("line_1", "line_2", "line_0")
+PLANE = ("line_1", "line_2")
 LOW_SCALE = 2048.0
 
 
-def phase_tables(line_owner, length):
-    wavenum = jnp.arange(length, dtype=jnp.int32)
-    owner = line_owner.reshape(32, 2).T.reshape(64)
-    wavenum = wavenum.reshape(32, 2).T.reshape(64)
-    products = wavenum[:, None] * owner[None, :] % length
-    angles = products.astype(jnp.float32) * (2.0 * math.pi / length)
+def by_receiver_owner(values):
+    return values.reshape(4, 4, 2, 2).transpose(3, 1, 2, 0).reshape(64)
+
+
+def by_line_owner(values):
+    return values.reshape(32, 2).T.reshape(64)
+
+
+def phases(wavenum, owner):
+    products = wavenum[:, None] * owner[None, :] % 64
+    angles = products.astype(jnp.float32) * (2.0 * math.pi / 64)
     return (jnp.cos(angles), jnp.sin(angles))
 
 
 def in_two_terms(table):
-    high = table.astype(jnp.bfloat16)
-    low = (table - high.astype(jnp.float32)).astype(jnp.bfloat16)
+    high = lax.reduce_precision(table, 8, 7)
+    low = lax.reduce_precision(table - high, 8, 7)
+    high = high.astype(jnp.bfloat16)
+    low = low.astype(jnp.bfloat16)
     return jnp.concatenate(
         [jnp.concatenate([high, high], 1), jnp.concatenate([low, low], 1)], 0
     )
 
 
 def transform_tables(line_owner):
-    length = line_owner.shape[0]
-    cosine, sine = phase_tables(line_owner, length)
+    wavenum = by_receiver_owner(jnp.arange(64, dtype=jnp.int32))
+    cosine, sine = phases(wavenum, by_receiver_owner(line_owner))
     forward = jnp.stack([jnp.stack([cosine, sine]), jnp.stack([-sine, cosine])])
     forward = forward.reshape(2, 2, 64, 2, 32).transpose(0, 2, 3, 1, 4).reshape(128, 128)
-    inverse = jnp.stack([jnp.stack([cosine.T, -sine.T]), jnp.stack([sine.T, cosine.T])]) / length
+    cosine, sine = phases(wavenum, by_line_owner(line_owner))
+    inverse = jnp.stack([jnp.stack([cosine.T, -sine.T]), jnp.stack([sine.T, cosine.T])]) / 64
     inverse = inverse.reshape(2, 2, 2, 32, 64).transpose(2, 0, 3, 1, 4).reshape(128, 128)
     return in_two_terms(forward), in_two_terms(inverse)
 
@@ -140,6 +150,40 @@
     return jnp.concatenate([live_field, jnp.concatenate([high, low], 3)], 1)
 
 
+def panel_blocks(reflection):
+    panel = reflection[0].reshape(4, 4, 2, 32, 1024).transpose(2, 1, 0, 3, 4).reshape(1024, 1024)
+    taken = jnp.arange(1024, dtype=jnp.int32)
+    part, line, device, receiver = taken // 512, taken // 256 % 2, taken // 32 % 8, taken % 32
+    place = ((device * 2 + part) * 2 + line) * 32 + receiver
+    moved = (place[:, None] == taken[None, :]).astype(jnp.bfloat16)
+    panel = jnp.dot(panel, moved, preferred_element_type=jnp.float32).astype(jnp.bfloat16)
+    return panel.reshape(1024, 8, 128).transpose(1, 0, 2)
+
+
+def exchanged(blocks):
+    rank = lax.axis_index(PLANE)
+    received = [lax.dynamic_index_in_dim(blocks, rank, keepdims=False)]
+    for distance in range(1, 8):
+        block = lax.dynamic_index_in_dim(blocks, rank ^ distance, keepdims=False)
+        pairs = [(i, i ^ distance) for i in range(8)]
+        received.append(lax.ppermute(block, PLANE, pairs))
+    return received
+
+
+def panel_halves(received):
+    rank = lax.axis_index(PLANE)
+    core = lax.axis_index("line_2")
+    stack = jnp.stack(received)
+    halves = []
+    for half in (1 - core, core):
+        rows = [
+            lax.dynamic_slice(stack, (rank ^ source, half * 512, 0), (1, 512, 128))[0]
+            for source in range(8)
+        ]
+        halves.append(jnp.concatenate(rows, 1))
+    return halves
+
+
 def summed(blocks, axis, scale):
     count = lax.axis_size(axis)
     blocks = (blocks * scale).astype(jnp.float16).reshape(count, -1, blocks.shape[-1])
@@ -155,23 +199,30 @@
 
 def on_device(field, live_count, line_owner, decomposer, reflection, direct_wave):
     forward, inverse = transform_tables(line_owner)
+    total_freqs = lax.axis_size("freq")
+    weight = 2.0 * (lax.axis_index("freq") + 1).astype(jnp.float32) / (total_freqs * (total_freqs + 1))
+    weight = jnp.full((32,), weight)
     message = outgoing(field, live_count, decomposer)
-    message = lax.all_to_all(message, LINE, 0, 0, tiled=True)
-    wave = lax.all_to_all(middle(message, forward, inverse), LINE, 0, 0, tiled=True)
-    wave = wave.reshape(32, 2, 2, 3, 8, 128).transpose(2, 1, 0, 4, 3, 5).reshape(2, 512, 384)
-    panel = reflection[0].reshape(4, 4, 2, 32, 1024).transpose(2, 1, 0, 3, 4).reshape(1024, 1024)
-    stacked = jnp.concatenate(
-        [jnp.concatenate([wave[0], wave[1]], 1), jnp.concatenate([-wave[1], wave[0]], 1)], 0
-    )
-    product = jnp.dot(panel, stacked, preferred_element_type=jnp.float32)
-    product = summed(product, "line_2", 1.0)
+    message, reflection, weight = lax.optimization_barrier((message, reflection, weight))
+    message = lax.all_to_all(message, RECEIVER, 0, 0, tiled=True)
+    received = exchanged(panel_blocks(reflection))
+    wave = middle(message, forward, inverse)
+    wave = lax.all_to_all(wave, "line_0", 0, 0, tiled=True)
+    other_panel, own_panel = panel_halves(received)
+    wave = wave.reshape(4, 8, 2, 2, 3, 8, 128).transpose(3, 1, 2, 0, 5, 4, 6).reshape(2, 8, 64, 384)
+    stacked = jnp.stack(
+        [jnp.concatenate([wave[0], wave[1]], 2), jnp.concatenate([-wave[1], wave[0]], 2)], 1
+    ).reshape(1024, 768)
+    sent = jnp.dot(other_panel, stacked, preferred_element_type=jnp.float32).astype(jnp.float16)
+    sent = lax.ppermute(sent, "line_2", [(0, 1), (1, 0)])
+    product = jnp.dot(own_panel, stacked, preferred_element_type=jnp.float32)
+    product = product + sent.astype(jnp.float32)
     product = summed(product, "line_1", 0.5)
     product = summed(product, "line_0", 0.125)
     reflected = product.reshape(32, 1, 2, 384)
     focusing = direct_wave - reflected
-    total_freqs = lax.axis_size("freq")
-    weight = 2.0 * (lax.axis_index("freq") + 1).astype(jnp.float32) / (total_freqs * (total_freqs + 1))
     partial_value = jnp.sum(reflected * reflected, axis=(1, 2, 3)) * weight
+    focusing, partial_value = lax.optimization_barrier((focusing, partial_value))
     energy_sum = over_copies(partial_value, "freq")
     trace_energy = jnp.sqrt(energy_sum / 768 + 1e-06)
     return (focusing, trace_energy)

time: 199 us -> 194 us (0.975)
  waiting for transfers between devices: 103 us -> 24.5 us
  blocking collectives: 20.3 us -> 64.6 us
  local copies, waits for them, and re-layouts: 15.3 us -> 26 us
  starting transfers between devices: 40 us -> 49.3 us
  matrix products: 1.83 us -> 8.65 us
    all_to_all x4 -> x2, waiting for transfers between devices: 103 us -> 15.8 us  [the longest x1 9.63 us: on_device(): wave = lax.all_to_all(wave, 'line_0', 0, 0, tiled=True)]
    all_to_all x2, blocking collectives: 20.3 us -> 51.4 us  [summed(): blocks = lax.all_to_all(blocks, axis, 0, 0, tiled=True)]
    ppermute x0 -> x8, starting transfers between devices: none -> 24.1 us  [the longest x7 22.2 us: exchanged(): received.append(lax.ppermute(block, PLANE, pairs))]
    all_to_all x4 -> x2, starting transfers between devices: 40 us -> 25.2 us  [the longest x1 18.1 us: on_device(): message = lax.all_to_all(message, RECEIVER, 0, 0, tiled=True)]
    all_to_all x0 -> x1, blocking collectives: none -> 13.3 us  [over_copies(): return lax.all_to_all(shards, axis, 0, 0, tiled=True).sum(axis=0)]
    unnamed x9 -> x23, local copies, waits for them, and re-layouts: 4.21 us -> 14.1 us
    ppermute x0 -> x8, waiting for transfers between devices: none -> 8.67 us  [the longest x7 6.42 us: exchanged(): received.append(lax.ppermute(block, PLANE, pairs))]
    dot_general x1 -> x3, matrix products: 1.83 us -> 8.65 us  [the longest x1 4.06 us: panel_blocks(): jnp.dot(panel, moved, preferred_element_type=jnp.float32)]
  transfers between devices with their start and end apart: 4 -> 10, of which waited for: 4 -> 4; matrix products, arithmetic and copies ran while one was open for 4% -> 14% of each run, Pallas kernels for 0% -> 5%
where the time goes in v2:
time: 194 us; the launch traced here: 192 us
  blocking collectives  64.6 us (33%)
  starting transfers between devices  49.3 us (25%)
  local copies, waits for them, and re-layouts  26 us (13%)
  waiting for transfers between devices  24.5 us (13%)
  Pallas kernels  9.21 us (5%)
  other arithmetic  9.05 us (5%)
  matrix products  8.65 us (4%)
    all_to_all x2, blocking collectives, summed(): blocks = lax.all_to_all(blocks, axis, 0, 0, tiled=True)  51.4 us
    ppermute x7, starting transfers between devices, exchanged(): received.append(lax.ppermute(block, PLANE, pairs))  22.2 us
    all_to_all x1, starting transfers between devices, on_device(): message = lax.all_to_all(message, RECEIVER, 0, 0, tiled=True)  18.1 us
    unnamed x23, local copies, waits for them, and re-layouts  14.1 us
    all_to_all x1, blocking collectives, over_copies(): return lax.all_to_all(shards, axis, 0, 0, tiled=True).sum(axis=0)  13.3 us
    all_to_all x1, waiting for transfers between devices, on_device(): wave = lax.all_to_all(wave, 'line_0', 0, 0, tiled=True)  9.63 us
    pallas_call x1, Pallas kernels, middle(): pl.pallas_call(middle_kernel, out_shape=jax.ShapeDtypeStruct((32, 12, 8,...  9.21 us
    all_to_all x1, starting transfers between devices, on_device(): wave = lax.all_to_all(wave, 'line_0', 0, 0, tiled=True)  7.11 us
  transfers between devices with their start and end apart: 10, of which 4 were waited for; matrix products, arithmetic and copies ran while one was open for 14% of the time, Pallas kernels for 5%

profile of v2, /device:TPU:2, one launch (start us, length us, event | category | flops | bytes accessed | tf_op | source)
XLA Modules:
  0.0 192.5 jit_solution(8958296986813127346)
XLA Ops:
  1.9 2.8 %copy.58 = f32[1,2,4,96,2,256]{3,2,5,4,1,0:T(4,128)S(1)} copy(f32[1,2,4,96,2,256]{5,4,3,2,1,0:T(2,128)} %param.6) | data formatting | bytes 3145728 | tf_op args[0]
  4.7 2.2 %squeeze.82 = f32[2,384,2,32,8]{1,4,3,2,0:T(8,128)} reshape(f32[1,2,4,96,2,256]{3,2,5,4,1,0:T(4,128)S(1)} %copy.58) | data formatting | bytes 3145728 | tf_op jit(solution)/shard_map/squeeze | solution.py:143
  10.0 18.1 %all-to-all-start = ((f16[32,13,8,128]{3,2,1,0:T(8,128)(2,1)}), f16[32,13,8,128]{3,2,1,0:T(8,128)(2,1)S(1)}, u32[]{:S(2)}, u32[]{:S(2)}) async-start(f16[32,13,8,128]{3,2,1,0:T(8,128)(2,1)} %pad_maximum_fusion.1), calls=%async_computation | async-start | bytes 1703936 | tf_op jit(solution)/shard_map/all_to_all | solution.py:207
  28.1 3.2 %reshape_squeeze.7 = bf16[4,4,2,32,1024]{4,3,2,1,0:T(8,128)(2,1)S(1)} reshape(bf16[1,1024,2,512]{3,2,1,0:T(2,128)(2,1)} %param.10) | data formatting | bytes 4194304 | tf_op jit(solution)/shard_map/reshape;squeeze | solution.py:154
  32.9 4.1 %fusion.2 = bf16[1024,1024]{0,1:T(8,128)(2,1)S(1)} fusion(bf16[1024,1024]{1,0:T(8,128)(2,1)} %bitcast.118, s32[1024]{0:T(1024)S(1)} %fusion.33), kind=kOutput, calls=%fused_computation.3 | convolution fusion | flops 2149580800 | bytes 4198400 | tf_op jit(solution)/shard_map/dot_general | solution.py:159
  39.6 2.2 %collective-permute-start = (bf16[1024,128]{0,1:T(8,128)(2,1)}, bf16[1024,128]{0,1:T(8,128)(2,1)}, u32[]{:S(2)}, u32[]{:S(2)}) collective-permute-start(bf16[1024,128]{0,1:T(8,128)(2,1)} %get-tuple-element.36), channel_id=1, source_target_pairs={{0,1},{1,0},{2,3},{3,2},{4,5},{5,4},{6,7},{7,6},{8,9},{9,8},{10,11... | collective-permute-start | bytes 786440 | tf_op jit(solution)/shard_map/ppermute | solution.py:169
  41.8 3.5 %collective-permute-start.1 = (bf16[1024,128]{0,1:T(8,128)(2,1)}, bf16[1024,128]{0,1:T(8,128)(2,1)}, u32[]{:S(2)}, u32[]{:S(2)}) collective-permute-start(bf16[1024,128]{0,1:T(8,128)(2,1)} %get-tuple-element.35), channel_id=1, source_target_pairs={{0,2},{1,3},{2,0},{3,1},{4,6},{5,7},{6,4},{7,5},{8,10},{9,11},{10,... | collective-permute-start | bytes 786440 | tf_op jit(solution)/shard_map/ppermute | solution.py:169
  45.4 1.9 collective-permute-start.2
  47.3 5.1 %collective-permute-start.3 = (bf16[1024,128]{0,1:T(8,128)(2,1)}, bf16[1024,128]{0,1:T(8,128)(2,1)S(1)}, u32[]{:S(2)}, u32[]{:S(2)}) collective-permute-start(bf16[1024,128]{0,1:T(8,128)(2,1)} %get-tuple-element.33), channel_id=1, source_target_pairs={{0,4},{1,5},{2,6},{3,7},{4,0},{5,1},{6,2},{7,3},{8,12},{9,13},{10,... | collective-permute-start | bytes 786440 | tf_op jit(solution)/shard_map/ppermute | solution.py:169
  52.5 2.0 %collective-permute-start.4 = (bf16[1024,128]{0,1:T(8,128)(2,1)}, bf16[1024,128]{0,1:T(8,128)(2,1)S(1)}, u32[]{:S(2)}, u32[]{:S(2)}) collective-permute-start(bf16[1024,128]{0,1:T(8,128)(2,1)} %get-tuple-element.32), channel_id=1, source_target_pairs={{0,5},{1,4},{2,7},{3,6},{4,1},{5,0},{6,3},{7,2},{8,13},{9,12},{10,... | collective-permute-start | bytes 786440 | tf_op jit(solution)/shard_map/ppermute | solution.py:169
  59.4 5.0 %collective-permute-start.5 = (bf16[1024,128]{0,1:T(8,128)(2,1)}, bf16[1024,128]{0,1:T(8,128)(2,1)}, u32[]{:S(2)}, u32[]{:S(2)}) collective-permute-start(bf16[1024,128]{0,1:T(8,128)(2,1)} %get-tuple-element.31), channel_id=1, source_target_pairs={{0,6},{1,7},{2,4},{3,5},{4,2},{5,3},{6,0},{7,1},{8,14},{9,15},{10,... | collective-permute-start | bytes 786440 | tf_op jit(solution)/shard_map/ppermute | solution.py:169
  65.4 6.2 %all-to-all-done = f16[32,13,8,128]{3,2,1,0:T(8,128)(2,1)S(1)} async-done(((f16[32,13,8,128]{3,2,1,0:T(8,128)(2,1)}), f16[32,13,8,128]{3,2,1,0:T(8,128)(2,1)S(1)}, u32[]{:S(2)}, u32[]{:S(2)}) %all-to-all-start) | async-done | bytes 852000 | tf_op jit(solution)/shard_map/all_to_all | solution.py:207
  73.0 9.2 %shard_map.77 = bf16[32,12,8,128]{3,2,1,0:T(8,128)(2,1)} custom-call(f32[3328,128]{1,0:T(8,128)} %bitcast_convert_fusion.message_ref, bf16[256,256]{1,0:T(8,128)(2,1)} %get-tuple-element.53.forward_ref, bf16[256,256]{1,0:T(8,128)(2,1)} %get-tuple-element.54.inverse_ref), custom_call_target="tpu_custom_call" | custom-call | tf_op jit(solution)/shard_map/pallas_call | solution.py:131
  82.2 7.1 %all-to-all-start.1 = ((bf16[32,12,8,128]{3,2,1,0:T(8,128)(2,1)}), bf16[32,12,8,128]{3,2,1,0:T(8,128)(2,1)S(1)}, u32[]{:S(2)}, u32[]{:S(2)}) async-start(bf16[32,12,8,128]{3,2,1,0:T(8,128)(2,1)} %shard_map.77), calls=%async_computation.1 | async-start | bytes 1572864 | tf_op jit(solution)/shard_map/all_to_all | solution.py:210
  89.3 2.4 %collective-permute-start.6 = (bf16[1024,128]{0,1:T(8,128)(2,1)}, bf16[1024,128]{0,1:T(8,128)(2,1)S(1)}, u32[]{:S(2)}, u32[]{:S(2)}) collective-permute-start(bf16[1024,128]{0,1:T(8,128)(2,1)} %get-tuple-element.30), channel_id=1, source_target_pairs={{0,7},{1,6},{2,5},{3,4},{4,3},{5,2},{6,1},{7,0},{8,15},{9,14},{10,... | collective-permute-start | bytes 786440 | tf_op jit(solution)/shard_map/ppermute | solution.py:169
  94.7 6.4 %collective-permute-done.6 = bf16[1024,128]{0,1:T(8,128)(2,1)S(1)} collective-permute-done((bf16[1024,128]{0,1:T(8,128)(2,1)}, bf16[1024,128]{0,1:T(8,128)(2,1)S(1)}, u32[]{:S(2)}, u32[]{:S(2)}) %collective-permute-start.6) | collective-permute-done | bytes 262176 | tf_op jit(solution)/shard_map/ppermute | solution.py:169
  107.0 9.6 %all-to-all-done.1 = bf16[32,12,8,128]{3,2,1,0:T(8,128)(2,1)S(1)} async-done(((bf16[32,12,8,128]{3,2,1,0:T(8,128)(2,1)}), bf16[32,12,8,128]{3,2,1,0:T(8,128)(2,1)S(1)}, u32[]{:S(2)}, u32[]{:S(2)}) %all-to-all-start.1) | async-done | bytes 786464 | tf_op jit(solution)/shard_map/all_to_all | solution.py:210
  117.4 2.3 %convolution_convert_fusion = f16[512,768]{1,0:T(8,128)(2,1)S(1)} fusion(bf16[512,1024]{0,1:T(8,128)(2,1)} %get-tuple-element.14, bf16[1024,768]{1,0:T(8,128)(2,1)S(1)} %bitcast.119), kind=kOutput, calls=%fused_computation.8 | convolution fusion | flops 805699584 | bytes 3407872 | tf_op jit(solution)/shard_map/dot_general | solution.py:216
  119.7 1.9 collective-permute-start.7
  121.6 2.3 %collective-permute-done.7 = f16[512,768]{1,0:T(8,128)(2,1)S(1)} collective-permute-done((f16[512,768]{1,0:T(8,128)(2,1)S(1)}, f16[512,768]{1,0:T(8,128)(2,1)S(1)}, u32[]{:S(2)}, u32[]{:S(2)}) %collective-permute-start.7) | collective-permute-done | bytes 786464 | tf_op jit(solution)/shard_map/ppermute | solution.py:217
  123.8 2.3 %multiply_convert_fusion = f16[512,768]{1,0:T(8,128)(2,1)S(1)} fusion(f16[512,768]{1,0:T(8,128)(2,1)S(1)} %collective-permute-done.7, bf16[512,1024]{0,1:T(8,128)(2,1)} %get-tuple-element.15, bf16[1024,768]{1,0:T(8,128)(2,1)S(1)} %bitcast.120), kind=kOutput, calls=%fused_computation.6 | convolution fusion | flops 806879232 | bytes 4194304 | tf_op jit(solution)/shard_map/dot_general | solution.py:218
  126.2 15.4 %all_to_all.26 = f16[4,128,768]{2,1,0:T(8,128)(2,1)S(1)} all-to-all(f16[4,128,768]{2,1,0:T(8,128)(2,1)S(1)} %bitcast.123), channel_id=1, replica_groups=mesh['freq'=16,'line_0'=4,'line_1'=4,'line_2'=2] {'line_1'}, dimensions={0} | all-to-all | bytes 1572864 | tf_op jit(solution)/shard_map/all_to_all | solution.py:190
  141.8 36.0 %all_to_all.27 = f16[4,32,768]{2,1,0:T(8,128)(2,1)S(1)} all-to-all(f16[4,32,768]{2,1,0:T(8,128)(2,1)S(1)} %bitcast.124), channel_id=1, replica_groups=mesh['freq'=16,'line_0'=4,'line_1'=4,'line_2'=2] {'line_0'}, dimensions={0} | all-to-all | bytes 393216 | tf_op jit(solution)/shard_map/all_to_all | solution.py:190
  178.7 13.3 %all_to_all.28 = f32[16,1,32]{2,1,0:T(1,128)S(1)} all-to-all(f32[16,1,32]{2,1,0:T(1,128)S(1)} %broadcast_in_dim.24), channel_id=1, replica_groups=mesh['freq'=16,'line_0'=4,'line_1'=4,'line_2'=2] {'freq'}, dimensions={0} | all-to-all | bytes 4096 | tf_op jit(solution)/shard_map/all_to_all | solution.py:197
  (79 shorter events, 26.9 us)
Async XLA Ops:
  4.6 2.2 %copy-start.3 = (s32[2]{0:T(128)S(1)}, s32[2]{0:T(128)}, u32[]{:S(2)}) copy-start(s32[2]{0:T(128)} %param.7) | copy-start | bytes 28
  10.0 61.6 %all-to-all-start = ((f16[32,13,8,128]{3,2,1,0:T(8,128)(2,1)}), f16[32,13,8,128]{3,2,1,0:T(8,128)(2,1)S(1)}, u32[]{:S(2)}, u32[]{:S(2)}) async-start(f16[32,13,8,128]{3,2,1,0:T(8,128)(2,1)} %pad_maximum_fusion.1), calls=%async_computation | async-start | bytes 1703936 | tf_op jit(solution)/shard_map/all_to_all | solution.py:207
  37.0 1.3 copy-start
  37.0 17.5 %copy-start.2 = (s32[64]{0:T(128)S(1)}, s32[64]{0:T(128)}, u32[]{:S(2)}) copy-start(s32[64]{0:T(128)} %param.8) | copy-start | bytes 772
  39.6 19.8 %collective-permute-start = (bf16[1024,128]{0,1:T(8,128)(2,1)}, bf16[1024,128]{0,1:T(8,128)(2,1)}, u32[]{:S(2)}, u32[]{:S(2)}) collective-permute-start(bf16[1024,128]{0,1:T(8,128)(2,1)} %get-tuple-element.36), channel_id=1, source_target_pairs={{0,1},{1,0},{2,3},{3,2},{4,5},{5,4},{6,7},{7,6},{8,9},{9,8},{10,11... | collective-permute-start | bytes 786440 | tf_op jit(solution)/shard_map/ppermute | solution.py:169
  41.8 47.5 %collective-permute-start.1 = (bf16[1024,128]{0,1:T(8,128)(2,1)}, bf16[1024,128]{0,1:T(8,128)(2,1)}, u32[]{:S(2)}, u32[]{:S(2)}) collective-permute-start(bf16[1024,128]{0,1:T(8,128)(2,1)} %get-tuple-element.35), channel_id=1, source_target_pairs={{0,2},{1,3},{2,0},{3,1},{4,6},{5,7},{6,4},{7,5},{8,10},{9,11},{10,... | collective-permute-start | bytes 786440 | tf_op jit(solution)/shard_map/ppermute | solution.py:169
  45.4 47.3 %collective-permute-start.2 = (bf16[1024,128]{0,1:T(8,128)(2,1)}, bf16[1024,128]{0,1:T(8,128)(2,1)}, u32[]{:S(2)}, u32[]{:S(2)}) collective-permute-start(bf16[1024,128]{0,1:T(8,128)(2,1)} %get-tuple-element.34), channel_id=1, source_target_pairs={{0,3},{1,2},{2,1},{3,0},{4,7},{5,6},{6,5},{7,4},{8,11},{9,10},{10,... | collective-permute-start | bytes 786440 | tf_op jit(solution)/shard_map/ppermute | solution.py:169
  47.3 46.4 %collective-permute-start.3 = (bf16[1024,128]{0,1:T(8,128)(2,1)}, bf16[1024,128]{0,1:T(8,128)(2,1)S(1)}, u32[]{:S(2)}, u32[]{:S(2)}) collective-permute-start(bf16[1024,128]{0,1:T(8,128)(2,1)} %get-tuple-element.33), channel_id=1, source_target_pairs={{0,4},{1,5},{2,6},{3,7},{4,0},{5,1},{6,2},{7,3},{8,12},{9,13},{10,... | collective-permute-start | bytes 786440 | tf_op jit(solution)/shard_map/ppermute | solution.py:169
  52.5 41.2 %collective-permute-start.4 = (bf16[1024,128]{0,1:T(8,128)(2,1)}, bf16[1024,128]{0,1:T(8,128)(2,1)S(1)}, u32[]{:S(2)}, u32[]{:S(2)}) collective-permute-start(bf16[1024,128]{0,1:T(8,128)(2,1)} %get-tuple-element.32), channel_id=1, source_target_pairs={{0,5},{1,4},{2,7},{3,6},{4,1},{5,0},{6,3},{7,2},{8,13},{9,12},{10,... | collective-permute-start | bytes 786440 | tf_op jit(solution)/shard_map/ppermute | solution.py:169
  59.4 34.3 %collective-permute-start.5 = (bf16[1024,128]{0,1:T(8,128)(2,1)}, bf16[1024,128]{0,1:T(8,128)(2,1)}, u32[]{:S(2)}, u32[]{:S(2)}) collective-permute-start(bf16[1024,128]{0,1:T(8,128)(2,1)} %get-tuple-element.31), channel_id=1, source_target_pairs={{0,6},{1,7},{2,4},{3,5},{4,2},{5,3},{6,0},{7,1},{8,14},{9,15},{10,... | collective-permute-start | bytes 786440 | tf_op jit(solution)/shard_map/ppermute | solution.py:169
  82.2 34.4 %all-to-all-start.1 = ((bf16[32,12,8,128]{3,2,1,0:T(8,128)(2,1)}), bf16[32,12,8,128]{3,2,1,0:T(8,128)(2,1)S(1)}, u32[]{:S(2)}, u32[]{:S(2)}) async-start(bf16[32,12,8,128]{3,2,1,0:T(8,128)(2,1)} %shard_map.77), calls=%async_computation.1 | async-start | bytes 1572864 | tf_op jit(solution)/shard_map/all_to_all | solution.py:210
  89.3 11.8 %collective-permute-start.6 = (bf16[1024,128]{0,1:T(8,128)(2,1)}, bf16[1024,128]{0,1:T(8,128)(2,1)S(1)}, u32[]{:S(2)}, u32[]{:S(2)}) collective-permute-start(bf16[1024,128]{0,1:T(8,128)(2,1)} %get-tuple-element.30), channel_id=1, source_target_pairs={{0,7},{1,6},{2,5},{3,4},{4,3},{5,2},{6,1},{7,0},{8,15},{9,14},{10,... | collective-permute-start | bytes 786440 | tf_op jit(solution)/shard_map/ppermute | solution.py:169
  119.7 4.2 %collective-permute-start.7 = (f16[512,768]{1,0:T(8,128)(2,1)S(1)}, f16[512,768]{1,0:T(8,128)(2,1)S(1)}, u32[]{:S(2)}, u32[]{:S(2)}) collective-permute-start(f16[512,768]{1,0:T(8,128)(2,1)S(1)} %convolution_convert_fusion), channel_id=1, source_target_pairs={{0,1},{1,0},{2,3},{3,2},{4,5},{5,4},{6,7},{7,6},{8,9},{9,8},{10,11... | collective-permute-start | bytes 2359304 | tf_op jit(solution)/shard_map/ppermute | solution.py:217
  126.2 51.7 %copy-start.1 = (f32[32,1,2,384]{3,2,1,0:T(2,128)S(1)}, f32[32,1,2,384]{3,2,1,0:T(2,128)}, u32[]{:S(2)}) copy-start(f32[32,1,2,384]{3,2,1,0:T(2,128)} %param.11) | copy-start | bytes 294916

commit v3 on v2

--- a/solution.py
+++ b/solution.py
@@ -11,7 +11,7 @@
 LINE = ("line_0", "line_1", "line_2")
 RECEIVER = ("line_1", "line_2", "line_0")
 PLANE = ("line_1", "line_2")
-LOW_SCALE = 2048.0
+LOW_SCALE = 256.0
 
 
 def by_receiver_owner(values):
@@ -42,17 +42,30 @@
     wavenum = by_receiver_owner(jnp.arange(64, dtype=jnp.int32))
     cosine, sine = phases(wavenum, by_receiver_owner(line_owner))
     forward = jnp.stack([jnp.stack([cosine, sine]), jnp.stack([-sine, cosine])])
-    forward = forward.reshape(2, 2, 64, 2, 32).transpose(0, 2, 3, 1, 4).reshape(128, 128)
+    forward = forward.transpose(0, 2, 1, 3).reshape(128, 128)
     cosine, sine = phases(wavenum, by_line_owner(line_owner))
     inverse = jnp.stack([jnp.stack([cosine.T, -sine.T]), jnp.stack([sine.T, cosine.T])]) / 64
     inverse = inverse.reshape(2, 2, 2, 32, 64).transpose(2, 0, 3, 1, 4).reshape(128, 128)
     return in_two_terms(forward), in_two_terms(inverse)
 
 
-def middle_kernel(message_ref, forward_ref, inverse_ref, out_ref, wave_ref):
-    lane = lax.broadcasted_iota(jnp.int32, (64, 128), 1)
+def spread_table():
+    row = jnp.arange(128, dtype=jnp.int32)[:, None]
+    column = jnp.arange(2048, dtype=jnp.int32)[None, :]
+    low, line, part, target, source = row // 64, row // 32 % 2, row // 16 % 2, row // 4 % 4, row % 4
+    shift, goal = column // 128 % 4, column // 32 % 4
+    found = (line == column // 1024) & (part == column // 512 % 2) & (target == goal)
+    found = found & (source == (goal - shift) % 4)
+    return jnp.where(found, jnp.where(low == 1, 1.0 / LOW_SCALE, 1.0), 0.0).astype(jnp.bfloat16)
+
+
+def middle_kernel(message_ref, forward_ref, inverse_ref, spread_ref, out_ref, wave_ref, spread_out_ref):
     forward = forward_ref[...]
     inverse = inverse_ref[...]
+    operators = jnp.concatenate(
+        [message_ref[pl.ds(96 + r, 32, stride=104), :] for r in range(8)], 0
+    ).astype(jnp.bfloat16)
+    spread_out_ref[...] = jnp.dot(operators, spread_ref[...], preferred_element_type=jnp.float32)
 
     def transform(table, value):
         high = value.astype(jnp.bfloat16)
@@ -70,55 +83,33 @@
             for t in range(3)
         ]
         spectrum = transform(forward, jnp.concatenate(tiles, 1))
-        operator = message_ref[pl.ds(96 + r, 32, stride=104), :]
-        operator = operator + pltpu.roll(operator, 64, 1) * jnp.float32(1.0 / LOW_SCALE)
-        operator = jnp.concatenate([operator, pltpu.roll(operator, 96, 1)], 0)
-        parts = []
-        for part in range(2):
-            t0, t1, t2 = [
-                spectrum[64 * part : 64 * part + 64, 128 * t : 128 * t + 128] for t in range(3)
-            ]
-            parts.append(
-                [
-                    t0,
-                    pltpu.roll(jnp.where(lane >= 96, t0, t1), 32, 1),
-                    pltpu.roll(jnp.where(lane >= 64, t1, t2), 64, 1),
-                    pltpu.roll(t2, 96, 1),
-                ]
-            )
-        rows = [[], []]
-        for target in range(4):
+        decomposed = []
+        for t in range(3):
+            field_real = spectrum[:64, 128 * t : 128 * t + 128]
+            field_imag = spectrum[64:, 128 * t : 128 * t + 128]
             real_sum = None
             imag_sum = None
-            for source in range(4):
-                at = target * 4 + source
-                weight_real = operator[:, at : at + 1]
-                weight_imag = operator[:, 16 + at : 17 + at]
-                field_real = parts[0][source]
-                field_imag = parts[1][source]
-                term_real = weight_real * field_real - weight_imag * field_imag
-                term_imag = weight_real * field_imag + weight_imag * field_real
+            for shift in range(4):
+                weight_real, weight_imag = [
+                    jnp.concatenate(
+                        [
+                            spread_out_ref[
+                                32 * r : 32 * r + 32, pl.ds(1024 * line + 512 * part + 128 * shift, 128)
+                            ]
+                            for line in range(2)
+                        ],
+                        0,
+                    )
+                    for part in range(2)
+                ]
+                moved_real = pltpu.roll(field_real, 32 * shift, 1) if shift else field_real
+                moved_imag = pltpu.roll(field_imag, 32 * shift, 1) if shift else field_imag
+                term_real = weight_real * moved_real - weight_imag * moved_imag
+                term_imag = weight_real * moved_imag + weight_imag * moved_real
                 real_sum = term_real if real_sum is None else real_sum + term_real
                 imag_sum = term_imag if imag_sum is None else imag_sum + term_imag
-            rows[0].append(real_sum)
-            rows[1].append(imag_sum)
-        decomposed = []
-        for part in range(2):
-            q0, q1, q2, q3 = rows[part]
-            q1 = pltpu.roll(q1, 96, 1)
-            q2 = pltpu.roll(q2, 64, 1)
-            q3 = pltpu.roll(q3, 32, 1)
-            decomposed.append(
-                jnp.concatenate(
-                    [
-                        jnp.where(lane < 96, q0, q1),
-                        jnp.where(lane < 64, q1, q2),
-                        jnp.where(lane < 32, q2, q3),
-                    ],
-                    1,
-                )
-            )
-        wave = transform(inverse, jnp.concatenate(decomposed, 0))
+            decomposed.append(jnp.concatenate([real_sum, imag_sum], 0))
+        wave = transform(inverse, jnp.concatenate(decomposed, 1))
         for g in range(4):
             for t in range(3):
                 wave_ref[pl.ds((g * 3 + t) * 8 + r, 32, stride=96), :] = wave[
@@ -127,27 +118,68 @@
     out_ref[...] = wave_ref[...].reshape(32, 12, 8, 128).astype(jnp.bfloat16)
 
 
-def middle(message, forward, inverse):
+def middle(message, forward, inverse, spread):
     return pl.pallas_call(
         middle_kernel,
         out_shape=jax.ShapeDtypeStruct((32, 12, 8, 128), jnp.bfloat16),
-        in_specs=[pl.BlockSpec(memory_space=pltpu.VMEM)] * 3,
+        in_specs=[pl.BlockSpec(memory_space=pltpu.VMEM)] * 4,
         out_specs=pl.BlockSpec(memory_space=pltpu.VMEM),
-        scratch_shapes=[pltpu.VMEM((3072, 128), jnp.float32)],
-    )(message.astype(jnp.float32).reshape(3328, 128), forward, inverse)
+        scratch_shapes=[
+            pltpu.VMEM((3072, 128), jnp.float32),
+            pltpu.VMEM((256, 2048), jnp.float32),
+        ],
+    )(message.astype(jnp.float32).reshape(3328, 128), forward, inverse, spread)
+
+
+def outgoing_kernel(live_ref, field_ref, operator_ref, tiles_ref, operator_out_ref):
+    row = lax.broadcasted_iota(jnp.int32, (128, 128), 0)
+    for line in range(2):
+        for half in range(2):
+            live = row + 128 * half < live_ref[line]
+            for t in range(3):
+                block = jnp.concatenate(
+                    [
+                        field_ref[pl.ds(384 * c + 128 * t + 2 * half + line, 32, stride=4), :]
+                        for c in range(4)
+                    ],
+                    0,
+                )
+                block = jnp.where(live, block.T, jnp.float32(0.0))
+                tiles_ref[16 * half : 16 * half + 16, 3 * line + t] = block.reshape(16, 8, 128)
+    for half in range(2):
+        high = []
+        low = []
+        for line in range(2):
+            block = operator_ref[pl.ds(2 * half + line, 32, stride=4), :]
+            rounded = block.astype(jnp.bfloat16).astype(jnp.float32)
+            rest = ((block - rounded) * LOW_SCALE).astype(jnp.bfloat16).astype(jnp.float32)
+            high.append(rounded)
+            low.append(rest)
+        block = jnp.concatenate(high + low, 0).T
+        operator_out_ref[16 * half : 16 * half + 16, 0] = block.reshape(16, 8, 128)
 
 
 def outgoing(field, live_count, decomposer):
-    receivers = field.shape[5]
-    live_mask = jnp.arange(receivers, dtype=jnp.int32)[None, :] < live_count[:, None]
-    live_field = jnp.where(live_mask, field[0], jnp.float32(0.0)).astype(jnp.float16)
-    live_field = live_field.reshape(2, 384, 2, 32, 8)
-    live_field = live_field.transpose(3, 2, 0, 4, 1).reshape(32, 2, 2, 8, 3, 128)
-    live_field = live_field.transpose(0, 1, 2, 4, 3, 5).reshape(32, 12, 8, 128)
-    operator = decomposer[0].reshape(32, 2, 256).transpose(2, 1, 0).reshape(32, 1, 8, 64)
-    high = operator.astype(jnp.float16)
-    low = ((operator - high.astype(jnp.float32)) * LOW_SCALE).astype(jnp.float16)
-    return jnp.concatenate([live_field, jnp.concatenate([high, low], 3)], 1)
+    rows = field.reshape(2, 4, 96, 2, 2, 128).transpose(0, 1, 2, 4, 3, 5).reshape(3072, 128)
+    operator_rows = decomposer.reshape(32, 2, 2, 128).transpose(0, 2, 1, 3).reshape(128, 128)
+    tiles, operators = pl.pallas_call(
+        outgoing_kernel,
+        grid=(2,),
+        out_shape=(
+            jax.ShapeDtypeStruct((32, 12, 8, 128), jnp.float32),
+            jax.ShapeDtypeStruct((32, 1, 8, 128), jnp.float32),
+        ),
+        in_specs=[
+            pl.BlockSpec(memory_space=pltpu.SMEM),
+            pl.BlockSpec((1536, 128), lambda part: (part, 0)),
+            pl.BlockSpec((128, 128), lambda part: (0, 0)),
+        ],
+        out_specs=(
+            pl.BlockSpec((32, 6, 8, 128), lambda part: (0, part, 0, 0)),
+            pl.BlockSpec((32, 1, 8, 128), lambda part: (0, 0, 0, 0)),
+        ),
+    )(live_count, rows, operator_rows)
+    return jnp.concatenate([tiles, operators], 1).astype(jnp.float16)
 
 
 def panel_blocks(reflection):
@@ -206,7 +238,7 @@
     message, reflection, weight = lax.optimization_barrier((message, reflection, weight))
     message = lax.all_to_all(message, RECEIVER, 0, 0, tiled=True)
     received = exchanged(panel_blocks(reflection))
-    wave = middle(message, forward, inverse)
+    wave = middle(message, forward, inverse, spread_table())
     wave = lax.all_to_all(wave, "line_0", 0, 0, tiled=True)
     other_panel, own_panel = panel_halves(received)
     wave = wave.reshape(4, 8, 2, 2, 3, 8, 128).transpose(3, 1, 2, 0, 5, 4, 6).reshape(2, 8, 64, 384)
@@ -219,7 +251,7 @@
     product = product + sent.astype(jnp.float32)
     product = summed(product, "line_1", 0.5)
     product = summed(product, "line_0", 0.125)
-    reflected = product.reshape(32, 1, 2, 384)
+    reflected = product.reshape(32, 2, 3, 4, 32).transpose(0, 1, 3, 2, 4).reshape(32, 1, 2, 384)
     focusing = direct_wave - reflected
     partial_value = jnp.sum(reflected * reflected, axis=(1, 2, 3)) * weight
     focusing, partial_value = lax.optimization_barrier((focusing, partial_value))

time: 194 us -> 190 us (0.979)
  blocking collectives: 64.6 us -> 53.6 us
  starting transfers between devices: 49.3 us -> 56.8 us
  local copies, waits for them, and re-layouts: 26 us -> 21.4 us
  waiting for transfers between devices: 24.5 us -> 27 us
    all_to_all x1 -> x0, blocking collectives: 13.3 us -> none  [over_copies(): return lax.all_to_all(shards, axis, 0, 0, tiled=True).sum(axis=0)]
    all_to_all x0 -> x1, starting transfers between devices: none -> 7.45 us  [over_copies(): return lax.all_to_all(shards, axis, 0, 0, tiled=True).sum(axis=0)]
    all_to_all x0 -> x1, waiting for transfers between devices: none -> 5.83 us  [over_copies(): return lax.all_to_all(shards, axis, 0, 0, tiled=True).sum(axis=0)]
    pallas_call x0 -> x1, Pallas kernels: none -> 2.74 us  [outgoing(): pl.pallas_call(outgoing_kernel, grid=(2,), out_shape=(jax.ShapeDtypeStruc...]
    another operation x0 -> x3, other arithmetic: none -> 2.45 us
    all_to_all x2, blocking collectives: 51.4 us -> 53.6 us  [summed(): blocks = lax.all_to_all(blocks, axis, 0, 0, tiled=True)]
    squeeze x1 -> x0, local copies, waits for them, and re-layouts: 2.19 us -> none  [outgoing(): field[0]]
    all_to_all x1, waiting for transfers between devices: 9.63 us -> 7.45 us  [on_device(): wave = lax.all_to_all(wave, 'line_0', 0, 0, tiled=True)]
  transfers between devices with their start and end apart: 10 -> 11, of which waited for: 4 -> 5; matrix products, arithmetic and copies ran while one was open for 14% -> 15% of each run, Pallas kernels for 5% -> 4%
where the time goes in v3:
time: 190 us; the launch traced here: 189 us
  starting transfers between devices  56.8 us (30%)
  blocking collectives  53.6 us (28%)
  waiting for transfers between devices  27 us (14%)
  local copies, waits for them, and re-layouts  21.4 us (11%)
  other arithmetic  10.3 us (5%)
  Pallas kernels  10.2 us (5%)
  matrix products  8.65 us (5%)
    all_to_all x2, blocking collectives, summed(): blocks = lax.all_to_all(blocks, axis, 0, 0, tiled=True)  53.6 us
    ppermute x7, starting transfers between devices, exchanged(): received.append(lax.ppermute(block, PLANE, pairs))  22.2 us
    all_to_all x1, starting transfers between devices, on_device(): message = lax.all_to_all(message, RECEIVER, 0, 0, tiled=True)  18.1 us
    unnamed x21, local copies, waits for them, and re-layouts  11.9 us
    pallas_call x1, Pallas kernels, middle(): pl.pallas_call(middle_kernel, out_shape=jax.ShapeDtypeStruct((32, 12, 8,...  7.49 us
    all_to_all x1, starting transfers between devices, over_copies(): return lax.all_to_all(shards, axis, 0, 0, tiled=True).sum(axis=0)  7.45 us
    all_to_all x1, waiting for transfers between devices, on_device(): wave = lax.all_to_all(wave, 'line_0', 0, 0, tiled=True)  7.45 us
    all_to_all x1, starting transfers between devices, on_device(): wave = lax.all_to_all(wave, 'line_0', 0, 0, tiled=True)  7.06 us
  transfers between devices with their start and end apart: 11, of which 5 were waited for; matrix products, arithmetic and copies ran while one was open for 15% of the time, Pallas kernels for 4%

profile of v3, /device:TPU:2, one launch (start us, length us, event | category | flops | bytes accessed | tf_op | source)
XLA Modules:
  0.0 189.1 jit_solution(18423231942171427277)
XLA Ops:
  0.6 2.7 %shard_map.77 = (f32[32,12,8,128]{3,2,1,0:T(8,128)}, f32[32,1,8,128]{3,2,1,0:T(8,128)}) custom-call(s32[2]{0:T(128)} %live_ref.1, f32[3072,128]{1,0:T(8,128)} %bitcast.120, f32[128,128]{1,0:T(8,128)} %bitcast.126), custom_call_target="tpu_custom_call" | custom-call | tf_op jit(solution)/shard_map/pallas_call | solution.py:165
  7.0 18.1 %all-to-all-start = ((f16[32,13,8,128]{3,2,1,0:T(8,128)(2,1)}), f16[32,13,8,128]{3,2,1,0:T(8,128)(2,1)S(1)}, u32[]{:S(2)}, u32[]{:S(2)}) async-start(f16[32,13,8,128]{3,2,1,0:T(8,128)(2,1)} %pad_maximum_fusion.1), calls=%async_computation | async-start | bytes 1703936 | tf_op jit(solution)/shard_map/all_to_all | solution.py:239
  25.1 3.2 %reshape_squeeze.3 = bf16[4,4,2,32,1024]{4,3,2,1,0:T(8,128)(2,1)S(1)} reshape(bf16[1,1024,2,512]{3,2,1,0:T(2,128)(2,1)} %param.10) | data formatting | bytes 4194304 | tf_op jit(solution)/shard_map/reshape;squeeze | solution.py:186
  29.9 4.1 %fusion.2 = bf16[1024,1024]{0,1:T(8,128)(2,1)S(1)} fusion(bf16[1024,1024]{1,0:T(8,128)(2,1)} %bitcast.119, s32[1024]{0:T(1024)S(1)} %fusion.46), kind=kOutput, calls=%fused_computation.3 | convolution fusion | flops 2149580800 | bytes 4198400 | tf_op jit(solution)/shard_map/dot_general | solution.py:191
  36.6 2.2 %collective-permute-start = (bf16[1024,128]{0,1:T(8,128)(2,1)}, bf16[1024,128]{0,1:T(8,128)(2,1)}, u32[]{:S(2)}, u32[]{:S(2)}) collective-permute-start(bf16[1024,128]{0,1:T(8,128)(2,1)} %get-tuple-element.48), channel_id=1, source_target_pairs={{0,1},{1,0},{2,3},{3,2},{4,5},{5,4},{6,7},{7,6},{8,9},{9,8},{10,11... | collective-permute-start | bytes 786440 | tf_op jit(solution)/shard_map/ppermute | solution.py:201
  38.8 3.5 %collective-permute-start.1 = (bf16[1024,128]{0,1:T(8,128)(2,1)}, bf16[1024,128]{0,1:T(8,128)(2,1)}, u32[]{:S(2)}, u32[]{:S(2)}) collective-permute-start(bf16[1024,128]{0,1:T(8,128)(2,1)} %get-tuple-element.47), channel_id=1, source_target_pairs={{0,2},{1,3},{2,0},{3,1},{4,6},{5,7},{6,4},{7,5},{8,10},{9,11},{10,... | collective-permute-start | bytes 786440 | tf_op jit(solution)/shard_map/ppermute | solution.py:201
  42.3 1.9 %collective-permute-start.2 = (bf16[1024,128]{0,1:T(8,128)(2,1)}, bf16[1024,128]{0,1:T(8,128)(2,1)}, u32[]{:S(2)}, u32[]{:S(2)}) collective-permute-start(bf16[1024,128]{0,1:T(8,128)(2,1)} %get-tuple-element.46), channel_id=1, source_target_pairs={{0,3},{1,2},{2,1},{3,0},{4,7},{5,6},{6,5},{7,4},{8,11},{9,10},{10,... | collective-permute-start | bytes 786440 | tf_op jit(solution)/shard_map/ppermute | solution.py:201
  44.2 5.1 %collective-permute-start.3 = (bf16[1024,128]{0,1:T(8,128)(2,1)}, bf16[1024,128]{0,1:T(8,128)(2,1)S(1)}, u32[]{:S(2)}, u32[]{:S(2)}) collective-permute-start(bf16[1024,128]{0,1:T(8,128)(2,1)} %get-tuple-element.45), channel_id=1, source_target_pairs={{0,4},{1,5},{2,6},{3,7},{4,0},{5,1},{6,2},{7,3},{8,12},{9,13},{10,... | collective-permute-start | bytes 786440 | tf_op jit(solution)/shard_map/ppermute | solution.py:201
  49.4 2.0 %collective-permute-start.4 = (bf16[1024,128]{0,1:T(8,128)(2,1)}, bf16[1024,128]{0,1:T(8,128)(2,1)S(1)}, u32[]{:S(2)}, u32[]{:S(2)}) collective-permute-start(bf16[1024,128]{0,1:T(8,128)(2,1)} %get-tuple-element.44), channel_id=1, source_target_pairs={{0,5},{1,4},{2,7},{3,6},{4,1},{5,0},{6,3},{7,2},{8,13},{9,12},{10,... | collective-permute-start | bytes 786440 | tf_op jit(solution)/shard_map/ppermute | solution.py:201
  57.5 4.8 %collective-permute-start.5 = (bf16[1024,128]{0,1:T(8,128)(2,1)}, bf16[1024,128]{0,1:T(8,128)(2,1)}, u32[]{:S(2)}, u32[]{:S(2)}) collective-permute-start(bf16[1024,128]{0,1:T(8,128)(2,1)} %get-tuple-element.43), channel_id=1, source_target_pairs={{0,6},{1,7},{2,4},{3,5},{4,2},{5,3},{6,0},{7,1},{8,14},{9,15},{10,... | collective-permute-start | bytes 786440 | tf_op jit(solution)/shard_map/ppermute | solution.py:201
  63.3 5.3 %all-to-all-done = f16[32,13,8,128]{3,2,1,0:T(8,128)(2,1)S(1)} async-done(((f16[32,13,8,128]{3,2,1,0:T(8,128)(2,1)}), f16[32,13,8,128]{3,2,1,0:T(8,128)(2,1)S(1)}, u32[]{:S(2)}, u32[]{:S(2)}) %all-to-all-start) | async-done | bytes 852000 | tf_op jit(solution)/shard_map/all_to_all | solution.py:239
  69.9 7.5 %shard_map.78 = bf16[32,12,8,128]{3,2,1,0:T(8,128)(2,1)} custom-call(f32[3328,128]{1,0:T(8,128)} %bitcast_convert_fusion.message_ref, bf16[256,256]{1,0:T(8,128)(2,1)} %get-tuple-element.73.forward_ref, bf16[256,256]{1,0:T(8,128)(2,1)} %get-tuple-element.74.inverse_ref, bf16[128,2048]{1,0:T(8,128)(2,1)} %select_convert_fusion.spread_ref), custom_call_target="tpu_custom_call" | custom-call | tf_op jit(solution)/shard_map/pallas_call | solution.py:122
  77.4 7.1 %all-to-all-start.1 = ((bf16[32,12,8,128]{3,2,1,0:T(8,128)(2,1)}), bf16[32,12,8,128]{3,2,1,0:T(8,128)(2,1)S(1)}, u32[]{:S(2)}, u32[]{:S(2)}) async-start(bf16[32,12,8,128]{3,2,1,0:T(8,128)(2,1)} %shard_map.78), calls=%async_computation.1 | async-start | bytes 1572864 | tf_op jit(solution)/shard_map/all_to_all | solution.py:242
  84.5 2.6 %collective-permute-start.6 = (bf16[1024,128]{0,1:T(8,128)(2,1)}, bf16[1024,128]{0,1:T(8,128)(2,1)S(1)}, u32[]{:S(2)}, u32[]{:S(2)}) collective-permute-start(bf16[1024,128]{0,1:T(8,128)(2,1)} %get-tuple-element.42), channel_id=1, source_target_pairs={{0,7},{1,6},{2,5},{3,4},{4,3},{5,2},{6,1},{7,0},{8,15},{9,14},{10,... | collective-permute-start | bytes 786440 | tf_op jit(solution)/shard_map/ppermute | solution.py:201
  90.1 6.2 %collective-permute-done.6 = bf16[1024,128]{0,1:T(8,128)(2,1)S(1)} collective-permute-done((bf16[1024,128]{0,1:T(8,128)(2,1)}, bf16[1024,128]{0,1:T(8,128)(2,1)S(1)}, u32[]{:S(2)}, u32[]{:S(2)}) %collective-permute-start.6) | collective-permute-done | bytes 262176 | tf_op jit(solution)/shard_map/ppermute | solution.py:201
  102.1 7.4 %all-to-all-done.1 = bf16[32,12,8,128]{3,2,1,0:T(8,128)(2,1)S(1)} async-done(((bf16[32,12,8,128]{3,2,1,0:T(8,128)(2,1)}), bf16[32,12,8,128]{3,2,1,0:T(8,128)(2,1)S(1)}, u32[]{:S(2)}, u32[]{:S(2)}) %all-to-all-start.1) | async-done | bytes 786464 | tf_op jit(solution)/shard_map/all_to_all | solution.py:242
  110.3 2.3 %convolution_convert_fusion = f16[512,768]{1,0:T(8,128)(2,1)S(1)} fusion(bf16[512,1024]{0,1:T(8,128)(2,1)} %get-tuple-element.26, bf16[1024,768]{1,0:T(8,128)(2,1)S(1)} %bitcast.121), kind=kOutput, calls=%fused_computation.7 | convolution fusion | flops 805699584 | bytes 3407872 | tf_op jit(solution)/shard_map/dot_general | solution.py:248
  112.5 1.9 %collective-permute-start.7 = (f16[512,768]{1,0:T(8,128)(2,1)S(1)}, f16[512,768]{1,0:T(8,128)(2,1)S(1)}, u32[]{:S(2)}, u32[]{:S(2)}) collective-permute-start(f16[512,768]{1,0:T(8,128)(2,1)S(1)} %convolution_convert_fusion), channel_id=1, source_target_pairs={{0,1},{1,0},{2,3},{3,2},{4,5},{5,4},{6,7},{7,6},{8,9},{9,8},{10,11... | collective-permute-start | bytes 2359304 | tf_op jit(solution)/shard_map/ppermute | solution.py:249
  114.5 2.3 %collective-permute-done.7 = f16[512,768]{1,0:T(8,128)(2,1)S(1)} collective-permute-done((f16[512,768]{1,0:T(8,128)(2,1)S(1)}, f16[512,768]{1,0:T(8,128)(2,1)S(1)}, u32[]{:S(2)}, u32[]{:S(2)}) %collective-permute-start.7) | collective-permute-done | bytes 786464 | tf_op jit(solution)/shard_map/ppermute | solution.py:249
  116.7 2.3 %multiply_convert_fusion = f16[512,768]{1,0:T(8,128)(2,1)S(1)} fusion(f16[512,768]{1,0:T(8,128)(2,1)S(1)} %collective-permute-done.7, bf16[512,1024]{0,1:T(8,128)(2,1)} %get-tuple-element.27, bf16[1024,768]{1,0:T(8,128)(2,1)S(1)} %bitcast.122), kind=kOutput, calls=%fused_computation.6 | convolution fusion | flops 806879232 | bytes 4194304 | tf_op jit(solution)/shard_map/dot_general | solution.py:250
  119.1 15.3 %all_to_all.26 = f16[4,128,768]{2,1,0:T(8,128)(2,1)S(1)} all-to-all(f16[4,128,768]{2,1,0:T(8,128)(2,1)S(1)} %bitcast.124), channel_id=1, replica_groups=mesh['freq'=16,'line_0'=4,'line_1'=4,'line_2'=2] {'line_1'}, dimensions={0} | all-to-all | bytes 1572864 | tf_op jit(solution)/shard_map/all_to_all | solution.py:222
  134.5 38.3 %all_to_all.27 = f16[4,32,768]{2,1,0:T(8,128)(2,1)S(1)} all-to-all(f16[4,32,768]{2,1,0:T(8,128)(2,1)S(1)} %bitcast.125), channel_id=1, replica_groups=mesh['freq'=16,'line_0'=4,'line_1'=4,'line_2'=2] {'line_0'}, dimensions={0} | all-to-all | bytes 393216 | tf_op jit(solution)/shard_map/all_to_all | solution.py:222
  174.5 7.5 %all-to-all-start.4 = ((f32[16,1,32]{2,1,0:T(1,128)}), f32[16,1,32]{2,1,0:T(1,128)S(1)}, u32[]{:S(2)}, u32[]{:S(2)}) async-start(f32[16,1,32]{2,1,0:T(1,128)} %broadcast_in_dim.38), calls=%async_computation.4 | async-start | bytes 16384 | tf_op jit(solution)/shard_map/all_to_all | solution.py:229
  182.7 5.8 %all-to-all-done.4 = f32[16,1,32]{2,1,0:T(1,128)S(1)} async-done(((f32[16,1,32]{2,1,0:T(1,128)}), f32[16,1,32]{2,1,0:T(1,128)S(1)}, u32[]{:S(2)}, u32[]{:S(2)}) %all-to-all-start.4) | async-done | bytes 2080 | tf_op jit(solution)/shard_map/all_to_all | solution.py:229
  (81 shorter events, 28.5 us)
Async XLA Ops:
  7.0 61.6 %all-to-all-start = ((f16[32,13,8,128]{3,2,1,0:T(8,128)(2,1)}), f16[32,13,8,128]{3,2,1,0:T(8,128)(2,1)S(1)}, u32[]{:S(2)}, u32[]{:S(2)}) async-start(f16[32,13,8,128]{3,2,1,0:T(8,128)(2,1)} %pad_maximum_fusion.1), calls=%async_computation | async-start | bytes 1703936 | tf_op jit(solution)/shard_map/all_to_all | solution.py:239
  34.0 1.3 copy-start
  34.0 17.4 %copy-start.2 = (s32[64]{0:T(128)S(1)}, s32[64]{0:T(128)}, u32[]{:S(2)}) copy-start(s32[64]{0:T(128)} %param.8) | copy-start | bytes 772
  36.6 20.9 %collective-permute-start = (bf16[1024,128]{0,1:T(8,128)(2,1)}, bf16[1024,128]{0,1:T(8,128)(2,1)}, u32[]{:S(2)}, u32[]{:S(2)}) collective-permute-start(bf16[1024,128]{0,1:T(8,128)(2,1)} %get-tuple-element.48), channel_id=1, source_target_pairs={{0,1},{1,0},{2,3},{3,2},{4,5},{5,4},{6,7},{7,6},{8,9},{9,8},{10,11... | collective-permute-start | bytes 786440 | tf_op jit(solution)/shard_map/ppermute | solution.py:201
  38.8 45.7 %collective-permute-start.1 = (bf16[1024,128]{0,1:T(8,128)(2,1)}, bf16[1024,128]{0,1:T(8,128)(2,1)}, u32[]{:S(2)}, u32[]{:S(2)}) collective-permute-start(bf16[1024,128]{0,1:T(8,128)(2,1)} %get-tuple-element.47), channel_id=1, source_target_pairs={{0,2},{1,3},{2,0},{3,1},{4,6},{5,7},{6,4},{7,5},{8,10},{9,11},{10,... | collective-permute-start | bytes 786440 | tf_op jit(solution)/shard_map/ppermute | solution.py:201
  42.3 45.8 %collective-permute-start.2 = (bf16[1024,128]{0,1:T(8,128)(2,1)}, bf16[1024,128]{0,1:T(8,128)(2,1)}, u32[]{:S(2)}, u32[]{:S(2)}) collective-permute-start(bf16[1024,128]{0,1:T(8,128)(2,1)} %get-tuple-element.46), channel_id=1, source_target_pairs={{0,3},{1,2},{2,1},{3,0},{4,7},{5,6},{6,5},{7,4},{8,11},{9,10},{10,... | collective-permute-start | bytes 786440 | tf_op jit(solution)/shard_map/ppermute | solution.py:201
  44.2 44.8 %collective-permute-start.3 = (bf16[1024,128]{0,1:T(8,128)(2,1)}, bf16[1024,128]{0,1:T(8,128)(2,1)S(1)}, u32[]{:S(2)}, u32[]{:S(2)}) collective-permute-start(bf16[1024,128]{0,1:T(8,128)(2,1)} %get-tuple-element.45), channel_id=1, source_target_pairs={{0,4},{1,5},{2,6},{3,7},{4,0},{5,1},{6,2},{7,3},{8,12},{9,13},{10,... | collective-permute-start | bytes 786440 | tf_op jit(solution)/shard_map/ppermute | solution.py:201
  49.4 39.7 %collective-permute-start.4 = (bf16[1024,128]{0,1:T(8,128)(2,1)}, bf16[1024,128]{0,1:T(8,128)(2,1)S(1)}, u32[]{:S(2)}, u32[]{:S(2)}) collective-permute-start(bf16[1024,128]{0,1:T(8,128)(2,1)} %get-tuple-element.44), channel_id=1, source_target_pairs={{0,5},{1,4},{2,7},{3,6},{4,1},{5,0},{6,3},{7,2},{8,13},{9,12},{10,... | collective-permute-start | bytes 786440 | tf_op jit(solution)/shard_map/ppermute | solution.py:201
  57.5 31.7 %collective-permute-start.5 = (bf16[1024,128]{0,1:T(8,128)(2,1)}, bf16[1024,128]{0,1:T(8,128)(2,1)}, u32[]{:S(2)}, u32[]{:S(2)}) collective-permute-start(bf16[1024,128]{0,1:T(8,128)(2,1)} %get-tuple-element.43), channel_id=1, source_target_pairs={{0,6},{1,7},{2,4},{3,5},{4,2},{5,3},{6,0},{7,1},{8,14},{9,15},{10,... | collective-permute-start | bytes 786440 | tf_op jit(solution)/shard_map/ppermute | solution.py:201
  77.4 32.1 %all-to-all-start.1 = ((bf16[32,12,8,128]{3,2,1,0:T(8,128)(2,1)}), bf16[32,12,8,128]{3,2,1,0:T(8,128)(2,1)S(1)}, u32[]{:S(2)}, u32[]{:S(2)}) async-start(bf16[32,12,8,128]{3,2,1,0:T(8,128)(2,1)} %shard_map.78), calls=%async_computation.1 | async-start | bytes 1572864 | tf_op jit(solution)/shard_map/all_to_all | solution.py:242
  84.5 11.8 %collective-permute-start.6 = (bf16[1024,128]{0,1:T(8,128)(2,1)}, bf16[1024,128]{0,1:T(8,128)(2,1)S(1)}, u32[]{:S(2)}, u32[]{:S(2)}) collective-permute-start(bf16[1024,128]{0,1:T(8,128)(2,1)} %get-tuple-element.42), channel_id=1, source_target_pairs={{0,7},{1,6},{2,5},{3,4},{4,3},{5,2},{6,1},{7,0},{8,15},{9,14},{10,... | collective-permute-start | bytes 786440 | tf_op jit(solution)/shard_map/ppermute | solution.py:201
  112.5 4.2 %collective-permute-start.7 = (f16[512,768]{1,0:T(8,128)(2,1)S(1)}, f16[512,768]{1,0:T(8,128)(2,1)S(1)}, u32[]{:S(2)}, u32[]{:S(2)}) collective-permute-start(f16[512,768]{1,0:T(8,128)(2,1)S(1)} %convolution_convert_fusion), channel_id=1, source_target_pairs={{0,1},{1,0},{2,3},{3,2},{4,5},{5,4},{6,7},{7,6},{8,9},{9,8},{10,11... | collective-permute-start | bytes 2359304 | tf_op jit(solution)/shard_map/ppermute | solution.py:249
  134.5 39.4 %copy-start.1 = (f32[32,1,2,384]{3,2,1,0:T(2,128)S(1)}, f32[32,1,2,384]{3,2,1,0:T(2,128)}, u32[]{:S(2)}) copy-start(f32[32,1,2,384]{3,2,1,0:T(2,128)} %param.11) | copy-start | bytes 294916
  174.5 14.0 %all-to-all-start.4 = ((f32[16,1,32]{2,1,0:T(1,128)}), f32[16,1,32]{2,1,0:T(1,128)S(1)}, u32[]{:S(2)}, u32[]{:S(2)}) async-start(f32[16,1,32]{2,1,0:T(1,128)} %broadcast_in_dim.38), calls=%async_computation.4 | async-start | bytes 16384 | tf_op jit(solution)/shard_map/all_to_all | solution.py:229

commit v4 on v3

--- a/solution.py
+++ b/solution.py
@@ -121,17 +121,21 @@
 def middle(message, forward, inverse, spread):
     return pl.pallas_call(
         middle_kernel,
-        out_shape=jax.ShapeDtypeStruct((32, 12, 8, 128), jnp.bfloat16),
+        out_shape=pltpu.VMEM((32, 12, 8, 128), jnp.bfloat16),
         in_specs=[pl.BlockSpec(memory_space=pltpu.VMEM)] * 4,
         out_specs=pl.BlockSpec(memory_space=pltpu.VMEM),
         scratch_shapes=[
             pltpu.VMEM((3072, 128), jnp.float32),
             pltpu.VMEM((256, 2048), jnp.float32),
         ],
-    )(message.astype(jnp.float32).reshape(3328, 128), forward, inverse, spread)
-
-
-def outgoing_kernel(live_ref, field_ref, operator_ref, tiles_ref, operator_out_ref):
+    )(
+        pltpu.with_memory_space_constraint(message.astype(jnp.float32).reshape(3328, 128), pltpu.VMEM),
+        *[pltpu.with_memory_space_constraint(table, pltpu.VMEM) for table in (forward, inverse, spread)],
+    )
+
+
+def outgoing_kernel(live_ref, field_ref, operator_ref, out_ref):
+    part = pl.program_id(0)
     row = lax.broadcasted_iota(jnp.int32, (128, 128), 0)
     for line in range(2):
         for half in range(2):
@@ -145,7 +149,7 @@
                     0,
                 )
                 block = jnp.where(live, block.T, jnp.float32(0.0))
-                tiles_ref[16 * half : 16 * half + 16, 3 * line + t] = block.reshape(16, 8, 128)
+                out_ref[16 * half : 16 * half + 16, 6 * part + 3 * line + t] = block.reshape(16, 8, 128)
     for half in range(2):
         high = []
         low = []
@@ -156,30 +160,24 @@
             high.append(rounded)
             low.append(rest)
         block = jnp.concatenate(high + low, 0).T
-        operator_out_ref[16 * half : 16 * half + 16, 0] = block.reshape(16, 8, 128)
+        out_ref[16 * half : 16 * half + 16, 12] = block.reshape(16, 8, 128)
 
 
 def outgoing(field, live_count, decomposer):
     rows = field.reshape(2, 4, 96, 2, 2, 128).transpose(0, 1, 2, 4, 3, 5).reshape(3072, 128)
     operator_rows = decomposer.reshape(32, 2, 2, 128).transpose(0, 2, 1, 3).reshape(128, 128)
-    tiles, operators = pl.pallas_call(
+    tiles = pl.pallas_call(
         outgoing_kernel,
         grid=(2,),
-        out_shape=(
-            jax.ShapeDtypeStruct((32, 12, 8, 128), jnp.float32),
-            jax.ShapeDtypeStruct((32, 1, 8, 128), jnp.float32),
-        ),
+        out_shape=pltpu.VMEM((32, 13, 8, 128), jnp.float32),
         in_specs=[
             pl.BlockSpec(memory_space=pltpu.SMEM),
             pl.BlockSpec((1536, 128), lambda part: (part, 0)),
             pl.BlockSpec((128, 128), lambda part: (0, 0)),
         ],
-        out_specs=(
-            pl.BlockSpec((32, 6, 8, 128), lambda part: (0, part, 0, 0)),
-            pl.BlockSpec((32, 1, 8, 128), lambda part: (0, 0, 0, 0)),
-        ),
+        out_specs=pl.BlockSpec(memory_space=pltpu.VMEM),
     )(live_count, rows, operator_rows)
-    return jnp.concatenate([tiles, operators], 1).astype(jnp.float16)
+    return tiles.astype(jnp.float16)
 
 
 def panel_blocks(reflection):
@@ -247,15 +245,18 @@
     ).reshape(1024, 768)
     sent = jnp.dot(other_panel, stacked, preferred_element_type=jnp.float32).astype(jnp.float16)
     sent = lax.ppermute(sent, "line_2", [(0, 1), (1, 0)])
-    product = jnp.dot(own_panel, stacked, preferred_element_type=jnp.float32)
+    product = lax.optimization_barrier(
+        jnp.dot(own_panel, stacked, preferred_element_type=jnp.float32)
+    )
     product = product + sent.astype(jnp.float32)
     product = summed(product, "line_1", 0.5)
     product = summed(product, "line_0", 0.125)
     reflected = product.reshape(32, 2, 3, 4, 32).transpose(0, 1, 3, 2, 4).reshape(32, 1, 2, 384)
+    partial_value = jnp.sum(product * product, axis=1) * weight
+    reflected, partial_value = lax.optimization_barrier((reflected, partial_value))
+    energy_sum = over_copies(partial_value, "freq")
+    reflected, energy_sum = lax.optimization_barrier((reflected, energy_sum))
     focusing = direct_wave - reflected
-    partial_value = jnp.sum(reflected * reflected, axis=(1, 2, 3)) * weight
-    focusing, partial_value = lax.optimization_barrier((focusing, partial_value))
-    energy_sum = over_copies(partial_value, "freq")
     trace_energy = jnp.sqrt(energy_sum / 768 + 1e-06)
     return (focusing, trace_energy)
 

time: 190 us -> 180 us (0.947)
  waiting for transfers between devices: 27 us -> 15.5 us
  blocking collectives: 53.6 us -> 65 us
  starting transfers between devices: 56.8 us -> 49.4 us
  local copies, waits for them, and re-layouts: 21.4 us -> 28.4 us
  other arithmetic: 10.3 us -> 5.77 us
  Pallas kernels: 10.2 us -> 7.63 us
  matrix products: 8.65 us -> 6.12 us
    all_to_all x0 -> x1, blocking collectives: none -> 13.6 us  [over_copies(): return lax.all_to_all(shards, axis, 0, 0, tiled=True).sum(axis=0)]
    all_to_all x1 -> x0, starting transfers between devices: 7.45 us -> none  [over_copies(): return lax.all_to_all(shards, axis, 0, 0, tiled=True).sum(axis=0)]
    unnamed x21 -> x19, local copies, waits for them, and re-layouts: 11.9 us -> 18.5 us
    all_to_all x1 -> x0, waiting for transfers between devices: 5.83 us -> none  [over_copies(): return lax.all_to_all(shards, axis, 0, 0, tiled=True).sum(axis=0)]
    ppermute x7, waiting for transfers between devices: 6.17 us -> 0.73 us  [exchanged(): received.append(lax.ppermute(block, PLANE, pairs))]
    pallas_call x2, Pallas kernels: 10.2 us -> 7.63 us  [the longest x1 5.83 us: middle(): pl.pallas_call(middle_kernel, out_shape=pltpu.VMEM((32, 12, 8, 128), jnp....]
    another operation x2 -> x0, other arithmetic: 2.44 us -> none
    all_to_all x2, blocking collectives: 53.6 us -> 51.4 us  [summed(): blocks = lax.all_to_all(blocks, axis, 0, 0, tiled=True)]
  transfers between devices with their start and end apart: 11 -> 10, of which waited for: 5 -> 4; matrix products, arithmetic and copies ran while one was open for 15% -> 20% of each run, Pallas kernels for 4% -> 3%
where the time goes in v4:
time: 180 us; the launch traced here: 179 us
  blocking collectives  65 us (36%)
  starting transfers between devices  49.4 us (27%)
  local copies, waits for them, and re-layouts  28.4 us (16%)
  waiting for transfers between devices  15.5 us (9%)
  Pallas kernels  7.63 us (4%)
  matrix products  6.12 us (3%)
  other arithmetic  5.77 us (3%)
    all_to_all x2, blocking collectives, summed(): blocks = lax.all_to_all(blocks, axis, 0, 0, tiled=True)  51.4 us
    ppermute x7, starting transfers between devices, exchanged(): received.append(lax.ppermute(block, PLANE, pairs))  22.3 us
    unnamed x19, local copies, waits for them, and re-layouts  18.5 us
    all_to_all x1, starting transfers between devices, on_device(): message = lax.all_to_all(message, RECEIVER, 0, 0, tiled=True)  18.1 us
    all_to_all x1, blocking collectives, over_copies(): return lax.all_to_all(shards, axis, 0, 0, tiled=True).sum(axis=0)  13.6 us
    all_to_all x1, starting transfers between devices, on_device(): wave = lax.all_to_all(wave, 'line_0', 0, 0, tiled=True)  7.07 us
    all_to_all x1, waiting for transfers between devices, on_device(): message = lax.all_to_all(message, RECEIVER, 0, 0, tiled=True)  6.87 us
    all_to_all x1, waiting for transfers between devices, on_device(): wave = lax.all_to_all(wave, 'line_0', 0, 0, tiled=True)  6.69 us
  transfers between devices with their start and end apart: 10, of which 4 were waited for; matrix products, arithmetic and copies ran while one was open for 20% of the time, Pallas kernels for 3%

profile of v4, /device:TPU:2, one launch (start us, length us, event | category | flops | bytes accessed | tf_op | source)
XLA Modules:
  0.0 178.9 jit_solution(7446473556175307077)
XLA Ops:
  0.6 1.8 %shard_map.77 = f32[32,13,8,128]{3,2,1,0:T(8,128)S(1)} custom-call(s32[2]{0:T(128)} %live_ref.1, f32[3072,128]{1,0:T(8,128)} %bitcast.119, f32[128,128]{1,0:T(8,128)} %bitcast.125), custom_call_target="tpu_custom_call" | custom-call | tf_op jit(solution)/shard_map/pallas_call | solution.py:169
  3.5 18.1 %all-to-all-start = ((f16[32,13,8,128]{3,2,1,0:T(8,128)(2,1)}), f16[32,13,8,128]{3,2,1,0:T(8,128)(2,1)S(1)}, u32[]{:S(2)}, u32[]{:S(2)}) async-start(f16[32,13,8,128]{3,2,1,0:T(8,128)(2,1)} %convert_element_type.90), calls=%async_computation | async-start | bytes 1703936 | tf_op jit(solution)/shard_map/all_to_all | solution.py:237
  21.6 3.2 %reshape_squeeze.3 = bf16[4,4,2,32,1024]{4,3,2,1,0:T(8,128)(2,1)S(1)} reshape(bf16[1,1024,2,512]{3,2,1,0:T(2,128)(2,1)} %param.10) | data formatting | bytes 4194304 | tf_op jit(solution)/shard_map/reshape;squeeze | solution.py:184
  26.4 4.1 %fusion.2 = bf16[1024,1024]{0,1:T(8,128)(2,1)S(1)} fusion(bf16[1024,1024]{1,0:T(8,128)(2,1)} %bitcast.118, s32[1024]{0:T(1024)S(1)} %fusion.46), kind=kOutput, calls=%fused_computation.3 | convolution fusion | flops 2149580800 | bytes 4198400 | tf_op jit(solution)/shard_map/dot_general | solution.py:189
  31.8 2.2 %collective-permute-start = (bf16[1024,128]{0,1:T(8,128)(2,1)}, bf16[1024,128]{0,1:T(8,128)(2,1)}, u32[]{:S(2)}, u32[]{:S(2)}) collective-permute-start(bf16[1024,128]{0,1:T(8,128)(2,1)} %get-tuple-element.48), channel_id=1, source_target_pairs={{0,1},{1,0},{2,3},{3,2},{4,5},{5,4},{6,7},{7,6},{8,9},{9,8},{10,11... | collective-permute-start | bytes 786440 | tf_op jit(solution)/shard_map/ppermute | solution.py:199
  34.0 3.5 %collective-permute-start.1 = (bf16[1024,128]{0,1:T(8,128)(2,1)}, bf16[1024,128]{0,1:T(8,128)(2,1)}, u32[]{:S(2)}, u32[]{:S(2)}) collective-permute-start(bf16[1024,128]{0,1:T(8,128)(2,1)} %get-tuple-element.47), channel_id=1, source_target_pairs={{0,2},{1,3},{2,0},{3,1},{4,6},{5,7},{6,4},{7,5},{8,10},{9,11},{10,... | collective-permute-start | bytes 786440 | tf_op jit(solution)/shard_map/ppermute | solution.py:199
  37.5 1.9 %collective-permute-start.2 = (bf16[1024,128]{0,1:T(8,128)(2,1)}, bf16[1024,128]{0,1:T(8,128)(2,1)}, u32[]{:S(2)}, u32[]{:S(2)}) collective-permute-start(bf16[1024,128]{0,1:T(8,128)(2,1)} %get-tuple-element.46), channel_id=1, source_target_pairs={{0,3},{1,2},{2,1},{3,0},{4,7},{5,6},{6,5},{7,4},{8,11},{9,10},{10,... | collective-permute-start | bytes 786440 | tf_op jit(solution)/shard_map/ppermute | solution.py:199
  39.5 5.1 %collective-permute-start.3 = (bf16[1024,128]{0,1:T(8,128)(2,1)}, bf16[1024,128]{0,1:T(8,128)(2,1)}, u32[]{:S(2)}, u32[]{:S(2)}) collective-permute-start(bf16[1024,128]{0,1:T(8,128)(2,1)} %get-tuple-element.45), channel_id=1, source_target_pairs={{0,4},{1,5},{2,6},{3,7},{4,0},{5,1},{6,2},{7,3},{8,12},{9,13},{10,... | collective-permute-start | bytes 786440 | tf_op jit(solution)/shard_map/ppermute | solution.py:199
  44.6 2.0 %collective-permute-start.4 = (bf16[1024,128]{0,1:T(8,128)(2,1)}, bf16[1024,128]{0,1:T(8,128)(2,1)}, u32[]{:S(2)}, u32[]{:S(2)}) collective-permute-start(bf16[1024,128]{0,1:T(8,128)(2,1)} %get-tuple-element.44), channel_id=1, source_target_pairs={{0,5},{1,4},{2,7},{3,6},{4,1},{5,0},{6,3},{7,2},{8,13},{9,12},{10,... | collective-permute-start | bytes 786440 | tf_op jit(solution)/shard_map/ppermute | solution.py:199
  51.7 4.8 %collective-permute-start.5 = (bf16[1024,128]{0,1:T(8,128)(2,1)}, bf16[1024,128]{0,1:T(8,128)(2,1)}, u32[]{:S(2)}, u32[]{:S(2)}) collective-permute-start(bf16[1024,128]{0,1:T(8,128)(2,1)} %get-tuple-element.43), channel_id=1, source_target_pairs={{0,6},{1,7},{2,4},{3,5},{4,2},{5,3},{6,0},{7,1},{8,14},{9,15},{10,... | collective-permute-start | bytes 786440 | tf_op jit(solution)/shard_map/ppermute | solution.py:199
  56.5 1.7 bitcast_dynamic-update-slice_fusion.6
  58.2 6.9 %all-to-all-done = f16[32,13,8,128]{3,2,1,0:T(8,128)(2,1)S(1)} async-done(((f16[32,13,8,128]{3,2,1,0:T(8,128)(2,1)}), f16[32,13,8,128]{3,2,1,0:T(8,128)(2,1)S(1)}, u32[]{:S(2)}, u32[]{:S(2)}) %all-to-all-start) | async-done | bytes 852000 | tf_op jit(solution)/shard_map/all_to_all | solution.py:237
  65.2 5.8 %shard_map.78 = bf16[32,12,8,128]{3,2,1,0:T(8,128)(2,1)} custom-call(f32[3328,128]{1,0:T(8,128)S(1)} %bitcast_convert_fusion.message_ref, bf16[256,256]{1,0:T(8,128)(2,1)S(1)} %get-tuple-element.75.forward_ref, bf16[256,256]{1,0:T(8,128)(2,1)S(1)} %get-tuple-element.76.inverse_ref, bf16[128,2048]{1,0:T(8,128)(2,1)S(1)} %select_convert_fusion.spread_ref), custom_call_target="tpu_custom_call" | custom-call | tf_op jit(solution)/shard_map/pallas_call | solution.py:122
  71.1 7.1 %all-to-all-start.1 = ((bf16[32,12,8,128]{3,2,1,0:T(8,128)(2,1)}), bf16[32,12,8,128]{3,2,1,0:T(8,128)(2,1)S(1)}, u32[]{:S(2)}, u32[]{:S(2)}) async-start(bf16[32,12,8,128]{3,2,1,0:T(8,128)(2,1)} %shard_map.78), calls=%async_computation.1 | async-start | bytes 1572864 | tf_op jit(solution)/shard_map/all_to_all | solution.py:240
  78.1 2.7 %collective-permute-start.6 = (bf16[1024,128]{0,1:T(8,128)(2,1)}, bf16[1024,128]{0,1:T(8,128)(2,1)S(1)}, u32[]{:S(2)}, u32[]{:S(2)}) collective-permute-start(bf16[1024,128]{0,1:T(8,128)(2,1)} %get-tuple-element.42), channel_id=1, source_target_pairs={{0,7},{1,6},{2,5},{3,4},{4,3},{5,2},{6,1},{7,0},{8,15},{9,14},{10,... | collective-permute-start | bytes 786440 | tf_op jit(solution)/shard_map/ppermute | solution.py:199
  80.9 1.7 bitcast_dynamic-update-slice_fusion.5
  82.5 1.7 bitcast_dynamic-update-slice_fusion.4
  84.2 1.7 bitcast_dynamic-update-slice_fusion.3
  87.5 1.7 bitcast_dynamic-update-slice_fusion.1
  98.7 6.7 %all-to-all-done.1 = bf16[32,12,8,128]{3,2,1,0:T(8,128)(2,1)S(1)} async-done(((bf16[32,12,8,128]{3,2,1,0:T(8,128)(2,1)}), bf16[32,12,8,128]{3,2,1,0:T(8,128)(2,1)S(1)}, u32[]{:S(2)}, u32[]{:S(2)}) %all-to-all-start.1) | async-done | bytes 786464 | tf_op jit(solution)/shard_map/all_to_all | solution.py:240
  107.2 1.9 %collective-permute-start.7 = (f16[512,768]{1,0:T(8,128)(2,1)S(1)}, f16[512,768]{1,0:T(8,128)(2,1)S(1)}, u32[]{:S(2)}, u32[]{:S(2)}) collective-permute-start(f16[512,768]{1,0:T(8,128)(2,1)S(1)} %convolution_convert_fusion), channel_id=1, source_target_pairs={{0,1},{1,0},{2,3},{3,2},{4,5},{5,4},{6,7},{7,6},{8,9},{9,8},{10,11... | collective-permute-start | bytes 2359304 | tf_op jit(solution)/shard_map/ppermute | solution.py:247
  111.6 15.3 %all_to_all.26 = f16[4,128,768]{2,1,0:T(8,128)(2,1)S(1)} all-to-all(f16[4,128,768]{2,1,0:T(8,128)(2,1)S(1)} %bitcast.115), channel_id=1, replica_groups=mesh['freq'=16,'line_0'=4,'line_1'=4,'line_2'=2] {'line_1'}, dimensions={0} | all-to-all | bytes 1572864 | tf_op jit(solution)/shard_map/all_to_all | solution.py:220
  127.0 36.1 %all_to_all.27 = f16[4,32,768]{2,1,0:T(8,128)(2,1)S(1)} all-to-all(f16[4,32,768]{2,1,0:T(8,128)(2,1)S(1)} %bitcast.124), channel_id=1, replica_groups=mesh['freq'=16,'line_0'=4,'line_1'=4,'line_2'=2] {'line_0'}, dimensions={0} | all-to-all | bytes 393216 | tf_op jit(solution)/shard_map/all_to_all | solution.py:220
  164.0 13.6 %all_to_all.28 = f32[16,1,32]{2,1,0:T(1,128)S(1)} all-to-all(f32[16,1,32]{2,1,0:T(1,128)S(1)} %broadcast_in_dim.38), channel_id=1, replica_groups=mesh['freq'=16,'line_0'=4,'line_1'=4,'line_2'=2] {'freq'}, dimensions={0} | all-to-all | bytes 4096 | tf_op jit(solution)/shard_map/all_to_all | solution.py:227
  (76 shorter events, 26.5 us)
Async XLA Ops:
  3.5 61.6 %all-to-all-start = ((f16[32,13,8,128]{3,2,1,0:T(8,128)(2,1)}), f16[32,13,8,128]{3,2,1,0:T(8,128)(2,1)S(1)}, u32[]{:S(2)}, u32[]{:S(2)}) async-start(f16[32,13,8,128]{3,2,1,0:T(8,128)(2,1)} %convert_element_type.90), calls=%async_computation | async-start | bytes 1703936 | tf_op jit(solution)/shard_map/all_to_all | solution.py:237
  30.5 16.2 %copy-start.1 = (s32[64]{0:T(128)S(1)}, s32[64]{0:T(128)}, u32[]{:S(2)}) copy-start(s32[64]{0:T(128)} %param.8) | copy-start | bytes 772
  31.8 19.9 %collective-permute-start = (bf16[1024,128]{0,1:T(8,128)(2,1)}, bf16[1024,128]{0,1:T(8,128)(2,1)}, u32[]{:S(2)}, u32[]{:S(2)}) collective-permute-start(bf16[1024,128]{0,1:T(8,128)(2,1)} %get-tuple-element.48), channel_id=1, source_target_pairs={{0,1},{1,0},{2,3},{3,2},{4,5},{5,4},{6,7},{7,6},{8,9},{9,8},{10,11... | collective-permute-start | bytes 786440 | tf_op jit(solution)/shard_map/ppermute | solution.py:199
  34.0 44.2 %collective-permute-start.1 = (bf16[1024,128]{0,1:T(8,128)(2,1)}, bf16[1024,128]{0,1:T(8,128)(2,1)}, u32[]{:S(2)}, u32[]{:S(2)}) collective-permute-start(bf16[1024,128]{0,1:T(8,128)(2,1)} %get-tuple-element.47), channel_id=1, source_target_pairs={{0,2},{1,3},{2,0},{3,1},{4,6},{5,7},{6,4},{7,5},{8,10},{9,11},{10,... | collective-permute-start | bytes 786440 | tf_op jit(solution)/shard_map/ppermute | solution.py:199
  37.5 45.0 %collective-permute-start.2 = (bf16[1024,128]{0,1:T(8,128)(2,1)}, bf16[1024,128]{0,1:T(8,128)(2,1)}, u32[]{:S(2)}, u32[]{:S(2)}) collective-permute-start(bf16[1024,128]{0,1:T(8,128)(2,1)} %get-tuple-element.46), channel_id=1, source_target_pairs={{0,3},{1,2},{2,1},{3,0},{4,7},{5,6},{6,5},{7,4},{8,11},{9,10},{10,... | collective-permute-start | bytes 786440 | tf_op jit(solution)/shard_map/ppermute | solution.py:199
  39.5 44.7 %collective-permute-start.3 = (bf16[1024,128]{0,1:T(8,128)(2,1)}, bf16[1024,128]{0,1:T(8,128)(2,1)}, u32[]{:S(2)}, u32[]{:S(2)}) collective-permute-start(bf16[1024,128]{0,1:T(8,128)(2,1)} %get-tuple-element.45), channel_id=1, source_target_pairs={{0,4},{1,5},{2,6},{3,7},{4,0},{5,1},{6,2},{7,3},{8,12},{9,13},{10,... | collective-permute-start | bytes 786440 | tf_op jit(solution)/shard_map/ppermute | solution.py:199
  44.6 41.3 %collective-permute-start.4 = (bf16[1024,128]{0,1:T(8,128)(2,1)}, bf16[1024,128]{0,1:T(8,128)(2,1)}, u32[]{:S(2)}, u32[]{:S(2)}) collective-permute-start(bf16[1024,128]{0,1:T(8,128)(2,1)} %get-tuple-element.44), channel_id=1, source_target_pairs={{0,5},{1,4},{2,7},{3,6},{4,1},{5,0},{6,3},{7,2},{8,13},{9,12},{10,... | collective-permute-start | bytes 786440 | tf_op jit(solution)/shard_map/ppermute | solution.py:199
  51.7 35.9 %collective-permute-start.5 = (bf16[1024,128]{0,1:T(8,128)(2,1)}, bf16[1024,128]{0,1:T(8,128)(2,1)}, u32[]{:S(2)}, u32[]{:S(2)}) collective-permute-start(bf16[1024,128]{0,1:T(8,128)(2,1)} %get-tuple-element.43), channel_id=1, source_target_pairs={{0,6},{1,7},{2,4},{3,5},{4,2},{5,3},{6,0},{7,1},{8,14},{9,15},{10,... | collective-permute-start | bytes 786440 | tf_op jit(solution)/shard_map/ppermute | solution.py:199
  71.1 34.3 %all-to-all-start.1 = ((bf16[32,12,8,128]{3,2,1,0:T(8,128)(2,1)}), bf16[32,12,8,128]{3,2,1,0:T(8,128)(2,1)S(1)}, u32[]{:S(2)}, u32[]{:S(2)}) async-start(bf16[32,12,8,128]{3,2,1,0:T(8,128)(2,1)} %shard_map.78), calls=%async_computation.1 | async-start | bytes 1572864 | tf_op jit(solution)/shard_map/all_to_all | solution.py:240
  78.1 11.8 %collective-permute-start.6 = (bf16[1024,128]{0,1:T(8,128)(2,1)}, bf16[1024,128]{0,1:T(8,128)(2,1)S(1)}, u32[]{:S(2)}, u32[]{:S(2)}) collective-permute-start(bf16[1024,128]{0,1:T(8,128)(2,1)} %get-tuple-element.42), channel_id=1, source_target_pairs={{0,7},{1,6},{2,5},{3,4},{4,3},{5,2},{6,1},{7,0},{8,15},{9,14},{10,... | collective-permute-start | bytes 786440 | tf_op jit(solution)/shard_map/ppermute | solution.py:199
  107.2 4.2 %collective-permute-start.7 = (f16[512,768]{1,0:T(8,128)(2,1)S(1)}, f16[512,768]{1,0:T(8,128)(2,1)S(1)}, u32[]{:S(2)}, u32[]{:S(2)}) collective-permute-start(f16[512,768]{1,0:T(8,128)(2,1)S(1)} %convolution_convert_fusion), channel_id=1, source_target_pairs={{0,1},{1,0},{2,3},{3,2},{4,5},{5,4},{6,7},{7,6},{8,9},{9,8},{10,11... | collective-permute-start | bytes 2359304 | tf_op jit(solution)/shard_map/ppermute | solution.py:247
  126.9 50.8 %copy-start = (f32[32,1,2,384]{3,2,1,0:T(2,128)S(1)}, f32[32,1,2,384]{3,2,1,0:T(2,128)}, u32[]{:S(2)}) copy-start(f32[32,1,2,384]{3,2,1,0:T(2,128)} %param.11) | copy-start | bytes 294916

commit v5 on v4

--- a/solution.py
+++ b/solution.py
@@ -11,7 +11,6 @@
 LINE = ("line_0", "line_1", "line_2")
 RECEIVER = ("line_1", "line_2", "line_0")
 PLANE = ("line_1", "line_2")
-LOW_SCALE = 256.0
 
 
 def by_receiver_owner(values):
@@ -52,19 +51,26 @@
 def spread_table():
     row = jnp.arange(128, dtype=jnp.int32)[:, None]
     column = jnp.arange(2048, dtype=jnp.int32)[None, :]
-    low, line, part, target, source = row // 64, row // 32 % 2, row // 16 % 2, row // 4 % 4, row % 4
+    line, part, target, source = row // 32 % 2, row // 16 % 2, row // 4 % 4, row % 4
     shift, goal = column // 128 % 4, column // 32 % 4
     found = (line == column // 1024) & (part == column // 512 % 2) & (target == goal)
     found = found & (source == (goal - shift) % 4)
-    return jnp.where(found, jnp.where(low == 1, 1.0 / LOW_SCALE, 1.0), 0.0).astype(jnp.bfloat16)
+    return found.astype(jnp.bfloat16)
 
 
 def middle_kernel(message_ref, forward_ref, inverse_ref, spread_ref, out_ref, wave_ref, spread_out_ref):
     forward = forward_ref[...]
     inverse = inverse_ref[...]
-    operators = jnp.concatenate(
-        [message_ref[pl.ds(96 + r, 32, stride=104), :] for r in range(8)], 0
-    ).astype(jnp.bfloat16)
+    lane = lax.broadcasted_iota(jnp.int32, (32, 128), 1)
+    early = []
+    late = []
+    for r in range(4):
+        block = message_ref[pl.ds(96 + r, 32, stride=100), :]
+        high = block.astype(jnp.bfloat16).astype(jnp.float32)
+        low = block - high
+        early.append(jnp.where(lane < 64, high, pltpu.roll(low, 64, 1)))
+        late.append(jnp.where(lane < 64, pltpu.roll(high, 64, 1), low))
+    operators = jnp.concatenate(early + late, 0).astype(jnp.bfloat16)
     spread_out_ref[...] = jnp.dot(operators, spread_ref[...], preferred_element_type=jnp.float32)
 
     def transform(table, value):
@@ -78,7 +84,7 @@
     for r in range(8):
         tiles = [
             jnp.concatenate(
-                [message_ref[pl.ds((g * 3 + t) * 8 + r, 32, stride=104), :] for g in range(4)], 0
+                [message_ref[pl.ds((g * 3 + t) * 8 + r, 32, stride=100), :] for g in range(4)], 0
             )
             for t in range(3)
         ]
@@ -129,38 +135,49 @@
             pltpu.VMEM((256, 2048), jnp.float32),
         ],
     )(
-        pltpu.with_memory_space_constraint(message.astype(jnp.float32).reshape(3328, 128), pltpu.VMEM),
+        pltpu.with_memory_space_constraint(message.astype(jnp.float32).reshape(3200, 128), pltpu.VMEM),
         *[pltpu.with_memory_space_constraint(table, pltpu.VMEM) for table in (forward, inverse, spread)],
     )
 
 
 def outgoing_kernel(live_ref, field_ref, operator_ref, out_ref):
-    part = pl.program_id(0)
     row = lax.broadcasted_iota(jnp.int32, (128, 128), 0)
-    for line in range(2):
+    lane = lax.broadcasted_iota(jnp.int32, (128, 128), 1)
+
+    def put_field(part):
+        for line in range(2):
+            for half in range(2):
+                live = row + 128 * half < live_ref[line]
+                for t in range(3):
+                    block = jnp.concatenate(
+                        [
+                            field_ref[pl.ds(384 * c + 128 * t + 2 * half + line, 32, stride=4), :]
+                            for c in range(4)
+                        ],
+                        0,
+                    )
+                    block = jnp.where(live, block.T, jnp.float32(0.0))
+                    for device in range(16):
+                        place = 100 * (16 * half + device) + 48 * part + 24 * line + 8 * t
+                        out_ref[place : place + 8, :] = block[8 * device : 8 * device + 8]
+
+    def put_operators():
         for half in range(2):
-            live = row + 128 * half < live_ref[line]
-            for t in range(3):
-                block = jnp.concatenate(
-                    [
-                        field_ref[pl.ds(384 * c + 128 * t + 2 * half + line, 32, stride=4), :]
-                        for c in range(4)
-                    ],
-                    0,
-                )
-                block = jnp.where(live, block.T, jnp.float32(0.0))
-                out_ref[16 * half : 16 * half + 16, 6 * part + 3 * line + t] = block.reshape(16, 8, 128)
-    for half in range(2):
-        high = []
-        low = []
-        for line in range(2):
-            block = operator_ref[pl.ds(2 * half + line, 32, stride=4), :]
-            rounded = block.astype(jnp.bfloat16).astype(jnp.float32)
-            rest = ((block - rounded) * LOW_SCALE).astype(jnp.bfloat16).astype(jnp.float32)
-            high.append(rounded)
-            low.append(rest)
-        block = jnp.concatenate(high + low, 0).T
-        out_ref[16 * half : 16 * half + 16, 12] = block.reshape(16, 8, 128)
+            lines = [operator_ref[pl.ds(2 * half + line, 32, stride=4), :] for line in range(2)]
+            block = jnp.concatenate(lines + lines, 0).T
+            block = jnp.where(lane < 64, block, pltpu.roll(block, 124, 0))
+            for device in range(16):
+                place = 100 * (16 * half + device) + 96
+                out_ref[place : place + 4, :] = block[8 * device : 8 * device + 4]
+
+    @pl.when(pl.program_id(0) == 0)
+    def _():
+        put_field(0)
+        put_operators()
+
+    @pl.when(pl.program_id(0) == 1)
+    def _():
+        put_field(1)
 
 
 def outgoing(field, live_count, decomposer):
@@ -169,7 +186,7 @@
     tiles = pl.pallas_call(
         outgoing_kernel,
         grid=(2,),
-        out_shape=pltpu.VMEM((32, 13, 8, 128), jnp.float32),
+        out_shape=pltpu.VMEM((3200, 128), jnp.float32),
         in_specs=[
             pl.BlockSpec(memory_space=pltpu.SMEM),
             pl.BlockSpec((1536, 128), lambda part: (part, 0)),
@@ -177,7 +194,7 @@
         ],
         out_specs=pl.BlockSpec(memory_space=pltpu.VMEM),
     )(live_count, rows, operator_rows)
-    return tiles.astype(jnp.float16)
+    return tiles.reshape(32, 25, 4, 128).astype(jnp.float16)
 
 
 def panel_blocks(reflection):

time: 180 us -> 178 us (0.989)
  blocking collectives: 65 us -> 69.1 us
  local copies, waits for them, and re-layouts: 28.4 us -> 24.6 us
  waiting for transfers between devices: 15.5 us -> 13.5 us
    all_to_all x2, blocking collectives: 51.4 us -> 55.8 us  [summed(): blocks = lax.all_to_all(blocks, axis, 0, 0, tiled=True)]
    unnamed x19 -> x21, local copies, waits for them, and re-layouts: 18.5 us -> 15.7 us
  transfers between devices with their start and end apart: 10 -> 10, of which waited for: 4 -> 4; matrix products, arithmetic and copies ran while one was open for 20% -> 18% of each run, Pallas kernels for 3% -> 3%
where the time goes in v5:
time: 178 us; the launch traced here: 177 us
  blocking collectives  69.1 us (39%)
  starting transfers between devices  49.4 us (28%)
  local copies, waits for them, and re-layouts  24.6 us (14%)
  waiting for transfers between devices  13.5 us (8%)
  Pallas kernels  7.57 us (4%)
  matrix products  6.12 us (3%)
  other arithmetic  5.72 us (3%)
    all_to_all x2, blocking collectives, summed(): blocks = lax.all_to_all(blocks, axis, 0, 0, tiled=True)  55.8 us
    ppermute x7, starting transfers between devices, exchanged(): received.append(lax.ppermute(block, PLANE, pairs))  21.9 us
    all_to_all x1, starting transfers between devices, on_device(): message = lax.all_to_all(message, RECEIVER, 0, 0, tiled=True)  18.1 us
    unnamed x21, local copies, waits for them, and re-layouts  15.7 us
    all_to_all x1, blocking collectives, over_copies(): return lax.all_to_all(shards, axis, 0, 0, tiled=True).sum(axis=0)  13.3 us
    all_to_all x1, starting transfers between devices, on_device(): wave = lax.all_to_all(wave, 'line_0', 0, 0, tiled=True)  7.54 us
    all_to_all x1, waiting for transfers between devices, on_device(): wave = lax.all_to_all(wave, 'line_0', 0, 0, tiled=True)  6.54 us
    pallas_call x1, Pallas kernels, middle(): pl.pallas_call(middle_kernel, out_shape=pltpu.VMEM((32, 12, 8, 128), jnp....  5.79 us
  transfers between devices with their start and end apart: 10, of which 4 were waited for; matrix products, arithmetic and copies ran while one was open for 18% of the time, Pallas kernels for 3%

profile of v5, /device:TPU:2, one launch (start us, length us, event | category | flops | bytes accessed | tf_op | source)
XLA Modules:
  0.0 177.1 jit_solution(18350339462605489010)
XLA Ops:
  0.6 1.8 %shard_map.77 = f32[3200,128]{1,0:T(8,128)S(1)} custom-call(s32[2]{0:T(128)} %live_ref.1, f32[3072,128]{1,0:T(8,128)} %bitcast.123, f32[128,128]{1,0:T(8,128)} %bitcast.126), custom_call_target="tpu_custom_call" | custom-call | tf_op jit(solution)/shard_map/pallas_call | solution.py:186
  3.4 18.1 %all-to-all-start = ((f16[32,25,4,128]{3,2,1,0:T(4,128)(2,1)}), f16[32,25,4,128]{3,2,1,0:T(4,128)(2,1)S(1)}, u32[]{:S(2)}, u32[]{:S(2)}) async-start(f16[32,25,4,128]{3,2,1,0:T(4,128)(2,1)} %bitcast.6), calls=%async_computation | async-start | bytes 1638400 | tf_op jit(solution)/shard_map/all_to_all | solution.py:254
  21.6 3.2 %reshape_squeeze.3 = bf16[4,4,2,32,1024]{4,3,2,1,0:T(8,128)(2,1)S(1)} reshape(bf16[1,1024,2,512]{3,2,1,0:T(2,128)(2,1)} %param.10) | data formatting | bytes 4194304 | tf_op jit(solution)/shard_map/reshape;squeeze | solution.py:201
  26.4 4.1 %fusion.2 = bf16[1024,1024]{0,1:T(8,128)(2,1)S(1)} fusion(bf16[1024,1024]{1,0:T(8,128)(2,1)} %bitcast.119, s32[1024]{0:T(1024)S(1)} %fusion.46), kind=kOutput, calls=%fused_computation.3 | convolution fusion | flops 2149580800 | bytes 4198400 | tf_op jit(solution)/shard_map/dot_general | solution.py:206
  31.8 2.2 %collective-permute-start = (bf16[1024,128]{0,1:T(8,128)(2,1)}, bf16[1024,128]{0,1:T(8,128)(2,1)}, u32[]{:S(2)}, u32[]{:S(2)}) collective-permute-start(bf16[1024,128]{0,1:T(8,128)(2,1)} %get-tuple-element.48), channel_id=1, source_target_pairs={{0,1},{1,0},{2,3},{3,2},{4,5},{5,4},{6,7},{7,6},{8,9},{9,8},{10,11... | collective-permute-start | bytes 786440 | tf_op jit(solution)/shard_map/ppermute | solution.py:216
  34.0 3.5 %collective-permute-start.1 = (bf16[1024,128]{0,1:T(8,128)(2,1)}, bf16[1024,128]{0,1:T(8,128)(2,1)}, u32[]{:S(2)}, u32[]{:S(2)}) collective-permute-start(bf16[1024,128]{0,1:T(8,128)(2,1)} %get-tuple-element.47), channel_id=1, source_target_pairs={{0,2},{1,3},{2,0},{3,1},{4,6},{5,7},{6,4},{7,5},{8,10},{9,11},{10,... | collective-permute-start | bytes 786440 | tf_op jit(solution)/shard_map/ppermute | solution.py:216
  37.5 1.9 %collective-permute-start.2 = (bf16[1024,128]{0,1:T(8,128)(2,1)}, bf16[1024,128]{0,1:T(8,128)(2,1)}, u32[]{:S(2)}, u32[]{:S(2)}) collective-permute-start(bf16[1024,128]{0,1:T(8,128)(2,1)} %get-tuple-element.46), channel_id=1, source_target_pairs={{0,3},{1,2},{2,1},{3,0},{4,7},{5,6},{6,5},{7,4},{8,11},{9,10},{10,... | collective-permute-start | bytes 786440 | tf_op jit(solution)/shard_map/ppermute | solution.py:216
  39.5 5.1 %collective-permute-start.3 = (bf16[1024,128]{0,1:T(8,128)(2,1)}, bf16[1024,128]{0,1:T(8,128)(2,1)}, u32[]{:S(2)}, u32[]{:S(2)}) collective-permute-start(bf16[1024,128]{0,1:T(8,128)(2,1)} %get-tuple-element.45), channel_id=1, source_target_pairs={{0,4},{1,5},{2,6},{3,7},{4,0},{5,1},{6,2},{7,3},{8,12},{9,13},{10,... | collective-permute-start | bytes 786440 | tf_op jit(solution)/shard_map/ppermute | solution.py:216
  44.6 2.0 %collective-permute-start.4 = (bf16[1024,128]{0,1:T(8,128)(2,1)}, bf16[1024,128]{0,1:T(8,128)(2,1)}, u32[]{:S(2)}, u32[]{:S(2)}) collective-permute-start(bf16[1024,128]{0,1:T(8,128)(2,1)} %get-tuple-element.44), channel_id=1, source_target_pairs={{0,5},{1,4},{2,7},{3,6},{4,1},{5,0},{6,3},{7,2},{8,13},{9,12},{10,... | collective-permute-start | bytes 786440 | tf_op jit(solution)/shard_map/ppermute | solution.py:216
  51.7 4.8 %collective-permute-start.5 = (bf16[1024,128]{0,1:T(8,128)(2,1)}, bf16[1024,128]{0,1:T(8,128)(2,1)}, u32[]{:S(2)}, u32[]{:S(2)}) collective-permute-start(bf16[1024,128]{0,1:T(8,128)(2,1)} %get-tuple-element.43), channel_id=1, source_target_pairs={{0,6},{1,7},{2,4},{3,5},{4,2},{5,3},{6,0},{7,1},{8,14},{9,15},{10,... | collective-permute-start | bytes 786440 | tf_op jit(solution)/shard_map/ppermute | solution.py:216
  56.5 1.7 bitcast_dynamic-update-slice_fusion.6
  58.2 5.2 %all-to-all-done = f16[32,25,4,128]{3,2,1,0:T(4,128)(2,1)S(1)} async-done(((f16[32,25,4,128]{3,2,1,0:T(4,128)(2,1)}), f16[32,25,4,128]{3,2,1,0:T(4,128)(2,1)S(1)}, u32[]{:S(2)}, u32[]{:S(2)}) %all-to-all-start) | async-done | bytes 819232 | tf_op jit(solution)/shard_map/all_to_all | solution.py:254
  63.5 5.8 %shard_map.78 = bf16[32,12,8,128]{3,2,1,0:T(8,128)(2,1)} custom-call(f32[3200,128]{1,0:T(8,128)S(1)} %convert.1.message_ref, bf16[256,256]{1,0:T(8,128)(2,1)S(1)} %get-tuple-element.75.forward_ref, bf16[256,256]{1,0:T(8,128)(2,1)S(1)} %get-tuple-element.76.inverse_ref, bf16[128,2048]{1,0:T(8,128)(2,1)S(1)} %and_convert_fusion.spread_ref), custom_call_target="tpu_custom_call" | custom-call | tf_op jit(solution)/shard_map/pallas_call | solution.py:128
  69.3 7.5 %all-to-all-start.1 = ((bf16[32,12,8,128]{3,2,1,0:T(8,128)(2,1)}), bf16[32,12,8,128]{3,2,1,0:T(8,128)(2,1)S(1)}, u32[]{:S(2)}, u32[]{:S(2)}) async-start(bf16[32,12,8,128]{3,2,1,0:T(8,128)(2,1)} %shard_map.78), calls=%async_computation.1 | async-start | bytes 1572864 | tf_op jit(solution)/shard_map/all_to_all | solution.py:257
  76.9 2.2 %collective-permute-start.6 = (bf16[1024,128]{0,1:T(8,128)(2,1)}, bf16[1024,128]{0,1:T(8,128)(2,1)S(1)}, u32[]{:S(2)}, u32[]{:S(2)}) collective-permute-start(bf16[1024,128]{0,1:T(8,128)(2,1)} %get-tuple-element.42), channel_id=1, source_target_pairs={{0,7},{1,6},{2,5},{3,4},{4,3},{5,2},{6,1},{7,0},{8,15},{9,14},{10,... | collective-permute-start | bytes 786440 | tf_op jit(solution)/shard_map/ppermute | solution.py:216
  79.1 1.7 bitcast_dynamic-update-slice_fusion.5
  80.8 1.7 bitcast_dynamic-update-slice_fusion.4
  82.4 1.7 bitcast_dynamic-update-slice_fusion.3
  85.8 1.7 bitcast_dynamic-update-slice_fusion.1
  92.9 6.5 %all-to-all-done.1 = bf16[32,12,8,128]{3,2,1,0:T(8,128)(2,1)S(1)} async-done(((bf16[32,12,8,128]{3,2,1,0:T(8,128)(2,1)}), bf16[32,12,8,128]{3,2,1,0:T(8,128)(2,1)S(1)}, u32[]{:S(2)}, u32[]{:S(2)}) %all-to-all-start.1) | async-done | bytes 786464 | tf_op jit(solution)/shard_map/all_to_all | solution.py:257
  101.3 1.9 %collective-permute-start.7 = (f16[512,768]{1,0:T(8,128)(2,1)S(1)}, f16[512,768]{1,0:T(8,128)(2,1)S(1)}, u32[]{:S(2)}, u32[]{:S(2)}) collective-permute-start(f16[512,768]{1,0:T(8,128)(2,1)S(1)} %convolution_convert_fusion), channel_id=1, source_target_pairs={{0,1},{1,0},{2,3},{3,2},{4,5},{5,4},{6,7},{7,6},{8,9},{9,8},{10,11... | collective-permute-start | bytes 2359304 | tf_op jit(solution)/shard_map/ppermute | solution.py:264
  105.7 15.3 %all_to_all.26 = f16[4,128,768]{2,1,0:T(8,128)(2,1)S(1)} all-to-all(f16[4,128,768]{2,1,0:T(8,128)(2,1)S(1)} %bitcast.116), channel_id=1, replica_groups=mesh['freq'=16,'line_0'=4,'line_1'=4,'line_2'=2] {'line_1'}, dimensions={0} | all-to-all | bytes 1572864 | tf_op jit(solution)/shard_map/all_to_all | solution.py:237
  121.1 40.6 %all_to_all.27 = f16[4,32,768]{2,1,0:T(8,128)(2,1)S(1)} all-to-all(f16[4,32,768]{2,1,0:T(8,128)(2,1)S(1)} %bitcast.125), channel_id=1, replica_groups=mesh['freq'=16,'line_0'=4,'line_1'=4,'line_2'=2] {'line_0'}, dimensions={0} | all-to-all | bytes 393216 | tf_op jit(solution)/shard_map/all_to_all | solution.py:237
  162.5 13.3 %all_to_all.28 = f32[16,1,32]{2,1,0:T(1,128)S(1)} all-to-all(f32[16,1,32]{2,1,0:T(1,128)S(1)} %broadcast_in_dim.5), channel_id=1, replica_groups=mesh['freq'=16,'line_0'=4,'line_1'=4,'line_2'=2] {'freq'}, dimensions={0} | all-to-all | bytes 4096 | tf_op jit(solution)/shard_map/all_to_all | solution.py:244
  (77 shorter events, 22.5 us)
Async XLA Ops:
  3.4 60.0 %all-to-all-start = ((f16[32,25,4,128]{3,2,1,0:T(4,128)(2,1)}), f16[32,25,4,128]{3,2,1,0:T(4,128)(2,1)S(1)}, u32[]{:S(2)}, u32[]{:S(2)}) async-start(f16[32,25,4,128]{3,2,1,0:T(4,128)(2,1)} %bitcast.6), calls=%async_computation | async-start | bytes 1638400 | tf_op jit(solution)/shard_map/all_to_all | solution.py:254
  30.5 16.2 %copy-start.2 = (s32[64]{0:T(128)S(1)}, s32[64]{0:T(128)}, u32[]{:S(2)}) copy-start(s32[64]{0:T(128)} %param.8) | copy-start | bytes 772
  31.8 19.9 %collective-permute-start = (bf16[1024,128]{0,1:T(8,128)(2,1)}, bf16[1024,128]{0,1:T(8,128)(2,1)}, u32[]{:S(2)}, u32[]{:S(2)}) collective-permute-start(bf16[1024,128]{0,1:T(8,128)(2,1)} %get-tuple-element.48), channel_id=1, source_target_pairs={{0,1},{1,0},{2,3},{3,2},{4,5},{5,4},{6,7},{7,6},{8,9},{9,8},{10,11... | collective-permute-start | bytes 786440 | tf_op jit(solution)/shard_map/ppermute | solution.py:216
  34.0 42.9 %collective-permute-start.1 = (bf16[1024,128]{0,1:T(8,128)(2,1)}, bf16[1024,128]{0,1:T(8,128)(2,1)}, u32[]{:S(2)}, u32[]{:S(2)}) collective-permute-start(bf16[1024,128]{0,1:T(8,128)(2,1)} %get-tuple-element.47), channel_id=1, source_target_pairs={{0,2},{1,3},{2,0},{3,1},{4,6},{5,7},{6,4},{7,5},{8,10},{9,11},{10,... | collective-permute-start | bytes 786440 | tf_op jit(solution)/shard_map/ppermute | solution.py:216
  37.5 43.2 %collective-permute-start.2 = (bf16[1024,128]{0,1:T(8,128)(2,1)}, bf16[1024,128]{0,1:T(8,128)(2,1)}, u32[]{:S(2)}, u32[]{:S(2)}) collective-permute-start(bf16[1024,128]{0,1:T(8,128)(2,1)} %get-tuple-element.46), channel_id=1, source_target_pairs={{0,3},{1,2},{2,1},{3,0},{4,7},{5,6},{6,5},{7,4},{8,11},{9,10},{10,... | collective-permute-start | bytes 786440 | tf_op jit(solution)/shard_map/ppermute | solution.py:216
  39.5 43.0 %collective-permute-start.3 = (bf16[1024,128]{0,1:T(8,128)(2,1)}, bf16[1024,128]{0,1:T(8,128)(2,1)}, u32[]{:S(2)}, u32[]{:S(2)}) collective-permute-start(bf16[1024,128]{0,1:T(8,128)(2,1)} %get-tuple-element.45), channel_id=1, source_target_pairs={{0,4},{1,5},{2,6},{3,7},{4,0},{5,1},{6,2},{7,3},{8,12},{9,13},{10,... | collective-permute-start | bytes 786440 | tf_op jit(solution)/shard_map/ppermute | solution.py:216
  44.6 39.5 %collective-permute-start.4 = (bf16[1024,128]{0,1:T(8,128)(2,1)}, bf16[1024,128]{0,1:T(8,128)(2,1)}, u32[]{:S(2)}, u32[]{:S(2)}) collective-permute-start(bf16[1024,128]{0,1:T(8,128)(2,1)} %get-tuple-element.44), channel_id=1, source_target_pairs={{0,5},{1,4},{2,7},{3,6},{4,1},{5,0},{6,3},{7,2},{8,13},{9,12},{10,... | collective-permute-start | bytes 786440 | tf_op jit(solution)/shard_map/ppermute | solution.py:216
  51.7 34.1 %collective-permute-start.5 = (bf16[1024,128]{0,1:T(8,128)(2,1)}, bf16[1024,128]{0,1:T(8,128)(2,1)}, u32[]{:S(2)}, u32[]{:S(2)}) collective-permute-start(bf16[1024,128]{0,1:T(8,128)(2,1)} %get-tuple-element.43), channel_id=1, source_target_pairs={{0,6},{1,7},{2,4},{3,5},{4,2},{5,3},{6,0},{7,1},{8,14},{9,15},{10,... | collective-permute-start | bytes 786440 | tf_op jit(solution)/shard_map/ppermute | solution.py:216
  69.3 30.1 %all-to-all-start.1 = ((bf16[32,12,8,128]{3,2,1,0:T(8,128)(2,1)}), bf16[32,12,8,128]{3,2,1,0:T(8,128)(2,1)S(1)}, u32[]{:S(2)}, u32[]{:S(2)}) async-start(bf16[32,12,8,128]{3,2,1,0:T(8,128)(2,1)} %shard_map.78), calls=%async_computation.1 | async-start | bytes 1572864 | tf_op jit(solution)/shard_map/all_to_all | solution.py:257
  76.9 11.0 %collective-permute-start.6 = (bf16[1024,128]{0,1:T(8,128)(2,1)}, bf16[1024,128]{0,1:T(8,128)(2,1)S(1)}, u32[]{:S(2)}, u32[]{:S(2)}) collective-permute-start(bf16[1024,128]{0,1:T(8,128)(2,1)} %get-tuple-element.42), channel_id=1, source_target_pairs={{0,7},{1,6},{2,5},{3,4},{4,3},{5,2},{6,1},{7,0},{8,15},{9,14},{10,... | collective-permute-start | bytes 786440 | tf_op jit(solution)/shard_map/ppermute | solution.py:216
  88.6 4.1 %copy-start = (bf16[8,1024,128]{1,2,0:T(8,128)(2,1)S(1)}, bf16[8,1024,128]{1,2,0:T(8,128)(2,1)}, u32[]{:S(2)}) copy-start(bf16[8,1024,128]{1,2,0:T(8,128)(2,1)} %bitcast_dynamic-update-slice_fusion) | copy-start | bytes 6291460
  101.3 4.2 %collective-permute-start.7 = (f16[512,768]{1,0:T(8,128)(2,1)S(1)}, f16[512,768]{1,0:T(8,128)(2,1)S(1)}, u32[]{:S(2)}, u32[]{:S(2)}) collective-permute-start(f16[512,768]{1,0:T(8,128)(2,1)S(1)} %convolution_convert_fusion), channel_id=1, source_target_pairs={{0,1},{1,0},{2,3},{3,2},{4,5},{5,4},{6,7},{7,6},{8,9},{9,8},{10,11... | collective-permute-start | bytes 2359304 | tf_op jit(solution)/shard_map/ppermute | solution.py:264
  121.0 54.9 %copy-start.1 = (f32[32,1,2,384]{3,2,1,0:T(2,128)S(1)}, f32[32,1,2,384]{3,2,1,0:T(2,128)}, u32[]{:S(2)}) copy-start(f32[32,1,2,384]{3,2,1,0:T(2,128)} %param.11) | copy-start | bytes 294916

commit v6 on v5

--- a/solution.py
+++ b/solution.py
@@ -58,7 +58,7 @@
     return found.astype(jnp.bfloat16)
 
 
-def middle_kernel(message_ref, forward_ref, inverse_ref, spread_ref, out_ref, wave_ref, spread_out_ref):
+def middle_kernel(message_ref, forward_ref, inverse_ref, spread_ref, out_ref, wave_ref, spread_out_ref, spectrum_ref, decomposed_ref):
     forward = forward_ref[...]
     inverse = inverse_ref[...]
     lane = lax.broadcasted_iota(jnp.int32, (32, 128), 1)
@@ -73,54 +73,65 @@
     operators = jnp.concatenate(early + late, 0).astype(jnp.bfloat16)
     spread_out_ref[...] = jnp.dot(operators, spread_ref[...], preferred_element_type=jnp.float32)
 
-    def transform(table, value):
-        high = value.astype(jnp.bfloat16)
-        low = (value - high.astype(jnp.float32)).astype(jnp.bfloat16)
-        both = jnp.dot(
-            table, jnp.concatenate([high, low], 0), preferred_element_type=jnp.float32
-        )
-        return both[:128] + both[128:]
-
-    for r in range(8):
+    def load(r):
         tiles = [
             jnp.concatenate(
                 [message_ref[pl.ds((g * 3 + t) * 8 + r, 32, stride=100), :] for g in range(4)], 0
             )
             for t in range(3)
         ]
-        spectrum = transform(forward, jnp.concatenate(tiles, 1))
-        decomposed = []
+        value = jnp.concatenate(tiles, 1)
+        high = value.astype(jnp.bfloat16)
+        low = (value - high.astype(jnp.float32)).astype(jnp.bfloat16)
+        both = jnp.dot(
+            forward, jnp.concatenate([high, low], 0), preferred_element_type=jnp.float32
+        )
+        spectrum_ref[r % 2] = both[:128] + both[128:]
+
+    def decompose(r):
         for t in range(3):
-            field_real = spectrum[:64, 128 * t : 128 * t + 128]
-            field_imag = spectrum[64:, 128 * t : 128 * t + 128]
-            real_sum = None
-            imag_sum = None
-            for shift in range(4):
-                weight_real, weight_imag = [
-                    jnp.concatenate(
-                        [
-                            spread_out_ref[
-                                32 * r : 32 * r + 32, pl.ds(1024 * line + 512 * part + 128 * shift, 128)
-                            ]
-                            for line in range(2)
-                        ],
-                        0,
-                    )
-                    for part in range(2)
-                ]
-                moved_real = pltpu.roll(field_real, 32 * shift, 1) if shift else field_real
-                moved_imag = pltpu.roll(field_imag, 32 * shift, 1) if shift else field_imag
-                term_real = weight_real * moved_real - weight_imag * moved_imag
-                term_imag = weight_real * moved_imag + weight_imag * moved_real
-                real_sum = term_real if real_sum is None else real_sum + term_real
-                imag_sum = term_imag if imag_sum is None else imag_sum + term_imag
-            decomposed.append(jnp.concatenate([real_sum, imag_sum], 0))
-        wave = transform(inverse, jnp.concatenate(decomposed, 1))
+            at = pl.ds(128 * t, 128)
+            for line in range(2):
+                rows = pl.ds(32 * line, 32)
+                imag_rows = pl.ds(64 + 32 * line, 32)
+                field_real = spectrum_ref[r % 2, rows, at]
+                field_imag = spectrum_ref[r % 2, imag_rows, at]
+                real_sum = None
+                imag_sum = None
+                for shift in range(4):
+                    weight_real, weight_imag = [
+                        spread_out_ref[
+                            32 * r : 32 * r + 32, pl.ds(1024 * line + 512 * part + 128 * shift, 128)
+                        ]
+                        for part in range(2)
+                    ]
+                    moved_real = pltpu.roll(field_real, 32 * shift, 1) if shift else field_real
+                    moved_imag = pltpu.roll(field_imag, 32 * shift, 1) if shift else field_imag
+                    term_real = weight_real * moved_real - weight_imag * moved_imag
+                    term_imag = weight_real * moved_imag + weight_imag * moved_real
+                    real_sum = term_real if real_sum is None else real_sum + term_real
+                    imag_sum = term_imag if imag_sum is None else imag_sum + term_imag
+                for value, first in ((real_sum, 0), (imag_sum, 64)):
+                    high = value.astype(jnp.bfloat16)
+                    low = (value - high.astype(jnp.float32)).astype(jnp.bfloat16)
+                    decomposed_ref[r % 2, pl.ds(first + 32 * line, 32), at] = high
+                    decomposed_ref[r % 2, pl.ds(128 + first + 32 * line, 32), at] = low
+
+    def store(r):
+        both = jnp.dot(inverse, decomposed_ref[r % 2], preferred_element_type=jnp.float32)
+        wave = both[:128] + both[128:]
         for g in range(4):
             for t in range(3):
                 wave_ref[pl.ds((g * 3 + t) * 8 + r, 32, stride=96), :] = wave[
                     32 * g : 32 * g + 32, 128 * t : 128 * t + 128
                 ]
+
+    load(0)
+    for r in range(8):
+        if r < 7:
+            load(r + 1)
+        decompose(r)
+        store(r)
     out_ref[...] = wave_ref[...].reshape(32, 12, 8, 128).astype(jnp.bfloat16)
 
 
@@ -133,6 +144,8 @@
         scratch_shapes=[
             pltpu.VMEM((3072, 128), jnp.float32),
             pltpu.VMEM((256, 2048), jnp.float32),
+            pltpu.VMEM((2, 128, 384), jnp.float32),
+            pltpu.VMEM((2, 256, 384), jnp.bfloat16),
         ],
     )(
         pltpu.with_memory_space_constraint(message.astype(jnp.float32).reshape(3200, 128), pltpu.VMEM),
@@ -238,17 +251,52 @@
     return blocks.astype(jnp.float32).sum(axis=0) * (1.0 / scale)
 
 
-def over_copies(shard, axis):
-    count = lax.axis_size(axis)
-    shards = jnp.broadcast_to(shard[None], (count, *shard.shape))
-    return lax.all_to_all(shards, axis, 0, 0, tiled=True).sum(axis=0)
+def closing_kernel(blocks_ref, direct_ref, weight_ref, focusing_ref, energies_ref):
+    lane = lax.broadcasted_iota(jnp.int32, (32, 128), 1)
+    energy = jnp.zeros((32, 128), jnp.float32)
+    for part in range(2):
+        tiles = []
+        for t in range(3):
+            at = pl.ds(384 * part + 128 * t, 128)
+            tile = blocks_ref[0, :, at] + blocks_ref[1, :, at]
+            tile = (tile + blocks_ref[2, :, at] + blocks_ref[3, :, at]) * jnp.float32(8.0)
+            energy = energy + tile * tile
+            tiles.append(tile)
+        for t in range(3):
+            natural = None
+            for place in range(4):
+                chunk = 4 * t + place
+                source = tiles[chunk % 3]
+                shift = 32 * (place - chunk // 3) % 128
+                moved = pltpu.roll(source, shift, 1) if shift else source
+                natural = moved if natural is None else jnp.where(lane < 32 * place, natural, moved)
+            at = pl.ds(128 * t, 128)
+            focusing_ref[:, 0, part, at] = direct_ref[:, 0, part, at] - natural
+    total = jnp.sum(energy, axis=1, keepdims=True) * weight_ref[...]
+    energies_ref[...] = total.T[:16].reshape(16, 1, 32)
+
+
+def closing(blocks, direct_wave, weight):
+    return pl.pallas_call(
+        closing_kernel,
+        out_shape=(
+            jax.ShapeDtypeStruct((32, 1, 2, 384), jnp.float32),
+            pltpu.VMEM((16, 1, 32), jnp.float32),
+        ),
+        in_specs=[pl.BlockSpec(memory_space=pltpu.VMEM)] * 3,
+        out_specs=(pl.BlockSpec(memory_space=pltpu.VMEM), pl.BlockSpec(memory_space=pltpu.VMEM)),
+    )(
+        pltpu.with_memory_space_constraint(blocks.astype(jnp.float32), pltpu.VMEM),
+        pltpu.with_memory_space_constraint(direct_wave, pltpu.VMEM),
+        pltpu.with_memory_space_constraint(weight, pltpu.VMEM),
+    )
 
 
 def on_device(field, live_count, line_owner, decomposer, reflection, direct_wave):
     forward, inverse = transform_tables(line_owner)
     total_freqs = lax.axis_size("freq")
     weight = 2.0 * (lax.axis_index("freq") + 1).astype(jnp.float32) / (total_freqs * (total_freqs + 1))
-    weight = jnp.full((32,), weight)
+    weight = jnp.full((1, 128), weight)
     message = outgoing(field, live_count, decomposer)
     message, reflection, weight = lax.optimization_barrier((message, reflection, weight))
     message = lax.all_to_all(message, RECEIVER, 0, 0, tiled=True)
@@ -267,13 +315,11 @@
     )
     product = product + sent.astype(jnp.float32)
     product = summed(product, "line_1", 0.5)
-    product = summed(product, "line_0", 0.125)
-    reflected = product.reshape(32, 2, 3, 4, 32).transpose(0, 1, 3, 2, 4).reshape(32, 1, 2, 384)
-    partial_value = jnp.sum(product * product, axis=1) * weight
-    reflected, partial_value = lax.optimization_barrier((reflected, partial_value))
-    energy_sum = over_copies(partial_value, "freq")
-    reflected, energy_sum = lax.optimization_barrier((reflected, energy_sum))
-    focusing = direct_wave - reflected
+    blocks = (product * 0.125).astype(jnp.float16).reshape(4, 32, 768)
+    blocks = lax.all_to_all(blocks, "line_0", 0, 0, tiled=True)
+    focusing, energies = closing(blocks, direct_wave, weight)
+    energies = lax.all_to_all(energies, "freq", 0, 0, tiled=True)
+    energy_sum = energies.reshape(16, 32).sum(axis=0)
     trace_energy = jnp.sqrt(energy_sum / 768 + 1e-06)
     return (focusing, trace_energy)
 

time: 178 us -> 178 us (level)
  waiting for transfers between devices: 13.5 us -> 16.5 us
  local copies, waits for them, and re-layouts: 24.6 us -> 22.3 us
    all_to_all x1 -> x2, blocking collectives: 13.3 us -> 54 us  [the longest x1 40.7 us: on_device(): blocks = lax.all_to_all(blocks, 'line_0', 0, 0, tiled=True)]
    all_to_all x2 -> x1, blocking collectives: 55.8 us -> 15.4 us  [summed(): blocks = lax.all_to_all(blocks, axis, 0, 0, tiled=True)]
    all_to_all x1, waiting for transfers between devices: 5.24 us -> 8.42 us  [on_device(): message = lax.all_to_all(message, RECEIVER, 0, 0, tiled=True)]
    unnamed x21 -> x20, local copies, waits for them, and re-layouts: 15.7 us -> 14.1 us
  transfers between devices with their start and end apart: 10 -> 10, of which waited for: 4 -> 4; matrix products, arithmetic and copies ran while one was open for 18% -> 17% of each run, Pallas kernels for 3% -> 3%
where the time goes in v6:
time: 178 us; the launch traced here: 177 us
  blocking collectives  69.4 us (39%)
  starting transfers between devices  49.5 us (28%)
  local copies, waits for them, and re-layouts  22.3 us (13%)
  waiting for transfers between devices  16.5 us (9%)
  Pallas kernels  7.27 us (4%)
  matrix products  6.12 us (3%)
  other arithmetic  4.68 us (3%)
    all_to_all x1, blocking collectives, on_device(): blocks = lax.all_to_all(blocks, 'line_0', 0, 0, tiled=True)  40.7 us
    ppermute x7, starting transfers between devices, exchanged(): received.append(lax.ppermute(block, PLANE, pairs))  21.8 us
    all_to_all x1, starting transfers between devices, on_device(): message = lax.all_to_all(message, RECEIVER, 0, 0, tiled=True)  18.2 us
    all_to_all x1, blocking collectives, summed(): blocks = lax.all_to_all(blocks, axis, 0, 0, tiled=True)  15.4 us
    unnamed x20, local copies, waits for them, and re-layouts  14.1 us
    all_to_all x1, blocking collectives, on_device(): energies = lax.all_to_all(energies, 'freq', 0, 0, tiled=True)  13.3 us
    all_to_all x1, waiting for transfers between devices, on_device(): message = lax.all_to_all(message, RECEIVER, 0, 0, tiled=True)  8.42 us
    all_to_all x1, starting transfers between devices, on_device(): wave = lax.all_to_all(wave, 'line_0', 0, 0, tiled=True)  7.5 us
  transfers between devices with their start and end apart: 10, of which 4 were waited for; matrix products, arithmetic and copies ran while one was open for 17% of the time, Pallas kernels for 3%

profile of v6, /device:TPU:2, one launch (start us, length us, event | category | flops | bytes accessed | tf_op | source)
XLA Modules:
  0.0 176.8 jit_solution(16445682687486494310)
XLA Ops:
  0.6 1.8 %shard_map.77 = f32[3200,128]{1,0:T(8,128)S(1)} custom-call(s32[2]{0:T(128)} %live_ref.1, f32[3072,128]{1,0:T(8,128)} %bitcast.117, f32[128,128]{1,0:T(8,128)} %bitcast.120), custom_call_target="tpu_custom_call" | custom-call | tf_op jit(solution)/shard_map/pallas_call | solution.py:199
  3.5 18.2 %all-to-all-start = ((f16[32,25,4,128]{3,2,1,0:T(4,128)(2,1)}), f16[32,25,4,128]{3,2,1,0:T(4,128)(2,1)}, u32[]{:S(2)}, u32[]{:S(2)}) async-start(f16[32,25,4,128]{3,2,1,0:T(4,128)(2,1)} %bitcast.6), calls=%async_computation | async-start | bytes 1638400 | tf_op jit(solution)/shard_map/all_to_all | solution.py:302
  21.7 3.2 %reshape_squeeze.3 = bf16[4,4,2,32,1024]{4,3,2,1,0:T(8,128)(2,1)S(1)} reshape(bf16[1,1024,2,512]{3,2,1,0:T(2,128)(2,1)} %param.10) | data formatting | bytes 4194304 | tf_op jit(solution)/shard_map/reshape;squeeze | solution.py:214
  26.5 4.1 %fusion.2 = bf16[1024,1024]{0,1:T(8,128)(2,1)S(1)} fusion(bf16[1024,1024]{1,0:T(8,128)(2,1)} %bitcast.114, s32[1024]{0:T(1024)S(1)} %fusion.46), kind=kOutput, calls=%fused_computation.3 | convolution fusion | flops 2149580800 | bytes 4198400 | tf_op jit(solution)/shard_map/dot_general | solution.py:219
  31.8 2.1 %collective-permute-start = (bf16[1024,128]{0,1:T(8,128)(2,1)S(1)}, bf16[1024,128]{0,1:T(8,128)(2,1)S(1)}, u32[]{:S(2)}, u32[]{:S(2)}) collective-permute-start(bf16[1024,128]{0,1:T(8,128)(2,1)S(1)} %get-tuple-element.34), channel_id=1, source_target_pairs={{0,1},{1,0},{2,3},{3,2},{4,5},{5,4},{6,7},{7,6},{8,9},{9,8},{10,11... | collective-permute-start | bytes 786440 | tf_op jit(solution)/shard_map/ppermute | solution.py:229
  33.9 3.5 %collective-permute-start.1 = (bf16[1024,128]{0,1:T(8,128)(2,1)}, bf16[1024,128]{0,1:T(8,128)(2,1)}, u32[]{:S(2)}, u32[]{:S(2)}) collective-permute-start(bf16[1024,128]{0,1:T(8,128)(2,1)} %get-tuple-element.33), channel_id=1, source_target_pairs={{0,2},{1,3},{2,0},{3,1},{4,6},{5,7},{6,4},{7,5},{8,10},{9,11},{10,... | collective-permute-start | bytes 786440 | tf_op jit(solution)/shard_map/ppermute | solution.py:229
  37.5 1.9 %collective-permute-start.2 = (bf16[1024,128]{0,1:T(8,128)(2,1)}, bf16[1024,128]{0,1:T(8,128)(2,1)}, u32[]{:S(2)}, u32[]{:S(2)}) collective-permute-start(bf16[1024,128]{0,1:T(8,128)(2,1)} %get-tuple-element.32), channel_id=1, source_target_pairs={{0,3},{1,2},{2,1},{3,0},{4,7},{5,6},{6,5},{7,4},{8,11},{9,10},{10,... | collective-permute-start | bytes 786440 | tf_op jit(solution)/shard_map/ppermute | solution.py:229
  39.4 5.1 %collective-permute-start.3 = (bf16[1024,128]{0,1:T(8,128)(2,1)}, bf16[1024,128]{0,1:T(8,128)(2,1)}, u32[]{:S(2)}, u32[]{:S(2)}) collective-permute-start(bf16[1024,128]{0,1:T(8,128)(2,1)} %get-tuple-element.31), channel_id=1, source_target_pairs={{0,4},{1,5},{2,6},{3,7},{4,0},{5,1},{6,2},{7,3},{8,12},{9,13},{10,... | collective-permute-start | bytes 786440 | tf_op jit(solution)/shard_map/ppermute | solution.py:229
  44.6 2.0 %collective-permute-start.4 = (bf16[1024,128]{0,1:T(8,128)(2,1)}, bf16[1024,128]{0,1:T(8,128)(2,1)}, u32[]{:S(2)}, u32[]{:S(2)}) collective-permute-start(bf16[1024,128]{0,1:T(8,128)(2,1)} %get-tuple-element.30), channel_id=1, source_target_pairs={{0,5},{1,4},{2,7},{3,6},{4,1},{5,0},{6,3},{7,2},{8,13},{9,12},{10,... | collective-permute-start | bytes 786440 | tf_op jit(solution)/shard_map/ppermute | solution.py:229
  49.6 4.8 %collective-permute-start.5 = (bf16[1024,128]{0,1:T(8,128)(2,1)}, bf16[1024,128]{0,1:T(8,128)(2,1)}, u32[]{:S(2)}, u32[]{:S(2)}) collective-permute-start(bf16[1024,128]{0,1:T(8,128)(2,1)} %get-tuple-element.29), channel_id=1, source_target_pairs={{0,6},{1,7},{2,4},{3,5},{4,2},{5,3},{6,0},{7,1},{8,14},{9,15},{10,... | collective-permute-start | bytes 786440 | tf_op jit(solution)/shard_map/ppermute | solution.py:229
  55.1 8.4 %all-to-all-done = f16[32,25,4,128]{3,2,1,0:T(4,128)(2,1)} async-done(((f16[32,25,4,128]{3,2,1,0:T(4,128)(2,1)}), f16[32,25,4,128]{3,2,1,0:T(4,128)(2,1)}, u32[]{:S(2)}, u32[]{:S(2)}) %all-to-all-start) | async-done | bytes 819232 | tf_op jit(solution)/shard_map/all_to_all | solution.py:302
  64.8 4.7 %shard_map.78 = bf16[32,12,8,128]{3,2,1,0:T(8,128)(2,1)} custom-call(f32[3200,128]{1,0:T(8,128)S(1)} %convert.1.message_ref, bf16[256,256]{1,0:T(8,128)(2,1)S(1)} %get-tuple-element.59.forward_ref, bf16[256,256]{1,0:T(8,128)(2,1)S(1)} %get-tuple-element.60.inverse_ref, bf16[128,2048]{1,0:T(8,128)(2,1)S(1)} %and_convert_fusion.spread_ref), custom_call_target="tpu_custom_call" | custom-call | tf_op jit(solution)/shard_map/pallas_call | solution.py:139
  69.5 7.5 %all-to-all-start.1 = ((bf16[32,12,8,128]{3,2,1,0:T(8,128)(2,1)}), bf16[32,12,8,128]{3,2,1,0:T(8,128)(2,1)S(1)}, u32[]{:S(2)}, u32[]{:S(2)}) async-start(bf16[32,12,8,128]{3,2,1,0:T(8,128)(2,1)} %shard_map.78), calls=%async_computation.1 | async-start | bytes 1572864 | tf_op jit(solution)/shard_map/all_to_all | solution.py:305
  77.0 2.3 %collective-permute-start.6 = (bf16[1024,128]{0,1:T(8,128)(2,1)}, bf16[1024,128]{0,1:T(8,128)(2,1)S(1)}, u32[]{:S(2)}, u32[]{:S(2)}) collective-permute-start(bf16[1024,128]{0,1:T(8,128)(2,1)} %get-tuple-element.28), channel_id=1, source_target_pairs={{0,7},{1,6},{2,5},{3,4},{4,3},{5,2},{6,1},{7,0},{8,15},{9,14},{10,... | collective-permute-start | bytes 786440 | tf_op jit(solution)/shard_map/ppermute | solution.py:229
  79.2 1.7 bitcast_dynamic-update-slice_fusion.5
  80.9 1.7 bitcast_dynamic-update-slice_fusion.4
  82.6 1.7 bitcast_dynamic-update-slice_fusion.3
  84.3 1.7 bitcast_dynamic-update-slice_fusion.2
  86.0 1.7 bitcast_dynamic-update-slice_fusion.1
  93.0 6.5 %all-to-all-done.1 = bf16[32,12,8,128]{3,2,1,0:T(8,128)(2,1)S(1)} async-done(((bf16[32,12,8,128]{3,2,1,0:T(8,128)(2,1)}), bf16[32,12,8,128]{3,2,1,0:T(8,128)(2,1)S(1)}, u32[]{:S(2)}, u32[]{:S(2)}) %all-to-all-start.1) | async-done | bytes 786464 | tf_op jit(solution)/shard_map/all_to_all | solution.py:305
  101.4 1.9 %collective-permute-start.7 = (f16[512,768]{1,0:T(8,128)(2,1)S(1)}, f16[512,768]{1,0:T(8,128)(2,1)S(1)}, u32[]{:S(2)}, u32[]{:S(2)}) collective-permute-start(f16[512,768]{1,0:T(8,128)(2,1)S(1)} %convolution_convert_fusion), channel_id=1, source_target_pairs={{0,1},{1,0},{2,3},{3,2},{4,5},{5,4},{6,7},{7,6},{8,9},{9,8},{10,11... | collective-permute-start | bytes 2359304 | tf_op jit(solution)/shard_map/ppermute | solution.py:312
  105.8 15.4 %all_to_all.25 = f16[4,128,768]{2,1,0:T(8,128)(2,1)S(1)} all-to-all(f16[4,128,768]{2,1,0:T(8,128)(2,1)S(1)} %bitcast.111), channel_id=1, replica_groups=mesh['freq'=16,'line_0'=4,'line_1'=4,'line_2'=2] {'line_1'}, dimensions={0} | all-to-all | bytes 1572864 | tf_op jit(solution)/shard_map/all_to_all | solution.py:250
  121.4 40.7 %all_to_all.26 = f16[4,32,768]{2,1,0:T(8,128)(2,1)S(1)} all-to-all(f16[4,32,768]{2,1,0:T(8,128)(2,1)S(1)} %bitcast.119), channel_id=1, replica_groups=mesh['freq'=16,'line_0'=4,'line_1'=4,'line_2'=2] {'line_0'}, dimensions={0} | all-to-all | bytes 393216 | tf_op jit(solution)/shard_map/all_to_all | solution.py:319
  162.9 13.3 %all_to_all.27 = f32[16,1,32]{2,1,0:T(1,128)S(1)} all-to-all(f32[16,1,32]{2,1,0:T(1,128)S(1)} %get-tuple-element.11), channel_id=1, replica_groups=mesh['freq'=16,'line_0'=4,'line_1'=4,'line_2'=2] {'freq'}, dimensions={0} | all-to-all | bytes 4096 | tf_op jit(solution)/shard_map/all_to_all | solution.py:321
  (70 shorter events, 19.8 us)
Async XLA Ops:
  3.5 60.1 %all-to-all-start = ((f16[32,25,4,128]{3,2,1,0:T(4,128)(2,1)}), f16[32,25,4,128]{3,2,1,0:T(4,128)(2,1)}, u32[]{:S(2)}, u32[]{:S(2)}) async-start(f16[32,25,4,128]{3,2,1,0:T(4,128)(2,1)} %bitcast.6), calls=%async_computation | async-start | bytes 1638400 | tf_op jit(solution)/shard_map/all_to_all | solution.py:302
  30.6 16.0 %copy-start.2 = (s32[64]{0:T(128)S(1)}, s32[64]{0:T(128)}, u32[]{:S(2)}) copy-start(s32[64]{0:T(128)} %param.8) | copy-start | bytes 772
  31.8 17.8 %collective-permute-start = (bf16[1024,128]{0,1:T(8,128)(2,1)S(1)}, bf16[1024,128]{0,1:T(8,128)(2,1)S(1)}, u32[]{:S(2)}, u32[]{:S(2)}) collective-permute-start(bf16[1024,128]{0,1:T(8,128)(2,1)S(1)} %get-tuple-element.34), channel_id=1, source_target_pairs={{0,1},{1,0},{2,3},{3,2},{4,5},{5,4},{6,7},{7,6},{8,9},{9,8},{10,11... | collective-permute-start | bytes 786440 | tf_op jit(solution)/shard_map/ppermute | solution.py:229
  33.9 43.0 %collective-permute-start.1 = (bf16[1024,128]{0,1:T(8,128)(2,1)}, bf16[1024,128]{0,1:T(8,128)(2,1)}, u32[]{:S(2)}, u32[]{:S(2)}) collective-permute-start(bf16[1024,128]{0,1:T(8,128)(2,1)} %get-tuple-element.33), channel_id=1, source_target_pairs={{0,2},{1,3},{2,0},{3,1},{4,6},{5,7},{6,4},{7,5},{8,10},{9,11},{10,... | collective-permute-start | bytes 786440 | tf_op jit(solution)/shard_map/ppermute | solution.py:229
  37.5 43.5 %collective-permute-start.2 = (bf16[1024,128]{0,1:T(8,128)(2,1)}, bf16[1024,128]{0,1:T(8,128)(2,1)}, u32[]{:S(2)}, u32[]{:S(2)}) collective-permute-start(bf16[1024,128]{0,1:T(8,128)(2,1)} %get-tuple-element.32), channel_id=1, source_target_pairs={{0,3},{1,2},{2,1},{3,0},{4,7},{5,6},{6,5},{7,4},{8,11},{9,10},{10,... | collective-permute-start | bytes 786440 | tf_op jit(solution)/shard_map/ppermute | solution.py:229
  39.4 43.2 %collective-permute-start.3 = (bf16[1024,128]{0,1:T(8,128)(2,1)}, bf16[1024,128]{0,1:T(8,128)(2,1)}, u32[]{:S(2)}, u32[]{:S(2)}) collective-permute-start(bf16[1024,128]{0,1:T(8,128)(2,1)} %get-tuple-element.31), channel_id=1, source_target_pairs={{0,4},{1,5},{2,6},{3,7},{4,0},{5,1},{6,2},{7,3},{8,12},{9,13},{10,... | collective-permute-start | bytes 786440 | tf_op jit(solution)/shard_map/ppermute | solution.py:229
  44.6 39.7 %collective-permute-start.4 = (bf16[1024,128]{0,1:T(8,128)(2,1)}, bf16[1024,128]{0,1:T(8,128)(2,1)}, u32[]{:S(2)}, u32[]{:S(2)}) collective-permute-start(bf16[1024,128]{0,1:T(8,128)(2,1)} %get-tuple-element.30), channel_id=1, source_target_pairs={{0,5},{1,4},{2,7},{3,6},{4,1},{5,0},{6,3},{7,2},{8,13},{9,12},{10,... | collective-permute-start | bytes 786440 | tf_op jit(solution)/shard_map/ppermute | solution.py:229
  49.6 36.4 %collective-permute-start.5 = (bf16[1024,128]{0,1:T(8,128)(2,1)}, bf16[1024,128]{0,1:T(8,128)(2,1)}, u32[]{:S(2)}, u32[]{:S(2)}) collective-permute-start(bf16[1024,128]{0,1:T(8,128)(2,1)} %get-tuple-element.29), channel_id=1, source_target_pairs={{0,6},{1,7},{2,4},{3,5},{4,2},{5,3},{6,0},{7,1},{8,14},{9,15},{10,... | collective-permute-start | bytes 786440 | tf_op jit(solution)/shard_map/ppermute | solution.py:229
  69.5 30.1 %all-to-all-start.1 = ((bf16[32,12,8,128]{3,2,1,0:T(8,128)(2,1)}), bf16[32,12,8,128]{3,2,1,0:T(8,128)(2,1)S(1)}, u32[]{:S(2)}, u32[]{:S(2)}) async-start(bf16[32,12,8,128]{3,2,1,0:T(8,128)(2,1)} %shard_map.78), calls=%async_computation.1 | async-start | bytes 1572864 | tf_op jit(solution)/shard_map/all_to_all | solution.py:305
  77.0 11.1 %collective-permute-start.6 = (bf16[1024,128]{0,1:T(8,128)(2,1)}, bf16[1024,128]{0,1:T(8,128)(2,1)S(1)}, u32[]{:S(2)}, u32[]{:S(2)}) collective-permute-start(bf16[1024,128]{0,1:T(8,128)(2,1)} %get-tuple-element.28), channel_id=1, source_target_pairs={{0,7},{1,6},{2,5},{3,4},{4,3},{5,2},{6,1},{7,0},{8,15},{9,14},{10,... | collective-permute-start | bytes 786440 | tf_op jit(solution)/shard_map/ppermute | solution.py:229
  88.7 4.1 %copy-start.1 = (bf16[8,1024,128]{1,2,0:T(8,128)(2,1)S(1)}, bf16[8,1024,128]{1,2,0:T(8,128)(2,1)}, u32[]{:S(2)}) copy-start(bf16[8,1024,128]{1,2,0:T(8,128)(2,1)} %bitcast_dynamic-update-slice_fusion) | copy-start | bytes 6291460
  101.4 4.2 %collective-permute-start.7 = (f16[512,768]{1,0:T(8,128)(2,1)S(1)}, f16[512,768]{1,0:T(8,128)(2,1)S(1)}, u32[]{:S(2)}, u32[]{:S(2)}) collective-permute-start(f16[512,768]{1,0:T(8,128)(2,1)S(1)} %convolution_convert_fusion), channel_id=1, source_target_pairs={{0,1},{1,0},{2,3},{3,2},{4,5},{5,4},{6,7},{7,6},{8,9},{9,8},{10,11... | collective-permute-start | bytes 2359304 | tf_op jit(solution)/shard_map/ppermute | solution.py:312
  105.8 56.3 %copy-start = (f32[32,1,2,384]{3,2,1,0:T(2,128)S(1)}, f32[32,1,2,384]{3,2,1,0:T(2,128)}, u32[]{:S(2)}) copy-start(f32[32,1,2,384]{3,2,1,0:T(2,128)} %direct_ref.1) | copy-start | bytes 294916

commit v7 on v6

--- a/solution.py
+++ b/solution.py
@@ -58,7 +58,19 @@
     return found.astype(jnp.bfloat16)
 
 
-def middle_kernel(message_ref, forward_ref, inverse_ref, spread_ref, out_ref, wave_ref, spread_out_ref, spectrum_ref, decomposed_ref):
+def middle_kernel(
+    message_ref,
+    forward_ref,
+    inverse_ref,
+    spread_ref,
+    out_ref,
+    wave_ref,
+    spread_out_ref,
+    spectrum_ref,
+    decomposed_ref,
+    ready_ref,
+    sent,
+):
     forward = forward_ref[...]
     inverse = inverse_ref[...]
     lane = lax.broadcasted_iota(jnp.int32, (32, 128), 1)
@@ -73,29 +85,34 @@
     operators = jnp.concatenate(early + late, 0).astype(jnp.bfloat16)
     spread_out_ref[...] = jnp.dot(operators, spread_ref[...], preferred_element_type=jnp.float32)
 
-    def load(r):
-        tiles = [
-            jnp.concatenate(
-                [message_ref[pl.ds((g * 3 + t) * 8 + r, 32, stride=100), :] for g in range(4)], 0
-            )
-            for t in range(3)
-        ]
-        value = jnp.concatenate(tiles, 1)
+    def load(t, pair):
+        value = jnp.concatenate(
+            [
+                jnp.concatenate(
+                    [
+                        message_ref[pl.ds((g * 3 + t) * 8 + 2 * pair + side, 32, stride=100), :]
+                        for g in range(4)
+                    ],
+                    0,
+                )
+                for side in range(2)
+            ],
+            1,
+        )
         high = value.astype(jnp.bfloat16)
         low = (value - high.astype(jnp.float32)).astype(jnp.bfloat16)
         both = jnp.dot(
             forward, jnp.concatenate([high, low], 0), preferred_element_type=jnp.float32
         )
-        spectrum_ref[r % 2] = both[:128] + both[128:]
-
-    def decompose(r):
-        for t in range(3):
-            at = pl.ds(128 * t, 128)
+        spectrum_ref[pair % 2] = both[:128] + both[128:]
+
+    def decompose(t, pair):
+        for side in range(2):
+            r = 2 * pair + side
+            at = pl.ds(128 * side, 128)
             for line in range(2):
-                rows = pl.ds(32 * line, 32)
-                imag_rows = pl.ds(64 + 32 * line, 32)
-                field_real = spectrum_ref[r % 2, rows, at]
-                field_imag = spectrum_ref[r % 2, imag_rows, at]
+                field_real = spectrum_ref[pair % 2, pl.ds(32 * line, 32), at]
+                field_imag = spectrum_ref[pair % 2, pl.ds(64 + 32 * line, 32), at]
                 real_sum = None
                 imag_sum = None
                 for shift in range(4):
@@ -114,38 +131,46 @@
                 for value, first in ((real_sum, 0), (imag_sum, 64)):
                     high = value.astype(jnp.bfloat16)
                     low = (value - high.astype(jnp.float32)).astype(jnp.bfloat16)
-                    decomposed_ref[r % 2, pl.ds(first + 32 * line, 32), at] = high
-                    decomposed_ref[r % 2, pl.ds(128 + first + 32 * line, 32), at] = low
-
-    def store(r):
-        both = jnp.dot(inverse, decomposed_ref[r % 2], preferred_element_type=jnp.float32)
+                    decomposed_ref[pair % 2, pl.ds(first + 32 * line, 32), at] = high
+                    decomposed_ref[pair % 2, pl.ds(128 + first + 32 * line, 32), at] = low
+
+    def store(t, pair):
+        both = jnp.dot(inverse, decomposed_ref[pair % 2], preferred_element_type=jnp.float32)
         wave = both[:128] + both[128:]
-        for g in range(4):
-            for t in range(3):
-                wave_ref[pl.ds((g * 3 + t) * 8 + r, 32, stride=96), :] = wave[
-                    32 * g : 32 * g + 32, 128 * t : 128 * t + 128
-                ]
-
-    load(0)
-    for r in range(8):
-        if r < 7:
-            load(r + 1)
-        decompose(r)
-        store(r)
-    out_ref[...] = wave_ref[...].reshape(32, 12, 8, 128).astype(jnp.bfloat16)
+        for side in range(2):
+            for g in range(4):
+                rows = pl.ds(g * 8 + 2 * pair + side, 32, stride=32)
+                wave_ref[rows, :] = wave[32 * g : 32 * g + 32, 128 * side : 128 * side + 128]
+
+    def leaving(t):
+        return pltpu.make_async_copy(ready_ref.at[t], out_ref.at[:, :, t], sent.at[t])
+
+    for t in range(3):
+        load(t, 0)
+        for pair in range(4):
+            if pair < 3:
+                load(t, pair + 1)
+            decompose(t, pair)
+            store(t, pair)
+        ready_ref[t] = wave_ref[...].reshape(32, 4, 8, 128).astype(jnp.bfloat16)
+        leaving(t).start()
+    for t in range(3):
+        leaving(t).wait()
 
 
 def middle(message, forward, inverse, spread):
     return pl.pallas_call(
         middle_kernel,
-        out_shape=pltpu.VMEM((32, 12, 8, 128), jnp.bfloat16),
+        out_shape=jax.ShapeDtypeStruct((32, 4, 3, 8, 128), jnp.bfloat16),
         in_specs=[pl.BlockSpec(memory_space=pltpu.VMEM)] * 4,
-        out_specs=pl.BlockSpec(memory_space=pltpu.VMEM),
+        out_specs=pl.BlockSpec(memory_space=pl.ANY),
         scratch_shapes=[
-            pltpu.VMEM((3072, 128), jnp.float32),
+            pltpu.VMEM((1024, 128), jnp.float32),
             pltpu.VMEM((256, 2048), jnp.float32),
-            pltpu.VMEM((2, 128, 384), jnp.float32),
-            pltpu.VMEM((2, 256, 384), jnp.bfloat16),
+            pltpu.VMEM((2, 128, 256), jnp.float32),
+            pltpu.VMEM((2, 256, 256), jnp.bfloat16),
+            pltpu.VMEM((3, 32, 4, 8, 128), jnp.bfloat16),
+            pltpu.SemaphoreType.DMA((3,)),
         ],
     )(
         pltpu.with_memory_space_constraint(message.astype(jnp.float32).reshape(3200, 128), pltpu.VMEM),
@@ -157,22 +182,17 @@
     row = lax.broadcasted_iota(jnp.int32, (128, 128), 0)
     lane = lax.broadcasted_iota(jnp.int32, (128, 128), 1)
 
-    def put_field(part):
+    def put_field(part, t):
         for line in range(2):
             for half in range(2):
                 live = row + 128 * half < live_ref[line]
-                for t in range(3):
-                    block = jnp.concatenate(
-                        [
-                            field_ref[pl.ds(384 * c + 128 * t + 2 * half + line, 32, stride=4), :]
-                            for c in range(4)
-                        ],
-                        0,
-                    )
-                    block = jnp.where(live, block.T, jnp.float32(0.0))
-                    for device in range(16):
-                        place = 100 * (16 * half + device) + 48 * part + 24 * line + 8 * t
-                        out_ref[place : place + 8, :] = block[8 * device : 8 * device + 8]
+                block = jnp.concatenate(
+                    [field_ref[0, c, pl.ds(2 * half + line, 32, stride=4), :] for c in range(4)], 0
+                )
+                block = jnp.where(live, block.T, jnp.float32(0.0))
+                for device in range(16):
+                    place = 100 * (16 * half + device) + 48 * part + 24 * line + 8 * t
+                    out_ref[place : place + 8, :] = block[8 * device : 8 * device + 8]
 
     def put_operators():
         for half in range(2):
@@ -183,27 +203,27 @@
                 place = 100 * (16 * half + device) + 96
                 out_ref[place : place + 4, :] = block[8 * device : 8 * device + 4]
 
-    @pl.when(pl.program_id(0) == 0)
-    def _():
-        put_field(0)
-        put_operators()
-
-    @pl.when(pl.program_id(0) == 1)
-    def _():
-        put_field(1)
+    for part in range(2):
+        for t in range(3):
+
+            @pl.when(pl.program_id(0) == 3 * part + t)
+            def _():
+                put_field(part, t)
+                if part == 0 and t == 0:
+                    put_operators()
 
 
 def outgoing(field, live_count, decomposer):
-    rows = field.reshape(2, 4, 96, 2, 2, 128).transpose(0, 1, 2, 4, 3, 5).reshape(3072, 128)
+    rows = field.reshape(2, 4, 96, 2, 2, 128).transpose(0, 1, 2, 4, 3, 5).reshape(2, 4, 384, 128)
     operator_rows = decomposer.reshape(32, 2, 2, 128).transpose(0, 2, 1, 3).reshape(128, 128)
     tiles = pl.pallas_call(
         outgoing_kernel,
-        grid=(2,),
+        grid=(6,),
         out_shape=pltpu.VMEM((3200, 128), jnp.float32),
         in_specs=[
             pl.BlockSpec(memory_space=pltpu.SMEM),
-            pl.BlockSpec((1536, 128), lambda part: (part, 0)),
-            pl.BlockSpec((128, 128), lambda part: (0, 0)),
+            pl.BlockSpec((1, 4, 128, 128), lambda step: (step // 3, 0, step % 3, 0)),
+            pl.BlockSpec((128, 128), lambda step: (0, 0)),
         ],
         out_specs=pl.BlockSpec(memory_space=pltpu.VMEM),
     )(live_count, rows, operator_rows)

time: 178 us -> 178 us (level)
  waiting for transfers between devices: 16.5 us -> 13.3 us
    all_to_all x1, waiting for transfers between devices: 8.42 us -> 5.22 us  [on_device(): message = lax.all_to_all(message, RECEIVER, 0, 0, tiled=True)]
  transfers between devices with their start and end apart: 10 -> 10, of which waited for: 4 -> 4; matrix products, arithmetic and copies ran while one was open for 17% -> 18% of each run, Pallas kernels for 3% -> 2%
where the time goes in v7:
time: 178 us; the launch traced here: 177 us
  blocking collectives  69.3 us (39%)
  starting transfers between devices  49.4 us (28%)
  local copies, waits for them, and re-layouts  23.3 us (13%)
  waiting for transfers between devices  13.3 us (7%)
  Pallas kernels  8.97 us (5%)
  matrix products  6.12 us (3%)
  other arithmetic  5.61 us (3%)
    all_to_all x1, blocking collectives, on_device(): blocks = lax.all_to_all(blocks, 'line_0', 0, 0, tiled=True)  40.6 us
    ppermute x7, starting transfers between devices, exchanged(): received.append(lax.ppermute(block, PLANE, pairs))  21.9 us
    all_to_all x1, starting transfers between devices, on_device(): message = lax.all_to_all(message, RECEIVER, 0, 0, tiled=True)  18.1 us
    all_to_all x1, blocking collectives, summed(): blocks = lax.all_to_all(blocks, axis, 0, 0, tiled=True)  15.4 us
    unnamed x20, local copies, waits for them, and re-layouts  15 us
    all_to_all x1, blocking collectives, on_device(): energies = lax.all_to_all(energies, 'freq', 0, 0, tiled=True)  13.3 us
    all_to_all x1, starting transfers between devices, on_device(): wave = lax.all_to_all(wave, 'line_0', 0, 0, tiled=True)  7.55 us
    all_to_all x1, waiting for transfers between devices, on_device(): wave = lax.all_to_all(wave, 'line_0', 0, 0, tiled=True)  6.52 us
  transfers between devices with their start and end apart: 10, of which 4 were waited for; matrix products, arithmetic and copies ran while one was open for 18% of the time, Pallas kernels for 2%

profile of v7, /device:TPU:2, one launch (start us, length us, event | category | flops | bytes accessed | tf_op | source)
XLA Modules:
  0.0 177.2 jit_solution(3599677408248179758)
XLA Ops:
  0.6 3.7 %shard_map.77 = f32[3200,128]{1,0:T(8,128)S(1)} custom-call(s32[2]{0:T(128)} %live_ref.1, f32[2,4,384,128]{3,2,1,0:T(8,128)} %bitcast.118, f32[128,128]{1,0:T(8,128)} %bitcast.121), custom_call_target="tpu_custom_call" | custom-call | tf_op jit(solution)/shard_map/pallas_call | solution.py:219
  5.4 18.1 %all-to-all-start = ((f16[32,25,4,128]{3,2,1,0:T(4,128)(2,1)}), f16[32,25,4,128]{3,2,1,0:T(4,128)(2,1)S(1)}, u32[]{:S(2)}, u32[]{:S(2)}) async-start(f16[32,25,4,128]{3,2,1,0:T(4,128)(2,1)} %bitcast.6), calls=%async_computation | async-start | bytes 1638400 | tf_op jit(solution)/shard_map/all_to_all | solution.py:322
  23.5 3.2 %reshape_squeeze.3 = bf16[4,4,2,32,1024]{4,3,2,1,0:T(8,128)(2,1)S(1)} reshape(bf16[1,1024,2,512]{3,2,1,0:T(2,128)(2,1)} %param.10) | data formatting | bytes 4194304 | tf_op jit(solution)/shard_map/reshape;squeeze | solution.py:234
  28.4 4.1 %fusion.2 = bf16[1024,1024]{0,1:T(8,128)(2,1)S(1)} fusion(bf16[1024,1024]{1,0:T(8,128)(2,1)} %bitcast.115, s32[1024]{0:T(1024)S(1)} %fusion.46), kind=kOutput, calls=%fused_computation.3 | convolution fusion | flops 2149580800 | bytes 4198400 | tf_op jit(solution)/shard_map/dot_general | solution.py:239
  33.8 2.2 %collective-permute-start = (bf16[1024,128]{0,1:T(8,128)(2,1)}, bf16[1024,128]{0,1:T(8,128)(2,1)}, u32[]{:S(2)}, u32[]{:S(2)}) collective-permute-start(bf16[1024,128]{0,1:T(8,128)(2,1)} %get-tuple-element.34), channel_id=1, source_target_pairs={{0,1},{1,0},{2,3},{3,2},{4,5},{5,4},{6,7},{7,6},{8,9},{9,8},{10,11... | collective-permute-start | bytes 786440 | tf_op jit(solution)/shard_map/ppermute | solution.py:249
  35.9 3.5 %collective-permute-start.1 = (bf16[1024,128]{0,1:T(8,128)(2,1)}, bf16[1024,128]{0,1:T(8,128)(2,1)}, u32[]{:S(2)}, u32[]{:S(2)}) collective-permute-start(bf16[1024,128]{0,1:T(8,128)(2,1)} %get-tuple-element.33), channel_id=1, source_target_pairs={{0,2},{1,3},{2,0},{3,1},{4,6},{5,7},{6,4},{7,5},{8,10},{9,11},{10,... | collective-permute-start | bytes 786440 | tf_op jit(solution)/shard_map/ppermute | solution.py:249
  39.5 1.9 %collective-permute-start.2 = (bf16[1024,128]{0,1:T(8,128)(2,1)}, bf16[1024,128]{0,1:T(8,128)(2,1)}, u32[]{:S(2)}, u32[]{:S(2)}) collective-permute-start(bf16[1024,128]{0,1:T(8,128)(2,1)} %get-tuple-element.32), channel_id=1, source_target_pairs={{0,3},{1,2},{2,1},{3,0},{4,7},{5,6},{6,5},{7,4},{8,11},{9,10},{10,... | collective-permute-start | bytes 786440 | tf_op jit(solution)/shard_map/ppermute | solution.py:249
  41.4 5.2 %collective-permute-start.3 = (bf16[1024,128]{0,1:T(8,128)(2,1)}, bf16[1024,128]{0,1:T(8,128)(2,1)}, u32[]{:S(2)}, u32[]{:S(2)}) collective-permute-start(bf16[1024,128]{0,1:T(8,128)(2,1)} %get-tuple-element.31), channel_id=1, source_target_pairs={{0,4},{1,5},{2,6},{3,7},{4,0},{5,1},{6,2},{7,3},{8,12},{9,13},{10,... | collective-permute-start | bytes 786440 | tf_op jit(solution)/shard_map/ppermute | solution.py:249
  46.6 2.0 %collective-permute-start.4 = (bf16[1024,128]{0,1:T(8,128)(2,1)}, bf16[1024,128]{0,1:T(8,128)(2,1)}, u32[]{:S(2)}, u32[]{:S(2)}) collective-permute-start(bf16[1024,128]{0,1:T(8,128)(2,1)} %get-tuple-element.30), channel_id=1, source_target_pairs={{0,5},{1,4},{2,7},{3,6},{4,1},{5,0},{6,3},{7,2},{8,13},{9,12},{10,... | collective-permute-start | bytes 786440 | tf_op jit(solution)/shard_map/ppermute | solution.py:249
  53.6 4.8 %collective-permute-start.5 = (bf16[1024,128]{0,1:T(8,128)(2,1)}, bf16[1024,128]{0,1:T(8,128)(2,1)}, u32[]{:S(2)}, u32[]{:S(2)}) collective-permute-start(bf16[1024,128]{0,1:T(8,128)(2,1)} %get-tuple-element.29), channel_id=1, source_target_pairs={{0,6},{1,7},{2,4},{3,5},{4,2},{5,3},{6,0},{7,1},{8,14},{9,15},{10,... | collective-permute-start | bytes 786440 | tf_op jit(solution)/shard_map/ppermute | solution.py:249
  58.5 1.7 bitcast_dynamic-update-slice_fusion.6
  60.1 5.2 %all-to-all-done = f16[32,25,4,128]{3,2,1,0:T(4,128)(2,1)S(1)} async-done(((f16[32,25,4,128]{3,2,1,0:T(4,128)(2,1)}), f16[32,25,4,128]{3,2,1,0:T(4,128)(2,1)S(1)}, u32[]{:S(2)}, u32[]{:S(2)}) %all-to-all-start) | async-done | bytes 819232 | tf_op jit(solution)/shard_map/all_to_all | solution.py:322
  65.5 4.4 %shard_map.78 = bf16[32,4,3,8,128]{4,3,2,1,0:T(8,128)(2,1)} custom-call(f32[3200,128]{1,0:T(8,128)S(1)} %convert.1.message_ref, bf16[256,256]{1,0:T(8,128)(2,1)S(1)} %get-tuple-element.59.forward_ref, bf16[256,256]{1,0:T(8,128)(2,1)S(1)} %get-tuple-element.60.inverse_ref, bf16[128,2048]{1,0:T(8,128)(2,1)S(1)} %and_convert_fusion.spread_ref), custom_call_target="tpu_custom_call" | custom-call | tf_op jit(solution)/shard_map/pallas_call | solution.py:162
  69.9 7.6 %all-to-all-start.1 = ((bf16[32,4,3,8,128]{4,3,2,1,0:T(8,128)(2,1)}), bf16[32,4,3,8,128]{4,3,2,1,0:T(8,128)(2,1)S(1)}, u32[]{:S(2)}, u32[]{:S(2)}) async-start(bf16[32,4,3,8,128]{4,3,2,1,0:T(8,128)(2,1)} %shard_map.78), calls=%async_computation.1 | async-start | bytes 1572864 | tf_op jit(solution)/shard_map/all_to_all | solution.py:325
  77.4 2.2 %collective-permute-start.6 = (bf16[1024,128]{0,1:T(8,128)(2,1)}, bf16[1024,128]{0,1:T(8,128)(2,1)S(1)}, u32[]{:S(2)}, u32[]{:S(2)}) collective-permute-start(bf16[1024,128]{0,1:T(8,128)(2,1)} %get-tuple-element.28), channel_id=1, source_target_pairs={{0,7},{1,6},{2,5},{3,4},{4,3},{5,2},{6,1},{7,0},{8,15},{9,14},{10,... | collective-permute-start | bytes 786440 | tf_op jit(solution)/shard_map/ppermute | solution.py:249
  79.7 1.7 bitcast_dynamic-update-slice_fusion.5
  81.4 1.7 bitcast_dynamic-update-slice_fusion.4
  84.7 1.7 bitcast_dynamic-update-slice_fusion.2
  86.4 1.7 bitcast_dynamic-update-slice_fusion.1
  93.5 6.5 %all-to-all-done.1 = bf16[32,4,3,8,128]{4,3,2,1,0:T(8,128)(2,1)S(1)} async-done(((bf16[32,4,3,8,128]{4,3,2,1,0:T(8,128)(2,1)}), bf16[32,4,3,8,128]{4,3,2,1,0:T(8,128)(2,1)S(1)}, u32[]{:S(2)}, u32[]{:S(2)}) %all-to-all-start.1) | async-done | bytes 786464 | tf_op jit(solution)/shard_map/all_to_all | solution.py:325
  101.8 1.9 %collective-permute-start.7 = (f16[512,768]{1,0:T(8,128)(2,1)S(1)}, f16[512,768]{1,0:T(8,128)(2,1)S(1)}, u32[]{:S(2)}, u32[]{:S(2)}) collective-permute-start(f16[512,768]{1,0:T(8,128)(2,1)S(1)} %convolution_convert_fusion), channel_id=1, source_target_pairs={{0,1},{1,0},{2,3},{3,2},{4,5},{5,4},{6,7},{7,6},{8,9},{9,8},{10,11... | collective-permute-start | bytes 2359304 | tf_op jit(solution)/shard_map/ppermute | solution.py:332
  106.3 15.4 %all_to_all.25 = f16[4,128,768]{2,1,0:T(8,128)(2,1)S(1)} all-to-all(f16[4,128,768]{2,1,0:T(8,128)(2,1)S(1)} %bitcast.112), channel_id=1, replica_groups=mesh['freq'=16,'line_0'=4,'line_1'=4,'line_2'=2] {'line_1'}, dimensions={0} | all-to-all | bytes 1572864 | tf_op jit(solution)/shard_map/all_to_all | solution.py:270
  121.8 40.6 %all_to_all.26 = f16[4,32,768]{2,1,0:T(8,128)(2,1)S(1)} all-to-all(f16[4,32,768]{2,1,0:T(8,128)(2,1)S(1)} %bitcast.120), channel_id=1, replica_groups=mesh['freq'=16,'line_0'=4,'line_1'=4,'line_2'=2] {'line_0'}, dimensions={0} | all-to-all | bytes 393216 | tf_op jit(solution)/shard_map/all_to_all | solution.py:339
  163.3 13.3 %all_to_all.27 = f32[16,1,32]{2,1,0:T(1,128)S(1)} all-to-all(f32[16,1,32]{2,1,0:T(1,128)S(1)} %get-tuple-element.11), channel_id=1, replica_groups=mesh['freq'=16,'line_0'=4,'line_1'=4,'line_2'=2] {'freq'}, dimensions={0} | all-to-all | bytes 4096 | tf_op jit(solution)/shard_map/all_to_all | solution.py:341
  (70 shorter events, 21.8 us)
Async XLA Ops:
  5.4 60.0 %all-to-all-start = ((f16[32,25,4,128]{3,2,1,0:T(4,128)(2,1)}), f16[32,25,4,128]{3,2,1,0:T(4,128)(2,1)S(1)}, u32[]{:S(2)}, u32[]{:S(2)}) async-start(f16[32,25,4,128]{3,2,1,0:T(4,128)(2,1)} %bitcast.6), calls=%async_computation | async-start | bytes 1638400 | tf_op jit(solution)/shard_map/all_to_all | solution.py:322
  32.4 16.2 %copy-start.2 = (s32[64]{0:T(128)S(1)}, s32[64]{0:T(128)}, u32[]{:S(2)}) copy-start(s32[64]{0:T(128)} %param.8) | copy-start | bytes 772
  33.8 19.9 %collective-permute-start = (bf16[1024,128]{0,1:T(8,128)(2,1)}, bf16[1024,128]{0,1:T(8,128)(2,1)}, u32[]{:S(2)}, u32[]{:S(2)}) collective-permute-start(bf16[1024,128]{0,1:T(8,128)(2,1)} %get-tuple-element.34), channel_id=1, source_target_pairs={{0,1},{1,0},{2,3},{3,2},{4,5},{5,4},{6,7},{7,6},{8,9},{9,8},{10,11... | collective-permute-start | bytes 786440 | tf_op jit(solution)/shard_map/ppermute | solution.py:249
  35.9 41.5 %collective-permute-start.1 = (bf16[1024,128]{0,1:T(8,128)(2,1)}, bf16[1024,128]{0,1:T(8,128)(2,1)}, u32[]{:S(2)}, u32[]{:S(2)}) collective-permute-start(bf16[1024,128]{0,1:T(8,128)(2,1)} %get-tuple-element.33), channel_id=1, source_target_pairs={{0,2},{1,3},{2,0},{3,1},{4,6},{5,7},{6,4},{7,5},{8,10},{9,11},{10,... | collective-permute-start | bytes 786440 | tf_op jit(solution)/shard_map/ppermute | solution.py:249
  39.5 41.9 %collective-permute-start.2 = (bf16[1024,128]{0,1:T(8,128)(2,1)}, bf16[1024,128]{0,1:T(8,128)(2,1)}, u32[]{:S(2)}, u32[]{:S(2)}) collective-permute-start(bf16[1024,128]{0,1:T(8,128)(2,1)} %get-tuple-element.32), channel_id=1, source_target_pairs={{0,3},{1,2},{2,1},{3,0},{4,7},{5,6},{6,5},{7,4},{8,11},{9,10},{10,... | collective-permute-start | bytes 786440 | tf_op jit(solution)/shard_map/ppermute | solution.py:249
  41.4 41.6 %collective-permute-start.3 = (bf16[1024,128]{0,1:T(8,128)(2,1)}, bf16[1024,128]{0,1:T(8,128)(2,1)}, u32[]{:S(2)}, u32[]{:S(2)}) collective-permute-start(bf16[1024,128]{0,1:T(8,128)(2,1)} %get-tuple-element.31), channel_id=1, source_target_pairs={{0,4},{1,5},{2,6},{3,7},{4,0},{5,1},{6,2},{7,3},{8,12},{9,13},{10,... | collective-permute-start | bytes 786440 | tf_op jit(solution)/shard_map/ppermute | solution.py:249
  46.6 38.2 %collective-permute-start.4 = (bf16[1024,128]{0,1:T(8,128)(2,1)}, bf16[1024,128]{0,1:T(8,128)(2,1)}, u32[]{:S(2)}, u32[]{:S(2)}) collective-permute-start(bf16[1024,128]{0,1:T(8,128)(2,1)} %get-tuple-element.30), channel_id=1, source_target_pairs={{0,5},{1,4},{2,7},{3,6},{4,1},{5,0},{6,3},{7,2},{8,13},{9,12},{10,... | collective-permute-start | bytes 786440 | tf_op jit(solution)/shard_map/ppermute | solution.py:249
  53.6 32.8 %collective-permute-start.5 = (bf16[1024,128]{0,1:T(8,128)(2,1)}, bf16[1024,128]{0,1:T(8,128)(2,1)}, u32[]{:S(2)}, u32[]{:S(2)}) collective-permute-start(bf16[1024,128]{0,1:T(8,128)(2,1)} %get-tuple-element.29), channel_id=1, source_target_pairs={{0,6},{1,7},{2,4},{3,5},{4,2},{5,3},{6,0},{7,1},{8,14},{9,15},{10,... | collective-permute-start | bytes 786440 | tf_op jit(solution)/shard_map/ppermute | solution.py:249
  69.9 30.1 %all-to-all-start.1 = ((bf16[32,4,3,8,128]{4,3,2,1,0:T(8,128)(2,1)}), bf16[32,4,3,8,128]{4,3,2,1,0:T(8,128)(2,1)S(1)}, u32[]{:S(2)}, u32[]{:S(2)}) async-start(bf16[32,4,3,8,128]{4,3,2,1,0:T(8,128)(2,1)} %shard_map.78), calls=%async_computation.1 | async-start | bytes 1572864 | tf_op jit(solution)/shard_map/all_to_all | solution.py:325
  77.4 11.0 %collective-permute-start.6 = (bf16[1024,128]{0,1:T(8,128)(2,1)}, bf16[1024,128]{0,1:T(8,128)(2,1)S(1)}, u32[]{:S(2)}, u32[]{:S(2)}) collective-permute-start(bf16[1024,128]{0,1:T(8,128)(2,1)} %get-tuple-element.28), channel_id=1, source_target_pairs={{0,7},{1,6},{2,5},{3,4},{4,3},{5,2},{6,1},{7,0},{8,15},{9,14},{10,... | collective-permute-start | bytes 786440 | tf_op jit(solution)/shard_map/ppermute | solution.py:249
  89.2 4.1 %copy-start.1 = (bf16[8,1024,128]{1,2,0:T(8,128)(2,1)S(1)}, bf16[8,1024,128]{1,2,0:T(8,128)(2,1)}, u32[]{:S(2)}) copy-start(bf16[8,1024,128]{1,2,0:T(8,128)(2,1)} %bitcast_dynamic-update-slice_fusion) | copy-start | bytes 6291460
  101.8 4.2 %collective-permute-start.7 = (f16[512,768]{1,0:T(8,128)(2,1)S(1)}, f16[512,768]{1,0:T(8,128)(2,1)S(1)}, u32[]{:S(2)}, u32[]{:S(2)}) collective-permute-start(f16[512,768]{1,0:T(8,128)(2,1)S(1)} %convolution_convert_fusion), channel_id=1, source_target_pairs={{0,1},{1,0},{2,3},{3,2},{4,5},{5,4},{6,7},{7,6},{8,9},{9,8},{10,11... | collective-permute-start | bytes 2359304 | tf_op jit(solution)/shard_map/ppermute | solution.py:332
  106.3 56.2 %copy-start = (f32[32,1,2,384]{3,2,1,0:T(2,128)S(1)}, f32[32,1,2,384]{3,2,1,0:T(2,128)}, u32[]{:S(2)}) copy-start(f32[32,1,2,384]{3,2,1,0:T(2,128)} %direct_ref.1) | copy-start | bytes 294916

commit v8 on v7

--- a/solution.py
+++ b/solution.py
@@ -182,17 +182,22 @@
     row = lax.broadcasted_iota(jnp.int32, (128, 128), 0)
     lane = lax.broadcasted_iota(jnp.int32, (128, 128), 1)
 
-    def put_field(part, t):
+    def put_field(part):
         for line in range(2):
             for half in range(2):
                 live = row + 128 * half < live_ref[line]
-                block = jnp.concatenate(
-                    [field_ref[0, c, pl.ds(2 * half + line, 32, stride=4), :] for c in range(4)], 0
-                )
-                block = jnp.where(live, block.T, jnp.float32(0.0))
-                for device in range(16):
-                    place = 100 * (16 * half + device) + 48 * part + 24 * line + 8 * t
-                    out_ref[place : place + 8, :] = block[8 * device : 8 * device + 8]
+                for t in range(3):
+                    block = jnp.concatenate(
+                        [
+                            field_ref[pl.ds(384 * c + 128 * t + 2 * half + line, 32, stride=4), :]
+                            for c in range(4)
+                        ],
+                        0,
+                    )
+                    block = jnp.where(live, block.T, jnp.float32(0.0))
+                    for device in range(16):
+                        place = 100 * (16 * half + device) + 48 * part + 24 * line + 8 * t
+                        out_ref[place : place + 8, :] = block[8 * device : 8 * device + 8]
 
     def put_operators():
         for half in range(2):
@@ -203,27 +208,27 @@
                 place = 100 * (16 * half + device) + 96
                 out_ref[place : place + 4, :] = block[8 * device : 8 * device + 4]
 
-    for part in range(2):
-        for t in range(3):
-
-            @pl.when(pl.program_id(0) == 3 * part + t)
-            def _():
-                put_field(part, t)
-                if part == 0 and t == 0:
-                    put_operators()
+    @pl.when(pl.program_id(0) == 0)
+    def _():
+        put_field(0)
+        put_operators()
+
+    @pl.when(pl.program_id(0) == 1)
+    def _():
+        put_field(1)
 
 
 def outgoing(field, live_count, decomposer):
-    rows = field.reshape(2, 4, 96, 2, 2, 128).transpose(0, 1, 2, 4, 3, 5).reshape(2, 4, 384, 128)
+    rows = field.reshape(2, 4, 96, 2, 2, 128).transpose(0, 1, 2, 4, 3, 5).reshape(3072, 128)
     operator_rows = decomposer.reshape(32, 2, 2, 128).transpose(0, 2, 1, 3).reshape(128, 128)
     tiles = pl.pallas_call(
         outgoing_kernel,
-        grid=(6,),
+        grid=(2,),
         out_shape=pltpu.VMEM((3200, 128), jnp.float32),
         in_specs=[
             pl.BlockSpec(memory_space=pltpu.SMEM),
-            pl.BlockSpec((1, 4, 128, 128), lambda step: (step // 3, 0, step % 3, 0)),
-            pl.BlockSpec((128, 128), lambda step: (0, 0)),
+            pl.BlockSpec((1536, 128), lambda part: (part, 0)),
+            pl.BlockSpec((128, 128), lambda part: (0, 0)),
         ],
         out_specs=pl.BlockSpec(memory_space=pltpu.VMEM),
     )(live_count, rows, operator_rows)

time: 178 us -> 176 us (0.989)
  Pallas kernels: 8.97 us -> 7.02 us
    pallas_call x1, Pallas kernels: 3.73 us -> 1.78 us  [outgoing(): pl.pallas_call(outgoing_kernel, grid=(2,), out_shape=pltpu.VMEM((3200, 12...]
  transfers between devices with their start and end apart: 10 -> 10, of which waited for: 4 -> 4; matrix products, arithmetic and copies ran while one was open for 18% -> 18% of each run, Pallas kernels for 2% -> 3%
where the time goes in v8:
time: 176 us; the launch traced here: 175 us
  blocking collectives  69.3 us (39%)
  starting transfers between devices  49.4 us (28%)
  local copies, waits for them, and re-layouts  23.3 us (13%)
  waiting for transfers between devices  13.3 us (8%)
  Pallas kernels  7.02 us (4%)
  matrix products  6.12 us (3%)
  other arithmetic  5.61 us (3%)
    all_to_all x1, blocking collectives, on_device(): blocks = lax.all_to_all(blocks, 'line_0', 0, 0, tiled=True)  40.6 us
    ppermute x7, starting transfers between devices, exchanged(): received.append(lax.ppermute(block, PLANE, pairs))  21.9 us
    all_to_all x1, starting transfers between devices, on_device(): message = lax.all_to_all(message, RECEIVER, 0, 0, tiled=True)  18.1 us
    all_to_all x1, blocking collectives, summed(): blocks = lax.all_to_all(blocks, axis, 0, 0, tiled=True)  15.4 us
    unnamed x20, local copies, waits for them, and re-layouts  15 us
    all_to_all x1, blocking collectives, on_device(): energies = lax.all_to_all(energies, 'freq', 0, 0, tiled=True)  13.3 us
    all_to_all x1, starting transfers between devices, on_device(): wave = lax.all_to_all(wave, 'line_0', 0, 0, tiled=True)  7.55 us
    all_to_all x1, waiting for transfers between devices, on_device(): wave = lax.all_to_all(wave, 'line_0', 0, 0, tiled=True)  6.52 us
  transfers between devices with their start and end apart: 10, of which 4 were waited for; matrix products, arithmetic and copies ran while one was open for 18% of the time, Pallas kernels for 3%

profile of v8, /device:TPU:2, one launch (start us, length us, event | category | flops | bytes accessed | tf_op | source)
XLA Modules:
  0.0 175.2 jit_solution(17384590545517089318)
XLA Ops:
  0.6 1.8 %shard_map.77 = f32[3200,128]{1,0:T(8,128)S(1)} custom-call(s32[2]{0:T(128)} %live_ref.1, f32[3072,128]{1,0:T(8,128)} %bitcast.118, f32[128,128]{1,0:T(8,128)} %bitcast.121), custom_call_target="tpu_custom_call" | custom-call | tf_op jit(solution)/shard_map/pallas_call | solution.py:224
  3.4 18.1 %all-to-all-start = ((f16[32,25,4,128]{3,2,1,0:T(4,128)(2,1)}), f16[32,25,4,128]{3,2,1,0:T(4,128)(2,1)S(1)}, u32[]{:S(2)}, u32[]{:S(2)}) async-start(f16[32,25,4,128]{3,2,1,0:T(4,128)(2,1)} %bitcast.6), calls=%async_computation | async-start | bytes 1638400 | tf_op jit(solution)/shard_map/all_to_all | solution.py:327
  21.6 3.2 %reshape_squeeze.3 = bf16[4,4,2,32,1024]{4,3,2,1,0:T(8,128)(2,1)S(1)} reshape(bf16[1,1024,2,512]{3,2,1,0:T(2,128)(2,1)} %param.10) | data formatting | bytes 4194304 | tf_op jit(solution)/shard_map/reshape;squeeze | solution.py:239
  26.4 4.1 %fusion.2 = bf16[1024,1024]{0,1:T(8,128)(2,1)S(1)} fusion(bf16[1024,1024]{1,0:T(8,128)(2,1)} %bitcast.115, s32[1024]{0:T(1024)S(1)} %fusion.46), kind=kOutput, calls=%fused_computation.3 | convolution fusion | flops 2149580800 | bytes 4198400 | tf_op jit(solution)/shard_map/dot_general | solution.py:244
  31.8 2.2 %collective-permute-start = (bf16[1024,128]{0,1:T(8,128)(2,1)}, bf16[1024,128]{0,1:T(8,128)(2,1)}, u32[]{:S(2)}, u32[]{:S(2)}) collective-permute-start(bf16[1024,128]{0,1:T(8,128)(2,1)} %get-tuple-element.34), channel_id=1, source_target_pairs={{0,1},{1,0},{2,3},{3,2},{4,5},{5,4},{6,7},{7,6},{8,9},{9,8},{10,11... | collective-permute-start | bytes 786440 | tf_op jit(solution)/shard_map/ppermute | solution.py:254
  34.0 3.5 %collective-permute-start.1 = (bf16[1024,128]{0,1:T(8,128)(2,1)}, bf16[1024,128]{0,1:T(8,128)(2,1)}, u32[]{:S(2)}, u32[]{:S(2)}) collective-permute-start(bf16[1024,128]{0,1:T(8,128)(2,1)} %get-tuple-element.33), channel_id=1, source_target_pairs={{0,2},{1,3},{2,0},{3,1},{4,6},{5,7},{6,4},{7,5},{8,10},{9,11},{10,... | collective-permute-start | bytes 786440 | tf_op jit(solution)/shard_map/ppermute | solution.py:254
  37.5 1.9 %collective-permute-start.2 = (bf16[1024,128]{0,1:T(8,128)(2,1)}, bf16[1024,128]{0,1:T(8,128)(2,1)}, u32[]{:S(2)}, u32[]{:S(2)}) collective-permute-start(bf16[1024,128]{0,1:T(8,128)(2,1)} %get-tuple-element.32), channel_id=1, source_target_pairs={{0,3},{1,2},{2,1},{3,0},{4,7},{5,6},{6,5},{7,4},{8,11},{9,10},{10,... | collective-permute-start | bytes 786440 | tf_op jit(solution)/shard_map/ppermute | solution.py:254
  39.5 5.2 %collective-permute-start.3 = (bf16[1024,128]{0,1:T(8,128)(2,1)}, bf16[1024,128]{0,1:T(8,128)(2,1)}, u32[]{:S(2)}, u32[]{:S(2)}) collective-permute-start(bf16[1024,128]{0,1:T(8,128)(2,1)} %get-tuple-element.31), channel_id=1, source_target_pairs={{0,4},{1,5},{2,6},{3,7},{4,0},{5,1},{6,2},{7,3},{8,12},{9,13},{10,... | collective-permute-start | bytes 786440 | tf_op jit(solution)/shard_map/ppermute | solution.py:254
  44.6 2.0 %collective-permute-start.4 = (bf16[1024,128]{0,1:T(8,128)(2,1)}, bf16[1024,128]{0,1:T(8,128)(2,1)}, u32[]{:S(2)}, u32[]{:S(2)}) collective-permute-start(bf16[1024,128]{0,1:T(8,128)(2,1)} %get-tuple-element.30), channel_id=1, source_target_pairs={{0,5},{1,4},{2,7},{3,6},{4,1},{5,0},{6,3},{7,2},{8,13},{9,12},{10,... | collective-permute-start | bytes 786440 | tf_op jit(solution)/shard_map/ppermute | solution.py:254
  51.7 4.8 %collective-permute-start.5 = (bf16[1024,128]{0,1:T(8,128)(2,1)}, bf16[1024,128]{0,1:T(8,128)(2,1)}, u32[]{:S(2)}, u32[]{:S(2)}) collective-permute-start(bf16[1024,128]{0,1:T(8,128)(2,1)} %get-tuple-element.29), channel_id=1, source_target_pairs={{0,6},{1,7},{2,4},{3,5},{4,2},{5,3},{6,0},{7,1},{8,14},{9,15},{10,... | collective-permute-start | bytes 786440 | tf_op jit(solution)/shard_map/ppermute | solution.py:254
  56.5 1.7 bitcast_dynamic-update-slice_fusion.6
  58.2 5.2 %all-to-all-done = f16[32,25,4,128]{3,2,1,0:T(4,128)(2,1)S(1)} async-done(((f16[32,25,4,128]{3,2,1,0:T(4,128)(2,1)}), f16[32,25,4,128]{3,2,1,0:T(4,128)(2,1)S(1)}, u32[]{:S(2)}, u32[]{:S(2)}) %all-to-all-start) | async-done | bytes 819232 | tf_op jit(solution)/shard_map/all_to_all | solution.py:327
  63.5 4.4 %shard_map.78 = bf16[32,4,3,8,128]{4,3,2,1,0:T(8,128)(2,1)} custom-call(f32[3200,128]{1,0:T(8,128)S(1)} %convert.1.message_ref, bf16[256,256]{1,0:T(8,128)(2,1)S(1)} %get-tuple-element.59.forward_ref, bf16[256,256]{1,0:T(8,128)(2,1)S(1)} %get-tuple-element.60.inverse_ref, bf16[128,2048]{1,0:T(8,128)(2,1)S(1)} %and_convert_fusion.spread_ref), custom_call_target="tpu_custom_call" | custom-call | tf_op jit(solution)/shard_map/pallas_call | solution.py:162
  67.9 7.6 %all-to-all-start.1 = ((bf16[32,4,3,8,128]{4,3,2,1,0:T(8,128)(2,1)}), bf16[32,4,3,8,128]{4,3,2,1,0:T(8,128)(2,1)S(1)}, u32[]{:S(2)}, u32[]{:S(2)}) async-start(bf16[32,4,3,8,128]{4,3,2,1,0:T(8,128)(2,1)} %shard_map.78), calls=%async_computation.1 | async-start | bytes 1572864 | tf_op jit(solution)/shard_map/all_to_all | solution.py:330
  75.5 2.2 %collective-permute-start.6 = (bf16[1024,128]{0,1:T(8,128)(2,1)}, bf16[1024,128]{0,1:T(8,128)(2,1)S(1)}, u32[]{:S(2)}, u32[]{:S(2)}) collective-permute-start(bf16[1024,128]{0,1:T(8,128)(2,1)} %get-tuple-element.28), channel_id=1, source_target_pairs={{0,7},{1,6},{2,5},{3,4},{4,3},{5,2},{6,1},{7,0},{8,15},{9,14},{10,... | collective-permute-start | bytes 786440 | tf_op jit(solution)/shard_map/ppermute | solution.py:254
  77.7 1.7 bitcast_dynamic-update-slice_fusion.5
  79.4 1.7 bitcast_dynamic-update-slice_fusion.4
  82.8 1.7 bitcast_dynamic-update-slice_fusion.2
  84.5 1.7 bitcast_dynamic-update-slice_fusion.1
  91.5 6.5 %all-to-all-done.1 = bf16[32,4,3,8,128]{4,3,2,1,0:T(8,128)(2,1)S(1)} async-done(((bf16[32,4,3,8,128]{4,3,2,1,0:T(8,128)(2,1)}), bf16[32,4,3,8,128]{4,3,2,1,0:T(8,128)(2,1)S(1)}, u32[]{:S(2)}, u32[]{:S(2)}) %all-to-all-start.1) | async-done | bytes 786464 | tf_op jit(solution)/shard_map/all_to_all | solution.py:330
  99.9 1.9 %collective-permute-start.7 = (f16[512,768]{1,0:T(8,128)(2,1)S(1)}, f16[512,768]{1,0:T(8,128)(2,1)S(1)}, u32[]{:S(2)}, u32[]{:S(2)}) collective-permute-start(f16[512,768]{1,0:T(8,128)(2,1)S(1)} %convolution_convert_fusion), channel_id=1, source_target_pairs={{0,1},{1,0},{2,3},{3,2},{4,5},{5,4},{6,7},{7,6},{8,9},{9,8},{10,11... | collective-permute-start | bytes 2359304 | tf_op jit(solution)/shard_map/ppermute | solution.py:337
  104.3 15.4 %all_to_all.25 = f16[4,128,768]{2,1,0:T(8,128)(2,1)S(1)} all-to-all(f16[4,128,768]{2,1,0:T(8,128)(2,1)S(1)} %bitcast.112), channel_id=1, replica_groups=mesh['freq'=16,'line_0'=4,'line_1'=4,'line_2'=2] {'line_1'}, dimensions={0} | all-to-all | bytes 1572864 | tf_op jit(solution)/shard_map/all_to_all | solution.py:275
  119.9 40.6 %all_to_all.26 = f16[4,32,768]{2,1,0:T(8,128)(2,1)S(1)} all-to-all(f16[4,32,768]{2,1,0:T(8,128)(2,1)S(1)} %bitcast.120), channel_id=1, replica_groups=mesh['freq'=16,'line_0'=4,'line_1'=4,'line_2'=2] {'line_0'}, dimensions={0} | all-to-all | bytes 393216 | tf_op jit(solution)/shard_map/all_to_all | solution.py:344
  161.3 13.3 %all_to_all.27 = f32[16,1,32]{2,1,0:T(1,128)S(1)} all-to-all(f32[16,1,32]{2,1,0:T(1,128)S(1)} %get-tuple-element.11), channel_id=1, replica_groups=mesh['freq'=16,'line_0'=4,'line_1'=4,'line_2'=2] {'freq'}, dimensions={0} | all-to-all | bytes 4096 | tf_op jit(solution)/shard_map/all_to_all | solution.py:346
  (70 shorter events, 21.8 us)
Async XLA Ops:
  3.4 60.0 %all-to-all-start = ((f16[32,25,4,128]{3,2,1,0:T(4,128)(2,1)}), f16[32,25,4,128]{3,2,1,0:T(4,128)(2,1)S(1)}, u32[]{:S(2)}, u32[]{:S(2)}) async-start(f16[32,25,4,128]{3,2,1,0:T(4,128)(2,1)} %bitcast.6), calls=%async_computation | async-start | bytes 1638400 | tf_op jit(solution)/shard_map/all_to_all | solution.py:327
  30.5 16.2 %copy-start.2 = (s32[64]{0:T(128)S(1)}, s32[64]{0:T(128)}, u32[]{:S(2)}) copy-start(s32[64]{0:T(128)} %param.8) | copy-start | bytes 772
  31.8 19.9 %collective-permute-start = (bf16[1024,128]{0,1:T(8,128)(2,1)}, bf16[1024,128]{0,1:T(8,128)(2,1)}, u32[]{:S(2)}, u32[]{:S(2)}) collective-permute-start(bf16[1024,128]{0,1:T(8,128)(2,1)} %get-tuple-element.34), channel_id=1, source_target_pairs={{0,1},{1,0},{2,3},{3,2},{4,5},{5,4},{6,7},{7,6},{8,9},{9,8},{10,11... | collective-permute-start | bytes 786440 | tf_op jit(solution)/shard_map/ppermute | solution.py:254
  34.0 41.5 %collective-permute-start.1 = (bf16[1024,128]{0,1:T(8,128)(2,1)}, bf16[1024,128]{0,1:T(8,128)(2,1)}, u32[]{:S(2)}, u32[]{:S(2)}) collective-permute-start(bf16[1024,128]{0,1:T(8,128)(2,1)} %get-tuple-element.33), channel_id=1, source_target_pairs={{0,2},{1,3},{2,0},{3,1},{4,6},{5,7},{6,4},{7,5},{8,10},{9,11},{10,... | collective-permute-start | bytes 786440 | tf_op jit(solution)/shard_map/ppermute | solution.py:254
  37.5 41.9 %collective-permute-start.2 = (bf16[1024,128]{0,1:T(8,128)(2,1)}, bf16[1024,128]{0,1:T(8,128)(2,1)}, u32[]{:S(2)}, u32[]{:S(2)}) collective-permute-start(bf16[1024,128]{0,1:T(8,128)(2,1)} %get-tuple-element.32), channel_id=1, source_target_pairs={{0,3},{1,2},{2,1},{3,0},{4,7},{5,6},{6,5},{7,4},{8,11},{9,10},{10,... | collective-permute-start | bytes 786440 | tf_op jit(solution)/shard_map/ppermute | solution.py:254
  39.5 41.6 %collective-permute-start.3 = (bf16[1024,128]{0,1:T(8,128)(2,1)}, bf16[1024,128]{0,1:T(8,128)(2,1)}, u32[]{:S(2)}, u32[]{:S(2)}) collective-permute-start(bf16[1024,128]{0,1:T(8,128)(2,1)} %get-tuple-element.31), channel_id=1, source_target_pairs={{0,4},{1,5},{2,6},{3,7},{4,0},{5,1},{6,2},{7,3},{8,12},{9,13},{10,... | collective-permute-start | bytes 786440 | tf_op jit(solution)/shard_map/ppermute | solution.py:254
  44.6 38.2 %collective-permute-start.4 = (bf16[1024,128]{0,1:T(8,128)(2,1)}, bf16[1024,128]{0,1:T(8,128)(2,1)}, u32[]{:S(2)}, u32[]{:S(2)}) collective-permute-start(bf16[1024,128]{0,1:T(8,128)(2,1)} %get-tuple-element.30), channel_id=1, source_target_pairs={{0,5},{1,4},{2,7},{3,6},{4,1},{5,0},{6,3},{7,2},{8,13},{9,12},{10,... | collective-permute-start | bytes 786440 | tf_op jit(solution)/shard_map/ppermute | solution.py:254
  51.7 32.8 %collective-permute-start.5 = (bf16[1024,128]{0,1:T(8,128)(2,1)}, bf16[1024,128]{0,1:T(8,128)(2,1)}, u32[]{:S(2)}, u32[]{:S(2)}) collective-permute-start(bf16[1024,128]{0,1:T(8,128)(2,1)} %get-tuple-element.29), channel_id=1, source_target_pairs={{0,6},{1,7},{2,4},{3,5},{4,2},{5,3},{6,0},{7,1},{8,14},{9,15},{10,... | collective-permute-start | bytes 786440 | tf_op jit(solution)/shard_map/ppermute | solution.py:254
  67.9 30.1 %all-to-all-start.1 = ((bf16[32,4,3,8,128]{4,3,2,1,0:T(8,128)(2,1)}), bf16[32,4,3,8,128]{4,3,2,1,0:T(8,128)(2,1)S(1)}, u32[]{:S(2)}, u32[]{:S(2)}) async-start(bf16[32,4,3,8,128]{4,3,2,1,0:T(8,128)(2,1)} %shard_map.78), calls=%async_computation.1 | async-start | bytes 1572864 | tf_op jit(solution)/shard_map/all_to_all | solution.py:330
  75.5 11.0 %collective-permute-start.6 = (bf16[1024,128]{0,1:T(8,128)(2,1)}, bf16[1024,128]{0,1:T(8,128)(2,1)S(1)}, u32[]{:S(2)}, u32[]{:S(2)}) collective-permute-start(bf16[1024,128]{0,1:T(8,128)(2,1)} %get-tuple-element.28), channel_id=1, source_target_pairs={{0,7},{1,6},{2,5},{3,4},{4,3},{5,2},{6,1},{7,0},{8,15},{9,14},{10,... | collective-permute-start | bytes 786440 | tf_op jit(solution)/shard_map/ppermute | solution.py:254
  87.2 4.1 %copy-start.1 = (bf16[8,1024,128]{1,2,0:T(8,128)(2,1)S(1)}, bf16[8,1024,128]{1,2,0:T(8,128)(2,1)}, u32[]{:S(2)}) copy-start(bf16[8,1024,128]{1,2,0:T(8,128)(2,1)} %bitcast_dynamic-update-slice_fusion) | copy-start | bytes 6291460
  99.9 4.2 %collective-permute-start.7 = (f16[512,768]{1,0:T(8,128)(2,1)S(1)}, f16[512,768]{1,0:T(8,128)(2,1)S(1)}, u32[]{:S(2)}, u32[]{:S(2)}) collective-permute-start(f16[512,768]{1,0:T(8,128)(2,1)S(1)} %convolution_convert_fusion), channel_id=1, source_target_pairs={{0,1},{1,0},{2,3},{3,2},{4,5},{5,4},{6,7},{7,6},{8,9},{9,8},{10,11... | collective-permute-start | bytes 2359304 | tf_op jit(solution)/shard_map/ppermute | solution.py:337
  104.3 56.2 %copy-start = (f32[32,1,2,384]{3,2,1,0:T(2,128)S(1)}, f32[32,1,2,384]{3,2,1,0:T(2,128)}, u32[]{:S(2)}) copy-start(f32[32,1,2,384]{3,2,1,0:T(2,128)} %direct_ref.1) | copy-start | bytes 294916

commit v9 on v8

--- a/solution.py
+++ b/solution.py
@@ -178,7 +178,17 @@
     )
 
 
-def outgoing_kernel(live_ref, field_ref, operator_ref, out_ref):
+def outgoing_kernel(
+    live_ref, field_hbm, operator_hbm, out_ref, field_ref, operator_ref, field_here, operator_here
+):
+    fetches = [
+        pltpu.make_async_copy(field_hbm.at[part], field_ref.at[part], field_here.at[part])
+        for part in range(2)
+    ]
+    operator_fetch = pltpu.make_async_copy(operator_hbm, operator_ref, operator_here)
+    operator_fetch.start()
+    for fetch in fetches:
+        fetch.start()
     row = lax.broadcasted_iota(jnp.int32, (128, 128), 0)
     lane = lax.broadcasted_iota(jnp.int32, (128, 128), 1)
 
@@ -189,7 +199,7 @@
                 for t in range(3):
                     block = jnp.concatenate(
                         [
-                            field_ref[pl.ds(384 * c + 128 * t + 2 * half + line, 32, stride=4), :]
+                            field_ref[part, pl.ds(384 * c + 128 * t + 2 * half + line, 32, stride=4), :]
                             for c in range(4)
                         ],
                         0,
@@ -208,29 +218,31 @@
                 place = 100 * (16 * half + device) + 96
                 out_ref[place : place + 4, :] = block[8 * device : 8 * device + 4]
 
-    @pl.when(pl.program_id(0) == 0)
-    def _():
-        put_field(0)
-        put_operators()
-
-    @pl.when(pl.program_id(0) == 1)
-    def _():
-        put_field(1)
+    operator_fetch.wait()
+    put_operators()
+    for part in range(2):
+        fetches[part].wait()
+        put_field(part)
 
 
 def outgoing(field, live_count, decomposer):
-    rows = field.reshape(2, 4, 96, 2, 2, 128).transpose(0, 1, 2, 4, 3, 5).reshape(3072, 128)
+    rows = field.reshape(2, 4, 96, 2, 2, 128).transpose(0, 1, 2, 4, 3, 5).reshape(2, 1536, 128)
     operator_rows = decomposer.reshape(32, 2, 2, 128).transpose(0, 2, 1, 3).reshape(128, 128)
     tiles = pl.pallas_call(
         outgoing_kernel,
-        grid=(2,),
         out_shape=pltpu.VMEM((3200, 128), jnp.float32),
         in_specs=[
             pl.BlockSpec(memory_space=pltpu.SMEM),
-            pl.BlockSpec((1536, 128), lambda part: (part, 0)),
-            pl.BlockSpec((128, 128), lambda part: (0, 0)),
+            pl.BlockSpec(memory_space=pl.ANY),
+            pl.BlockSpec(memory_space=pl.ANY),
         ],
         out_specs=pl.BlockSpec(memory_space=pltpu.VMEM),
+        scratch_shapes=[
+            pltpu.VMEM((2, 1536, 128), jnp.float32),
+            pltpu.VMEM((128, 128), jnp.float32),
+            pltpu.SemaphoreType.DMA((2,)),
+            pltpu.SemaphoreType.DMA,
+        ],
     )(live_count, rows, operator_rows)
     return tiles.reshape(32, 25, 4, 128).astype(jnp.float16)
 

time: 176 us -> 177 us (level)
  no operation moved by 1% of the time
where the time goes in v9:
time: 177 us; the launch traced here: 176 us
  blocking collectives  69.3 us (39%)
  starting transfers between devices  49.4 us (28%)
  local copies, waits for them, and re-layouts  23.3 us (13%)
  waiting for transfers between devices  13.3 us (8%)
  Pallas kernels  7.65 us (4%)
  matrix products  6.12 us (3%)
  other arithmetic  5.61 us (3%)
    all_to_all x1, blocking collectives, on_device(): blocks = lax.all_to_all(blocks, 'line_0', 0, 0, tiled=True)  40.6 us
    ppermute x7, starting transfers between devices, exchanged(): received.append(lax.ppermute(block, PLANE, pairs))  21.9 us
    all_to_all x1, starting transfers between devices, on_device(): message = lax.all_to_all(message, RECEIVER, 0, 0, tiled=True)  18.1 us
    all_to_all x1, blocking collectives, summed(): blocks = lax.all_to_all(blocks, axis, 0, 0, tiled=True)  15.4 us
    unnamed x20, local copies, waits for them, and re-layouts  15 us
    all_to_all x1, blocking collectives, on_device(): energies = lax.all_to_all(energies, 'freq', 0, 0, tiled=True)  13.3 us
    all_to_all x1, starting transfers between devices, on_device(): wave = lax.all_to_all(wave, 'line_0', 0, 0, tiled=True)  7.54 us
    all_to_all x1, waiting for transfers between devices, on_device(): wave = lax.all_to_all(wave, 'line_0', 0, 0, tiled=True)  6.52 us
  transfers between devices with their start and end apart: 10, of which 4 were waited for; matrix products, arithmetic and copies ran while one was open for 18% of the time, Pallas kernels for 3%

profile of v9, /device:TPU:2, one launch (start us, length us, event | category | flops | bytes accessed | tf_op | source)
XLA Modules:
  0.0 175.8 jit_solution(9294071668384881940)
XLA Ops:
  0.6 2.4 %shard_map.77 = f32[3200,128]{1,0:T(8,128)S(1)} custom-call(s32[2]{0:T(128)} %live_ref.1, f32[2,1536,128]{2,1,0:T(8,128)} %bitcast.118, f32[128,128]{1,0:T(8,128)} %bitcast.121), custom_call_target="tpu_custom_call" | custom-call | tf_op jit(solution)/shard_map/pallas_call | solution.py:231
  4.1 18.1 %all-to-all-start = ((f16[32,25,4,128]{3,2,1,0:T(4,128)(2,1)}), f16[32,25,4,128]{3,2,1,0:T(4,128)(2,1)S(1)}, u32[]{:S(2)}, u32[]{:S(2)}) async-start(f16[32,25,4,128]{3,2,1,0:T(4,128)(2,1)} %bitcast.6), calls=%async_computation | async-start | bytes 1638400 | tf_op jit(solution)/shard_map/all_to_all | solution.py:339
  22.2 3.2 %reshape_squeeze.3 = bf16[4,4,2,32,1024]{4,3,2,1,0:T(8,128)(2,1)S(1)} reshape(bf16[1,1024,2,512]{3,2,1,0:T(2,128)(2,1)} %param.10) | data formatting | bytes 4194304 | tf_op jit(solution)/shard_map/reshape;squeeze | solution.py:251
  27.0 4.1 %fusion.2 = bf16[1024,1024]{0,1:T(8,128)(2,1)S(1)} fusion(bf16[1024,1024]{1,0:T(8,128)(2,1)} %bitcast.115, s32[1024]{0:T(1024)S(1)} %fusion.46), kind=kOutput, calls=%fused_computation.3 | convolution fusion | flops 2149580800 | bytes 4198400 | tf_op jit(solution)/shard_map/dot_general | solution.py:256
  32.4 2.2 %collective-permute-start = (bf16[1024,128]{0,1:T(8,128)(2,1)}, bf16[1024,128]{0,1:T(8,128)(2,1)}, u32[]{:S(2)}, u32[]{:S(2)}) collective-permute-start(bf16[1024,128]{0,1:T(8,128)(2,1)} %get-tuple-element.34), channel_id=1, source_target_pairs={{0,1},{1,0},{2,3},{3,2},{4,5},{5,4},{6,7},{7,6},{8,9},{9,8},{10,11... | collective-permute-start | bytes 786440 | tf_op jit(solution)/shard_map/ppermute | solution.py:266
  34.6 3.5 %collective-permute-start.1 = (bf16[1024,128]{0,1:T(8,128)(2,1)}, bf16[1024,128]{0,1:T(8,128)(2,1)}, u32[]{:S(2)}, u32[]{:S(2)}) collective-permute-start(bf16[1024,128]{0,1:T(8,128)(2,1)} %get-tuple-element.33), channel_id=1, source_target_pairs={{0,2},{1,3},{2,0},{3,1},{4,6},{5,7},{6,4},{7,5},{8,10},{9,11},{10,... | collective-permute-start | bytes 786440 | tf_op jit(solution)/shard_map/ppermute | solution.py:266
  38.2 1.9 %collective-permute-start.2 = (bf16[1024,128]{0,1:T(8,128)(2,1)}, bf16[1024,128]{0,1:T(8,128)(2,1)}, u32[]{:S(2)}, u32[]{:S(2)}) collective-permute-start(bf16[1024,128]{0,1:T(8,128)(2,1)} %get-tuple-element.32), channel_id=1, source_target_pairs={{0,3},{1,2},{2,1},{3,0},{4,7},{5,6},{6,5},{7,4},{8,11},{9,10},{10,... | collective-permute-start | bytes 786440 | tf_op jit(solution)/shard_map/ppermute | solution.py:266
  40.1 5.1 %collective-permute-start.3 = (bf16[1024,128]{0,1:T(8,128)(2,1)}, bf16[1024,128]{0,1:T(8,128)(2,1)}, u32[]{:S(2)}, u32[]{:S(2)}) collective-permute-start(bf16[1024,128]{0,1:T(8,128)(2,1)} %get-tuple-element.31), channel_id=1, source_target_pairs={{0,4},{1,5},{2,6},{3,7},{4,0},{5,1},{6,2},{7,3},{8,12},{9,13},{10,... | collective-permute-start | bytes 786440 | tf_op jit(solution)/shard_map/ppermute | solution.py:266
  45.2 2.0 %collective-permute-start.4 = (bf16[1024,128]{0,1:T(8,128)(2,1)}, bf16[1024,128]{0,1:T(8,128)(2,1)}, u32[]{:S(2)}, u32[]{:S(2)}) collective-permute-start(bf16[1024,128]{0,1:T(8,128)(2,1)} %get-tuple-element.30), channel_id=1, source_target_pairs={{0,5},{1,4},{2,7},{3,6},{4,1},{5,0},{6,3},{7,2},{8,13},{9,12},{10,... | collective-permute-start | bytes 786440 | tf_op jit(solution)/shard_map/ppermute | solution.py:266
  52.3 4.8 %collective-permute-start.5 = (bf16[1024,128]{0,1:T(8,128)(2,1)}, bf16[1024,128]{0,1:T(8,128)(2,1)}, u32[]{:S(2)}, u32[]{:S(2)}) collective-permute-start(bf16[1024,128]{0,1:T(8,128)(2,1)} %get-tuple-element.29), channel_id=1, source_target_pairs={{0,6},{1,7},{2,4},{3,5},{4,2},{5,3},{6,0},{7,1},{8,14},{9,15},{10,... | collective-permute-start | bytes 786440 | tf_op jit(solution)/shard_map/ppermute | solution.py:266
  57.1 1.7 bitcast_dynamic-update-slice_fusion.6
  58.8 5.2 %all-to-all-done = f16[32,25,4,128]{3,2,1,0:T(4,128)(2,1)S(1)} async-done(((f16[32,25,4,128]{3,2,1,0:T(4,128)(2,1)}), f16[32,25,4,128]{3,2,1,0:T(4,128)(2,1)S(1)}, u32[]{:S(2)}, u32[]{:S(2)}) %all-to-all-start) | async-done | bytes 819232 | tf_op jit(solution)/shard_map/all_to_all | solution.py:339
  64.2 4.4 %shard_map.78 = bf16[32,4,3,8,128]{4,3,2,1,0:T(8,128)(2,1)} custom-call(f32[3200,128]{1,0:T(8,128)S(1)} %convert.1.message_ref, bf16[256,256]{1,0:T(8,128)(2,1)S(1)} %get-tuple-element.59.forward_ref, bf16[256,256]{1,0:T(8,128)(2,1)S(1)} %get-tuple-element.60.inverse_ref, bf16[128,2048]{1,0:T(8,128)(2,1)S(1)} %and_convert_fusion.spread_ref), custom_call_target="tpu_custom_call" | custom-call | tf_op jit(solution)/shard_map/pallas_call | solution.py:162
  68.6 7.5 %all-to-all-start.1 = ((bf16[32,4,3,8,128]{4,3,2,1,0:T(8,128)(2,1)}), bf16[32,4,3,8,128]{4,3,2,1,0:T(8,128)(2,1)S(1)}, u32[]{:S(2)}, u32[]{:S(2)}) async-start(bf16[32,4,3,8,128]{4,3,2,1,0:T(8,128)(2,1)} %shard_map.78), calls=%async_computation.1 | async-start | bytes 1572864 | tf_op jit(solution)/shard_map/all_to_all | solution.py:342
  76.1 2.2 %collective-permute-start.6 = (bf16[1024,128]{0,1:T(8,128)(2,1)}, bf16[1024,128]{0,1:T(8,128)(2,1)S(1)}, u32[]{:S(2)}, u32[]{:S(2)}) collective-permute-start(bf16[1024,128]{0,1:T(8,128)(2,1)} %get-tuple-element.28), channel_id=1, source_target_pairs={{0,7},{1,6},{2,5},{3,4},{4,3},{5,2},{6,1},{7,0},{8,15},{9,14},{10,... | collective-permute-start | bytes 786440 | tf_op jit(solution)/shard_map/ppermute | solution.py:266
  78.4 1.7 bitcast_dynamic-update-slice_fusion.5
  80.0 1.7 bitcast_dynamic-update-slice_fusion.4
  83.4 1.7 bitcast_dynamic-update-slice_fusion.2
  85.1 1.7 bitcast_dynamic-update-slice_fusion.1
  92.2 6.5 %all-to-all-done.1 = bf16[32,4,3,8,128]{4,3,2,1,0:T(8,128)(2,1)S(1)} async-done(((bf16[32,4,3,8,128]{4,3,2,1,0:T(8,128)(2,1)}), bf16[32,4,3,8,128]{4,3,2,1,0:T(8,128)(2,1)S(1)}, u32[]{:S(2)}, u32[]{:S(2)}) %all-to-all-start.1) | async-done | bytes 786464 | tf_op jit(solution)/shard_map/all_to_all | solution.py:342
  100.5 1.9 %collective-permute-start.7 = (f16[512,768]{1,0:T(8,128)(2,1)S(1)}, f16[512,768]{1,0:T(8,128)(2,1)S(1)}, u32[]{:S(2)}, u32[]{:S(2)}) collective-permute-start(f16[512,768]{1,0:T(8,128)(2,1)S(1)} %convolution_convert_fusion), channel_id=1, source_target_pairs={{0,1},{1,0},{2,3},{3,2},{4,5},{5,4},{6,7},{7,6},{8,9},{9,8},{10,11... | collective-permute-start | bytes 2359304 | tf_op jit(solution)/shard_map/ppermute | solution.py:349
  104.9 15.4 %all_to_all.25 = f16[4,128,768]{2,1,0:T(8,128)(2,1)S(1)} all-to-all(f16[4,128,768]{2,1,0:T(8,128)(2,1)S(1)} %bitcast.112), channel_id=1, replica_groups=mesh['freq'=16,'line_0'=4,'line_1'=4,'line_2'=2] {'line_1'}, dimensions={0} | all-to-all | bytes 1572864 | tf_op jit(solution)/shard_map/all_to_all | solution.py:287
  120.5 40.6 %all_to_all.26 = f16[4,32,768]{2,1,0:T(8,128)(2,1)S(1)} all-to-all(f16[4,32,768]{2,1,0:T(8,128)(2,1)S(1)} %bitcast.120), channel_id=1, replica_groups=mesh['freq'=16,'line_0'=4,'line_1'=4,'line_2'=2] {'line_0'}, dimensions={0} | all-to-all | bytes 393216 | tf_op jit(solution)/shard_map/all_to_all | solution.py:356
  162.0 13.3 %all_to_all.27 = f32[16,1,32]{2,1,0:T(1,128)S(1)} all-to-all(f32[16,1,32]{2,1,0:T(1,128)S(1)} %get-tuple-element.11), channel_id=1, replica_groups=mesh['freq'=16,'line_0'=4,'line_1'=4,'line_2'=2] {'freq'}, dimensions={0} | all-to-all | bytes 4096 | tf_op jit(solution)/shard_map/all_to_all | solution.py:358
  (70 shorter events, 21.8 us)
Async XLA Ops:
  4.1 60.0 %all-to-all-start = ((f16[32,25,4,128]{3,2,1,0:T(4,128)(2,1)}), f16[32,25,4,128]{3,2,1,0:T(4,128)(2,1)S(1)}, u32[]{:S(2)}, u32[]{:S(2)}) async-start(f16[32,25,4,128]{3,2,1,0:T(4,128)(2,1)} %bitcast.6), calls=%async_computation | async-start | bytes 1638400 | tf_op jit(solution)/shard_map/all_to_all | solution.py:339
  31.1 16.2 %copy-start.2 = (s32[64]{0:T(128)S(1)}, s32[64]{0:T(128)}, u32[]{:S(2)}) copy-start(s32[64]{0:T(128)} %param.8) | copy-start | bytes 772
  32.4 19.9 %collective-permute-start = (bf16[1024,128]{0,1:T(8,128)(2,1)}, bf16[1024,128]{0,1:T(8,128)(2,1)}, u32[]{:S(2)}, u32[]{:S(2)}) collective-permute-start(bf16[1024,128]{0,1:T(8,128)(2,1)} %get-tuple-element.34), channel_id=1, source_target_pairs={{0,1},{1,0},{2,3},{3,2},{4,5},{5,4},{6,7},{7,6},{8,9},{9,8},{10,11... | collective-permute-start | bytes 786440 | tf_op jit(solution)/shard_map/ppermute | solution.py:266
  34.6 41.5 %collective-permute-start.1 = (bf16[1024,128]{0,1:T(8,128)(2,1)}, bf16[1024,128]{0,1:T(8,128)(2,1)}, u32[]{:S(2)}, u32[]{:S(2)}) collective-permute-start(bf16[1024,128]{0,1:T(8,128)(2,1)} %get-tuple-element.33), channel_id=1, source_target_pairs={{0,2},{1,3},{2,0},{3,1},{4,6},{5,7},{6,4},{7,5},{8,10},{9,11},{10,... | collective-permute-start | bytes 786440 | tf_op jit(solution)/shard_map/ppermute | solution.py:266
  38.2 41.9 %collective-permute-start.2 = (bf16[1024,128]{0,1:T(8,128)(2,1)}, bf16[1024,128]{0,1:T(8,128)(2,1)}, u32[]{:S(2)}, u32[]{:S(2)}) collective-permute-start(bf16[1024,128]{0,1:T(8,128)(2,1)} %get-tuple-element.32), channel_id=1, source_target_pairs={{0,3},{1,2},{2,1},{3,0},{4,7},{5,6},{6,5},{7,4},{8,11},{9,10},{10,... | collective-permute-start | bytes 786440 | tf_op jit(solution)/shard_map/ppermute | solution.py:266
  40.1 41.6 %collective-permute-start.3 = (bf16[1024,128]{0,1:T(8,128)(2,1)}, bf16[1024,128]{0,1:T(8,128)(2,1)}, u32[]{:S(2)}, u32[]{:S(2)}) collective-permute-start(bf16[1024,128]{0,1:T(8,128)(2,1)} %get-tuple-element.31), channel_id=1, source_target_pairs={{0,4},{1,5},{2,6},{3,7},{4,0},{5,1},{6,2},{7,3},{8,12},{9,13},{10,... | collective-permute-start | bytes 786440 | tf_op jit(solution)/shard_map/ppermute | solution.py:266
  45.2 38.2 %collective-permute-start.4 = (bf16[1024,128]{0,1:T(8,128)(2,1)}, bf16[1024,128]{0,1:T(8,128)(2,1)}, u32[]{:S(2)}, u32[]{:S(2)}) collective-permute-start(bf16[1024,128]{0,1:T(8,128)(2,1)} %get-tuple-element.30), channel_id=1, source_target_pairs={{0,5},{1,4},{2,7},{3,6},{4,1},{5,0},{6,3},{7,2},{8,13},{9,12},{10,... | collective-permute-start | bytes 786440 | tf_op jit(solution)/shard_map/ppermute | solution.py:266
  52.3 32.8 %collective-permute-start.5 = (bf16[1024,128]{0,1:T(8,128)(2,1)}, bf16[1024,128]{0,1:T(8,128)(2,1)}, u32[]{:S(2)}, u32[]{:S(2)}) collective-permute-start(bf16[1024,128]{0,1:T(8,128)(2,1)} %get-tuple-element.29), channel_id=1, source_target_pairs={{0,6},{1,7},{2,4},{3,5},{4,2},{5,3},{6,0},{7,1},{8,14},{9,15},{10,... | collective-permute-start | bytes 786440 | tf_op jit(solution)/shard_map/ppermute | solution.py:266
  68.6 30.1 %all-to-all-start.1 = ((bf16[32,4,3,8,128]{4,3,2,1,0:T(8,128)(2,1)}), bf16[32,4,3,8,128]{4,3,2,1,0:T(8,128)(2,1)S(1)}, u32[]{:S(2)}, u32[]{:S(2)}) async-start(bf16[32,4,3,8,128]{4,3,2,1,0:T(8,128)(2,1)} %shard_map.78), calls=%async_computation.1 | async-start | bytes 1572864 | tf_op jit(solution)/shard_map/all_to_all | solution.py:342
  76.1 11.0 %collective-permute-start.6 = (bf16[1024,128]{0,1:T(8,128)(2,1)}, bf16[1024,128]{0,1:T(8,128)(2,1)S(1)}, u32[]{:S(2)}, u32[]{:S(2)}) collective-permute-start(bf16[1024,128]{0,1:T(8,128)(2,1)} %get-tuple-element.28), channel_id=1, source_target_pairs={{0,7},{1,6},{2,5},{3,4},{4,3},{5,2},{6,1},{7,0},{8,15},{9,14},{10,... | collective-permute-start | bytes 786440 | tf_op jit(solution)/shard_map/ppermute | solution.py:266
  87.9 4.1 %copy-start.1 = (bf16[8,1024,128]{1,2,0:T(8,128)(2,1)S(1)}, bf16[8,1024,128]{1,2,0:T(8,128)(2,1)}, u32[]{:S(2)}) copy-start(bf16[8,1024,128]{1,2,0:T(8,128)(2,1)} %bitcast_dynamic-update-slice_fusion) | copy-start | bytes 6291460
  100.5 4.2 %collective-permute-start.7 = (f16[512,768]{1,0:T(8,128)(2,1)S(1)}, f16[512,768]{1,0:T(8,128)(2,1)S(1)}, u32[]{:S(2)}, u32[]{:S(2)}) collective-permute-start(f16[512,768]{1,0:T(8,128)(2,1)S(1)} %convolution_convert_fusion), channel_id=1, source_target_pairs={{0,1},{1,0},{2,3},{3,2},{4,5},{5,4},{6,7},{7,6},{8,9},{9,8},{10,11... | collective-permute-start | bytes 2359304 | tf_op jit(solution)/shard_map/ppermute | solution.py:349
  104.9 56.2 %copy-start = (f32[32,1,2,384]{3,2,1,0:T(2,128)S(1)}, f32[32,1,2,384]{3,2,1,0:T(2,128)}, u32[]{:S(2)}) copy-start(f32[32,1,2,384]{3,2,1,0:T(2,128)} %direct_ref.1) | copy-start | bytes 294916
